TPU v7x, 32 devices: a 4x4x1 block of a 4x4x8 slice. The times are simulated.
32 devices in a mesh: dp: 1 (over z), cp: 32 (over y, x, core).
Axes of the slice: x: 4, y: 4, z: 1, core: 2. Of those that a mesh axis runs over, the one named last changes fastest.
The devices are a block of a 4x4x8 slice.
Arguments:
- x_seq: bfloat16 [1, 8192, 768], P('dp', 'cp')
- dy_seq: float32 [1, 8192, 768], P('dp', 'cp')
- ln1_gain: float32 [768], replicated
- ln1_bias: float32 [768], replicated
- ln2_gain: float32 [768], replicated
- ln2_bias: float32 [768], replicated
- w_qkv: bfloat16 [768, 12, 3, 64], replicated
- b_qkv: bfloat16 [12, 3, 64], replicated
- w_out: bfloat16 [768, 768], replicated
- b_out: bfloat16 [768], replicated
- w_up: bfloat16 [768, 3072], replicated
- b_up: bfloat16 [3072], replicated
- w_down: bfloat16 [3072, 768], replicated
- b_down: bfloat16 [768], replicated
Outputs:
- output 1: bfloat16 [1, 8192, 768], P('dp', 'cp')
- output 2: float32 [1, 8192, 768], P('dp', 'cp')
- output 3: float32 [768], P('dp')
- output 4: float32 [768], P('dp')
- output 5: float32 [768], P('dp')
- output 6: float32 [768], P('dp')
- output 7: float32 [768, 12, 3, 64], P('dp')
- output 8: float32 [12, 3, 64], P('dp')
- output 9: float32 [768, 768], P('dp')
- output 10: float32 [768], P('dp')
- output 11: float32 [768, 3072], P('dp')
- output 12: float32 [3072], P('dp')
- output 13: float32 [3072, 768], P('dp')
- output 14: float32 [768], P('dp')
All inputs are finite; a program needn't handle non-finite values.
Results may differ from a plain program's by a relative error of at most 0.0195307.
Values are sent between devices in bfloat16 or wider.
A program may use at most 768 MiB of HBM per device.

v0:
```python
import jax
import jax.numpy as jnp
from jax import lax
from jax.sharding import PartitionSpec as P

EPS = 1e-5
ROPE_BASE = 10000.0
NEG_BIG = -1e30


def layer_norm(row_vals, norm_gain, norm_shift):
    row_mean = jnp.mean(row_vals, axis=-1, keepdims=True)
    centered = row_vals - row_mean
    inv_std = lax.rsqrt(jnp.mean(centered * centered, axis=-1, keepdims=True) + EPS)
    x_norm = centered * inv_std
    return x_norm * norm_gain + norm_shift, x_norm, inv_std


def norm_backward(d_out, x_norm, inv_std, norm_gain):
    d_norm = d_out * norm_gain
    d_rows = inv_std * (d_norm - jnp.mean(d_norm, axis=-1, keepdims=True) - x_norm * jnp.mean(d_norm * x_norm, axis=-1, keepdims=True))
    return d_rows, jnp.sum(d_out * x_norm, axis=(0, 1)), jnp.sum(d_out, axis=(0, 1))


def rope_tables(positions, head_dim):
    rot_dim = head_dim // 4
    inv_freq = ROPE_BASE ** (-2.0 * jnp.arange(rot_dim // 2, dtype=jnp.float32) / rot_dim)
    angles = positions.astype(jnp.float32)[:, None] * inv_freq[None, :]
    return jnp.cos(angles), jnp.sin(angles)


def apply_rotary(head_vals, cos_t, sin_t):
    half_rot = cos_t.shape[-1]
    first_half = head_vals[..., :half_rot]
    second_half = head_vals[..., half_rot:2 * half_rot]
    cos_b = cos_t[None, :, None, :]
    sin_b = sin_t[None, :, None, :]
    return jnp.concatenate([first_half * cos_b - second_half * sin_b, second_half * cos_b + first_half * sin_b, head_vals[..., 2 * half_rot:]], axis=-1)


def exact_gelu(pre_act):
    return jax.nn.gelu(pre_act, approximate=False)


def block_scores(q_rows, k_blk, qk_scale, diag_mask):
    scores = jnp.einsum('bqhe,bkhe->bhqk', q_rows, k_blk, preferred_element_type=jnp.float32) * qk_scale
    if diag_mask is None:
        return scores
    return jnp.where(diag_mask, scores, NEG_BIG)


def fold_block(soft_state, q_rows, k_blk, v_blk, qk_scale, diag_mask):
    row_max, row_sum, out_acc = soft_state
    scores = block_scores(q_rows, k_blk, qk_scale, diag_mask)
    new_max = jnp.maximum(row_max, jnp.max(scores, axis=-1))
    attn_probs = jnp.exp(scores - new_max[..., None])
    rescale = jnp.exp(row_max - new_max)
    row_sum = row_sum * rescale + jnp.sum(attn_probs, axis=-1)
    part_out = jnp.einsum('bhqk,bkhe->bqhe', attn_probs.astype(jnp.bfloat16), v_blk, preferred_element_type=jnp.float32)
    out_acc = out_acc * jnp.swapaxes(rescale, 1, 2)[..., None] + part_out
    return new_max, row_sum, out_acc


def block_grads(q_rows, k_blk, v_blk, d_ctx_bf, log_sum, row_delta, qk_scale, diag_mask):
    scores = block_scores(q_rows, k_blk, qk_scale, diag_mask)
    attn_probs = jnp.exp(scores - log_sum[..., None])
    d_v = jnp.einsum('bhqk,bqhe->bkhe', attn_probs.astype(jnp.bfloat16), d_ctx_bf, preferred_element_type=jnp.float32)
    d_probs = jnp.einsum('bqhe,bkhe->bhqk', d_ctx_bf, v_blk, preferred_element_type=jnp.float32)
    d_scores = (attn_probs * (d_probs - row_delta[..., None]) * qk_scale).astype(jnp.bfloat16)
    d_q = jnp.einsum('bhqk,bkhe->bqhe', d_scores, k_blk, preferred_element_type=jnp.float32)
    d_k = jnp.einsum('bhqk,bqhe->bkhe', d_scores, q_rows, preferred_element_type=jnp.float32)
    return d_q, d_k, d_v


def solution(mesh):
    cp_size = mesh.shape['cp']
    shift_perm = [(sender, (sender + 1) % cp_size) for sender in range(cp_size)]
    row_spec = P('dp', 'cp', None)
    in_specs = (row_spec, row_spec) + (P(),) * 12
    out_specs = (row_spec, row_spec, P('dp'), P('dp'), P('dp'), P('dp'), P('dp', None, None, None), P('dp', None, None), P('dp', None), P('dp'), P('dp', None), P('dp'), P('dp', None), P('dp'))

    def local_layer(x_blk, dy_blk, ln1_gain, ln1_bias, ln2_gain, ln2_bias, w_qkv, b_qkv, w_out, b_out, w_up, b_up, w_down, b_down):
        batch_size, row_count, model_width = x_blk.shape
        head_count, head_dim = w_qkv.shape[1], w_qkv.shape[3]
        qk_scale = head_dim ** -0.5
        my_idx = lax.axis_index('cp')
        cos_t, sin_t = rope_tables(my_idx * row_count + jnp.arange(row_count), head_dim)
        local_pos = jnp.arange(row_count)
        diag_mask = local_pos[None, :] <= local_pos[:, None]

        x_rows = x_blk.astype(jnp.float32)
        h_attn, x_norm1, inv_std1 = layer_norm(x_rows, ln1_gain, ln1_bias)
        h_attn = h_attn.astype(jnp.bfloat16)
        qkv_rows = jnp.einsum('btd,dhce->bthce', h_attn, w_qkv, preferred_element_type=jnp.float32) + b_qkv.astype(jnp.float32)
        q_rows = apply_rotary(qkv_rows[:, :, :, 0], cos_t, sin_t).astype(jnp.bfloat16)
        k_own = apply_rotary(qkv_rows[:, :, :, 1], cos_t, sin_t).astype(jnp.bfloat16)
        v_own = qkv_rows[:, :, :, 2].astype(jnp.bfloat16)

        stat_shape = (batch_size, head_count, row_count)
        start_state = (jnp.full(stat_shape, NEG_BIG, jnp.float32), jnp.zeros(stat_shape, jnp.float32), jnp.zeros((batch_size, row_count, head_count, head_dim), jnp.float32))
        own_state = fold_block(start_state, q_rows, k_own, v_own, qk_scale, diag_mask)

        def fwd_step(step_idx, carry):
            k_cur, v_cur, soft_state = carry
            k_cur, v_cur = lax.ppermute((k_cur, v_cur), 'cp', shift_perm)
            soft_state = lax.cond(step_idx <= my_idx, lambda state_in: fold_block(state_in, q_rows, k_cur, v_cur, qk_scale, None), lambda state_in: state_in, soft_state)
            return k_cur, v_cur, soft_state

        row_max, row_sum, out_acc = lax.fori_loop(1, cp_size, fwd_step, (k_own, v_own, own_state))[2]
        attn_norm = out_acc / jnp.swapaxes(row_sum, 1, 2)[..., None]
        log_sum = row_max + jnp.log(row_sum)
        attn_ctx = attn_norm.astype(jnp.bfloat16).reshape(batch_size, row_count, model_width)
        attn_proj = jnp.einsum('btd,de->bte', attn_ctx, w_out, preferred_element_type=jnp.float32) + b_out.astype(jnp.float32)

        h_mlp, x_norm2, inv_std2 = layer_norm(x_rows, ln2_gain, ln2_bias)
        h_mlp = h_mlp.astype(jnp.bfloat16)
        up_proj = jnp.einsum('btd,df->btf', h_mlp, w_up, preferred_element_type=jnp.float32) + b_up.astype(jnp.float32)
        gelu_out, gelu_back = jax.vjp(exact_gelu, up_proj)
        gelu_bf = gelu_out.astype(jnp.bfloat16)
        mlp_proj = jnp.einsum('btf,fd->btd', gelu_bf, w_down, preferred_element_type=jnp.float32) + b_down.astype(jnp.float32)
        y_rows = (x_rows + attn_proj + mlp_proj).astype(jnp.bfloat16)

        dy_bf = dy_blk.astype(jnp.bfloat16)
        dy_sum = jnp.sum(dy_blk, axis=(0, 1))
        d_w_down = jnp.einsum('btf,btd->fd', gelu_bf, dy_bf, preferred_element_type=jnp.float32)
        d_gelu = jnp.einsum('btd,fd->btf', dy_bf, w_down, preferred_element_type=jnp.float32)
        d_up = gelu_back(d_gelu)[0]
        d_b_up = jnp.sum(d_up, axis=(0, 1))
        d_up_bf = d_up.astype(jnp.bfloat16)
        d_w_up = jnp.einsum('btd,btf->df', h_mlp, d_up_bf, preferred_element_type=jnp.float32)
        d_h_mlp = jnp.einsum('btf,df->btd', d_up_bf, w_up, preferred_element_type=jnp.float32)

        d_w_out = jnp.einsum('btd,bte->de', attn_ctx, dy_bf, preferred_element_type=jnp.float32)
        d_ctx = jnp.einsum('bte,de->btd', dy_bf, w_out, preferred_element_type=jnp.float32).reshape(batch_size, row_count, head_count, head_dim)
        row_delta = jnp.swapaxes(jnp.sum(d_ctx * attn_norm, axis=-1), 1, 2)
        d_ctx_bf = d_ctx.astype(jnp.bfloat16)
        dq_own, dk_own, dv_own = block_grads(q_rows, k_own, v_own, d_ctx_bf, log_sum, row_delta, qk_scale, diag_mask)

        def bwd_step(step_idx, carry):
            k_cur, v_cur, dk_cur, dv_cur, dq_acc = carry
            k_cur, v_cur, dk_cur, dv_cur = lax.ppermute((k_cur, v_cur, dk_cur, dv_cur), 'cp', shift_perm)

            def add_block(operands):
                dq_in, dk_in, dv_in = operands
                g_q, g_k, g_v = block_grads(q_rows, k_cur, v_cur, d_ctx_bf, log_sum, row_delta, qk_scale, None)
                return dq_in + g_q, dk_in + g_k, dv_in + g_v

            dq_acc, dk_cur, dv_cur = lax.cond(step_idx <= my_idx, add_block, lambda operands: operands, (dq_acc, dk_cur, dv_cur))
            return k_cur, v_cur, dk_cur, dv_cur, dq_acc

        loop_out = lax.fori_loop(1, cp_size, bwd_step, (k_own, v_own, dk_own, dv_own, dq_own))
        d_q = loop_out[4]
        d_k, d_v = lax.ppermute((loop_out[2], loop_out[3]), 'cp', shift_perm)

        d_q_raw = apply_rotary(d_q, cos_t, -sin_t)
        d_k_raw = apply_rotary(d_k, cos_t, -sin_t)
        d_qkv = jnp.stack([d_q_raw, d_k_raw, d_v], axis=3)
        d_b_qkv = jnp.sum(d_qkv, axis=(0, 1))
        d_qkv_bf = d_qkv.astype(jnp.bfloat16)
        d_w_qkv = jnp.einsum('btd,bthce->dhce', h_attn, d_qkv_bf, preferred_element_type=jnp.float32)
        d_h_attn = jnp.einsum('bthce,dhce->btd', d_qkv_bf, w_qkv, preferred_element_type=jnp.float32)

        dx_attn, d_ln1_gain, d_ln1_bias = norm_backward(d_h_attn, x_norm1, inv_std1, ln1_gain)
        dx_mlp, d_ln2_gain, d_ln2_bias = norm_backward(d_h_mlp, x_norm2, inv_std2, ln2_gain)
        dx_rows = dy_blk + dx_attn + dx_mlp

        summed = lax.psum((d_ln1_gain, d_ln1_bias, d_ln2_gain, d_ln2_bias, d_w_qkv, d_b_qkv, d_w_out, dy_sum, d_w_up, d_b_up, d_w_down), 'cp')
        return (y_rows, dx_rows) + tuple(summed) + (summed[7],)

    return jax.shard_map(local_layer, mesh=mesh, in_specs=in_specs, out_specs=out_specs, check_vma=False)
```

profile of v0, /device:TPU:97, one launch (start us, length us, event | category | flops | bytes accessed | tf_op | source)
XLA Modules:
  0.0 2377.7 jit_solution(15604385543621389771)
XLA Ops:
  35.3 613.3 %while.42 = (s32[]{:T(128)}, bf16[1,256,12,64]{1,3,2,0:T(8,128)(2,1)}, bf16[1,256,12,64]{1,3,2,0:T(8,128)(2,1)}, f32[1,12,256]{2,1,0:T(8,128)S(1)}, f32[1,12,256...) while((s32[]{:T(128)}, ...), condition=%wide.region_9.10_spmd, body=%wide.region_4.9_spmd.sunk | while | flops 208020480 | bytes 23495060 | solution.py:109
  660.4 1379.8 %while.43 = (s32[]{:T(128)}, bf16[1,256,12,64]{1,3,2,0:T(8,128)(2,1)}, bf16[1,256,12,64]{1,3,2,0:T(8,128)(2,1)}, f32[1,256,12,64]{1,3,2,0:T(8,128)}, f32[1,256,1...) while((s32[]{:T(128)}, ...), condition=%wide.region_14.15_spmd, body=%wide.region_11.14_spmd.sunk | while | flops 510984192 | bytes 45306416 | solution.py:151
  786.4 22.4 collective-permute-done.2
  821.1 31.0 %collective-permute-done.2 = bf16[1,256,12,64]{1,3,2,0:T(8,128)(2,1)} collective-permute-done((bf16[1,256,12,64]{1,3,2,0:T(8,128)(2,1)}, bf16[1,256,12,64]{1,3,2,0:T(8,128)(2,1)}, u32[]{:S(2)}, u32[]{:S(2)}) %collective-permute-start.2) | collective-permute-done | bytes 393248 | tf_op jit(solution)/shard_map/while/body/eval_jaxpr/ppermute | solution.py:141
  865.6 29.9 %collective-permute-done.2 = bf16[1,256,12,64]{1,3,2,0:T(8,128)(2,1)} collective-permute-done((bf16[1,256,12,64]{1,3,2,0:T(8,128)(2,1)}, bf16[1,256,12,64]{1,3,2,0:T(8,128)(2,1)}, u32[]{:S(2)}, u32[]{:S(2)}) %collective-permute-start.2) | collective-permute-done | bytes 393248 | tf_op jit(solution)/shard_map/while/body/eval_jaxpr/ppermute | solution.py:141
  903.4 35.4 %collective-permute-done.2 = bf16[1,256,12,64]{1,3,2,0:T(8,128)(2,1)} collective-permute-done((bf16[1,256,12,64]{1,3,2,0:T(8,128)(2,1)}, bf16[1,256,12,64]{1,3,2,0:T(8,128)(2,1)}, u32[]{:S(2)}, u32[]{:S(2)}) %collective-permute-start.2) | collective-permute-done | bytes 393248 | tf_op jit(solution)/shard_map/while/body/eval_jaxpr/ppermute | solution.py:141
  949.8 32.3 %collective-permute-done.2 = bf16[1,256,12,64]{1,3,2,0:T(8,128)(2,1)} collective-permute-done((bf16[1,256,12,64]{1,3,2,0:T(8,128)(2,1)}, bf16[1,256,12,64]{1,3,2,0:T(8,128)(2,1)}, u32[]{:S(2)}, u32[]{:S(2)}) %collective-permute-start.2) | collective-permute-done | bytes 393248 | tf_op jit(solution)/shard_map/while/body/eval_jaxpr/ppermute | solution.py:141
  997.8 27.7 %collective-permute-done.2 = bf16[1,256,12,64]{1,3,2,0:T(8,128)(2,1)} collective-permute-done((bf16[1,256,12,64]{1,3,2,0:T(8,128)(2,1)}, bf16[1,256,12,64]{1,3,2,0:T(8,128)(2,1)}, u32[]{:S(2)}, u32[]{:S(2)}) %collective-permute-start.2) | collective-permute-done | bytes 393248 | tf_op jit(solution)/shard_map/while/body/eval_jaxpr/ppermute | solution.py:141
  1041.9 28.4 %collective-permute-done.2 = bf16[1,256,12,64]{1,3,2,0:T(8,128)(2,1)} collective-permute-done((bf16[1,256,12,64]{1,3,2,0:T(8,128)(2,1)}, bf16[1,256,12,64]{1,3,2,0:T(8,128)(2,1)}, u32[]{:S(2)}, u32[]{:S(2)}) %collective-permute-start.2) | collective-permute-done | bytes 393248 | tf_op jit(solution)/shard_map/while/body/eval_jaxpr/ppermute | solution.py:141
  1082.7 33.4 %collective-permute-done.2 = bf16[1,256,12,64]{1,3,2,0:T(8,128)(2,1)} collective-permute-done((bf16[1,256,12,64]{1,3,2,0:T(8,128)(2,1)}, bf16[1,256,12,64]{1,3,2,0:T(8,128)(2,1)}, u32[]{:S(2)}, u32[]{:S(2)}) %collective-permute-start.2) | collective-permute-done | bytes 393248 | tf_op jit(solution)/shard_map/while/body/eval_jaxpr/ppermute | solution.py:141
  1123.9 37.9 %collective-permute-done.2 = bf16[1,256,12,64]{1,3,2,0:T(8,128)(2,1)} collective-permute-done((bf16[1,256,12,64]{1,3,2,0:T(8,128)(2,1)}, bf16[1,256,12,64]{1,3,2,0:T(8,128)(2,1)}, u32[]{:S(2)}, u32[]{:S(2)}) %collective-permute-start.2) | collective-permute-done | bytes 393248 | tf_op jit(solution)/shard_map/while/body/eval_jaxpr/ppermute | solution.py:141
  1169.8 37.9 %collective-permute-done.2 = bf16[1,256,12,64]{1,3,2,0:T(8,128)(2,1)} collective-permute-done((bf16[1,256,12,64]{1,3,2,0:T(8,128)(2,1)}, bf16[1,256,12,64]{1,3,2,0:T(8,128)(2,1)}, u32[]{:S(2)}, u32[]{:S(2)}) %collective-permute-start.2) | collective-permute-done | bytes 393248 | tf_op jit(solution)/shard_map/while/body/eval_jaxpr/ppermute | solution.py:141
  1215.6 37.9 %collective-permute-done.2 = bf16[1,256,12,64]{1,3,2,0:T(8,128)(2,1)} collective-permute-done((bf16[1,256,12,64]{1,3,2,0:T(8,128)(2,1)}, bf16[1,256,12,64]{1,3,2,0:T(8,128)(2,1)}, u32[]{:S(2)}, u32[]{:S(2)}) %collective-permute-start.2) | collective-permute-done | bytes 393248 | tf_op jit(solution)/shard_map/while/body/eval_jaxpr/ppermute | solution.py:141
  1262.8 36.5 %collective-permute-done.2 = bf16[1,256,12,64]{1,3,2,0:T(8,128)(2,1)} collective-permute-done((bf16[1,256,12,64]{1,3,2,0:T(8,128)(2,1)}, bf16[1,256,12,64]{1,3,2,0:T(8,128)(2,1)}, u32[]{:S(2)}, u32[]{:S(2)}) %collective-permute-start.2) | collective-permute-done | bytes 393248 | tf_op jit(solution)/shard_map/while/body/eval_jaxpr/ppermute | solution.py:141
  1310.7 34.4 %collective-permute-done.2 = bf16[1,256,12,64]{1,3,2,0:T(8,128)(2,1)} collective-permute-done((bf16[1,256,12,64]{1,3,2,0:T(8,128)(2,1)}, bf16[1,256,12,64]{1,3,2,0:T(8,128)(2,1)}, u32[]{:S(2)}, u32[]{:S(2)}) %collective-permute-start.2) | collective-permute-done | bytes 393248 | tf_op jit(solution)/shard_map/while/body/eval_jaxpr/ppermute | solution.py:141
  1353.0 37.9 %collective-permute-done.2 = bf16[1,256,12,64]{1,3,2,0:T(8,128)(2,1)} collective-permute-done((bf16[1,256,12,64]{1,3,2,0:T(8,128)(2,1)}, bf16[1,256,12,64]{1,3,2,0:T(8,128)(2,1)}, u32[]{:S(2)}, u32[]{:S(2)}) %collective-permute-start.2) | collective-permute-done | bytes 393248 | tf_op jit(solution)/shard_map/while/body/eval_jaxpr/ppermute | solution.py:141
  1398.8 37.9 %collective-permute-done.2 = bf16[1,256,12,64]{1,3,2,0:T(8,128)(2,1)} collective-permute-done((bf16[1,256,12,64]{1,3,2,0:T(8,128)(2,1)}, bf16[1,256,12,64]{1,3,2,0:T(8,128)(2,1)}, u32[]{:S(2)}, u32[]{:S(2)}) %collective-permute-start.2) | collective-permute-done | bytes 393248 | tf_op jit(solution)/shard_map/while/body/eval_jaxpr/ppermute | solution.py:141
  1444.7 37.9 %collective-permute-done.2 = bf16[1,256,12,64]{1,3,2,0:T(8,128)(2,1)} collective-permute-done((bf16[1,256,12,64]{1,3,2,0:T(8,128)(2,1)}, bf16[1,256,12,64]{1,3,2,0:T(8,128)(2,1)}, u32[]{:S(2)}, u32[]{:S(2)}) %collective-permute-start.2) | collective-permute-done | bytes 393248 | tf_op jit(solution)/shard_map/while/body/eval_jaxpr/ppermute | solution.py:141
  1490.5 37.9 %collective-permute-done.2 = bf16[1,256,12,64]{1,3,2,0:T(8,128)(2,1)} collective-permute-done((bf16[1,256,12,64]{1,3,2,0:T(8,128)(2,1)}, bf16[1,256,12,64]{1,3,2,0:T(8,128)(2,1)}, u32[]{:S(2)}, u32[]{:S(2)}) %collective-permute-start.2) | collective-permute-done | bytes 393248 | tf_op jit(solution)/shard_map/while/body/eval_jaxpr/ppermute | solution.py:141
  1536.3 37.9 %collective-permute-done.2 = bf16[1,256,12,64]{1,3,2,0:T(8,128)(2,1)} collective-permute-done((bf16[1,256,12,64]{1,3,2,0:T(8,128)(2,1)}, bf16[1,256,12,64]{1,3,2,0:T(8,128)(2,1)}, u32[]{:S(2)}, u32[]{:S(2)}) %collective-permute-start.2) | collective-permute-done | bytes 393248 | tf_op jit(solution)/shard_map/while/body/eval_jaxpr/ppermute | solution.py:141
  1582.1 37.9 %collective-permute-done.2 = bf16[1,256,12,64]{1,3,2,0:T(8,128)(2,1)} collective-permute-done((bf16[1,256,12,64]{1,3,2,0:T(8,128)(2,1)}, bf16[1,256,12,64]{1,3,2,0:T(8,128)(2,1)}, u32[]{:S(2)}, u32[]{:S(2)}) %collective-permute-start.2) | collective-permute-done | bytes 393248 | tf_op jit(solution)/shard_map/while/body/eval_jaxpr/ppermute | solution.py:141
  1627.9 37.9 %collective-permute-done.2 = bf16[1,256,12,64]{1,3,2,0:T(8,128)(2,1)} collective-permute-done((bf16[1,256,12,64]{1,3,2,0:T(8,128)(2,1)}, bf16[1,256,12,64]{1,3,2,0:T(8,128)(2,1)}, u32[]{:S(2)}, u32[]{:S(2)}) %collective-permute-start.2) | collective-permute-done | bytes 393248 | tf_op jit(solution)/shard_map/while/body/eval_jaxpr/ppermute | solution.py:141
  1673.8 37.9 %collective-permute-done.2 = bf16[1,256,12,64]{1,3,2,0:T(8,128)(2,1)} collective-permute-done((bf16[1,256,12,64]{1,3,2,0:T(8,128)(2,1)}, bf16[1,256,12,64]{1,3,2,0:T(8,128)(2,1)}, u32[]{:S(2)}, u32[]{:S(2)}) %collective-permute-start.2) | collective-permute-done | bytes 393248 | tf_op jit(solution)/shard_map/while/body/eval_jaxpr/ppermute | solution.py:141
  1719.6 37.9 %collective-permute-done.2 = bf16[1,256,12,64]{1,3,2,0:T(8,128)(2,1)} collective-permute-done((bf16[1,256,12,64]{1,3,2,0:T(8,128)(2,1)}, bf16[1,256,12,64]{1,3,2,0:T(8,128)(2,1)}, u32[]{:S(2)}, u32[]{:S(2)}) %collective-permute-start.2) | collective-permute-done | bytes 393248 | tf_op jit(solution)/shard_map/while/body/eval_jaxpr/ppermute | solution.py:141
  1765.4 37.9 %collective-permute-done.2 = bf16[1,256,12,64]{1,3,2,0:T(8,128)(2,1)} collective-permute-done((bf16[1,256,12,64]{1,3,2,0:T(8,128)(2,1)}, bf16[1,256,12,64]{1,3,2,0:T(8,128)(2,1)}, u32[]{:S(2)}, u32[]{:S(2)}) %collective-permute-start.2) | collective-permute-done | bytes 393248 | tf_op jit(solution)/shard_map/while/body/eval_jaxpr/ppermute | solution.py:141
  1811.2 37.9 %collective-permute-done.2 = bf16[1,256,12,64]{1,3,2,0:T(8,128)(2,1)} collective-permute-done((bf16[1,256,12,64]{1,3,2,0:T(8,128)(2,1)}, bf16[1,256,12,64]{1,3,2,0:T(8,128)(2,1)}, u32[]{:S(2)}, u32[]{:S(2)}) %collective-permute-start.2) | collective-permute-done | bytes 393248 | tf_op jit(solution)/shard_map/while/body/eval_jaxpr/ppermute | solution.py:141
  1857.0 37.9 %collective-permute-done.2 = bf16[1,256,12,64]{1,3,2,0:T(8,128)(2,1)} collective-permute-done((bf16[1,256,12,64]{1,3,2,0:T(8,128)(2,1)}, bf16[1,256,12,64]{1,3,2,0:T(8,128)(2,1)}, u32[]{:S(2)}, u32[]{:S(2)}) %collective-permute-start.2) | collective-permute-done | bytes 393248 | tf_op jit(solution)/shard_map/while/body/eval_jaxpr/ppermute | solution.py:141
  1902.9 37.9 %collective-permute-done.2 = bf16[1,256,12,64]{1,3,2,0:T(8,128)(2,1)} collective-permute-done((bf16[1,256,12,64]{1,3,2,0:T(8,128)(2,1)}, bf16[1,256,12,64]{1,3,2,0:T(8,128)(2,1)}, u32[]{:S(2)}, u32[]{:S(2)}) %collective-permute-start.2) | collective-permute-done | bytes 393248 | tf_op jit(solution)/shard_map/while/body/eval_jaxpr/ppermute | solution.py:141
  1948.7 37.9 %collective-permute-done.2 = bf16[1,256,12,64]{1,3,2,0:T(8,128)(2,1)} collective-permute-done((bf16[1,256,12,64]{1,3,2,0:T(8,128)(2,1)}, bf16[1,256,12,64]{1,3,2,0:T(8,128)(2,1)}, u32[]{:S(2)}, u32[]{:S(2)}) %collective-permute-start.2) | collective-permute-done | bytes 393248 | tf_op jit(solution)/shard_map/while/body/eval_jaxpr/ppermute | solution.py:141
  1994.5 37.9 %collective-permute-done.2 = bf16[1,256,12,64]{1,3,2,0:T(8,128)(2,1)} collective-permute-done((bf16[1,256,12,64]{1,3,2,0:T(8,128)(2,1)}, bf16[1,256,12,64]{1,3,2,0:T(8,128)(2,1)}, u32[]{:S(2)}, u32[]{:S(2)}) %collective-permute-start.2) | collective-permute-done | bytes 393248 | tf_op jit(solution)/shard_map/while/body/eval_jaxpr/ppermute | solution.py:141
  2098.9 103.5 %all-reduce = (f32[768]{0:T(1024)}, f32[768]{0:T(1024)}, f32[768]{0:T(1024)}, f32[768]{0:T(1024)}, f32[12,3,64]{2,0,1:T(8,128)}, /*index=5*/f32[768]{0:T(1024)}, f32[3072]{0:T(1024)}) all-reduce(f32[768]{0:T(1024)} %get-tuple-element.445, f32[768]{0:T(1024)} %get-tuple-element.442, ...), channel_id=1, replica_groups=mesh['dp'=1,'cp'=32] {'cp'}, use_global_device_ids=true, to_apply=%region_20.21 | all-reduce | flops 9216 | bytes 73728 | tf_op jit(solution)/shard_map/psum | solution.py:167
  2209.4 138.7 %all-reduce.4.cloned.1.call-done = (f32[768,12,3,64]{0,3,2,1:T(8,128)}, f32[768,768]{1,0:T(8,128)}, f32[768,3072]{1,0:T(8,128)}, f32[3072,768]{1,0:T(8,128)}) async-done(((f32[768,12,3,64]{0,3,2,1:T(8,128)}, f32[768,768]{1,0:T(8,128)}, f32[768,3072]{1,0:T(8,128)}, f32[3072,768]{1,0:T(8,128)}), (f32[768,12,3,64]{0,3,2,1:T(8,128)}, f32[768,768]{1,0:T(8,128)}, f32[768,3072]{1,0:T(8,128)}, ...) | async-done | bytes 28311568 | tf_op jit(solution)/shard_map/psum | solution.py:167
  (860 shorter events, 1141.9 us)
Async XLA Ops:
  7.2 2340.9 %all-reduce.4.cloned.1.call-start = ((), (), s32[]{:S(2)}) async-start(), calls=%async_computation | async-start | bytes 56623104 | tf_op jit(solution)/shard_map/psum | solution.py:167
  738.0 41.6 %collective-permute-start.4 = (f32[1,256,12,64]{1,3,2,0:T(8,128)}, f32[1,256,12,64]{1,3,2,0:T(8,128)}, u32[]{:S(2)}, u32[]{:S(2)}) collective-permute-start(f32[1,256,12,64]{1,3,2,0:T(8,128)} %get-tuple-element.721), channel_id=1, source_target_pairs={{0,1},{1,2},{2,3},{3,4},{4,5},{5,6},{6,7},{7,8},{8,9},{9,10},{10,1... | collective-permute-start | bytes 2359304 | tf_op jit(solution)/shard_map/while/body/eval_jaxpr/ppermute | solution.py:141
  1078.0 41.6 %collective-permute-start.4 = (f32[1,256,12,64]{1,3,2,0:T(8,128)}, f32[1,256,12,64]{1,3,2,0:T(8,128)}, u32[]{:S(2)}, u32[]{:S(2)}) collective-permute-start(f32[1,256,12,64]{1,3,2,0:T(8,128)} %get-tuple-element.721), channel_id=1, source_target_pairs={{0,1},{1,2},{2,3},{3,4},{4,5},{5,6},{6,7},{7,8},{8,9},{9,10},{10,1... | collective-permute-start | bytes 2359304 | tf_op jit(solution)/shard_map/while/body/eval_jaxpr/ppermute | solution.py:141
  1078.0 41.6 %collective-permute-start.5 = (f32[1,256,12,64]{1,3,2,0:T(8,128)}, f32[1,256,12,64]{1,3,2,0:T(8,128)}, u32[]{:S(2)}, u32[]{:S(2)}) collective-permute-start(f32[1,256,12,64]{1,3,2,0:T(8,128)} %get-tuple-element.722), channel_id=1, source_target_pairs={{0,1},{1,2},{2,3},{3,4},{4,5},{5,6},{6,7},{7,8},{8,9},{9,10},{10,1... | collective-permute-start | bytes 2359304 | tf_op jit(solution)/shard_map/while/body/eval_jaxpr/ppermute | solution.py:141
  1123.8 41.6 %collective-permute-start.4 = (f32[1,256,12,64]{1,3,2,0:T(8,128)}, f32[1,256,12,64]{1,3,2,0:T(8,128)}, u32[]{:S(2)}, u32[]{:S(2)}) collective-permute-start(f32[1,256,12,64]{1,3,2,0:T(8,128)} %get-tuple-element.721), channel_id=1, source_target_pairs={{0,1},{1,2},{2,3},{3,4},{4,5},{5,6},{6,7},{7,8},{8,9},{9,10},{10,1... | collective-permute-start | bytes 2359304 | tf_op jit(solution)/shard_map/while/body/eval_jaxpr/ppermute | solution.py:141
  1123.8 41.6 %collective-permute-start.5 = (f32[1,256,12,64]{1,3,2,0:T(8,128)}, f32[1,256,12,64]{1,3,2,0:T(8,128)}, u32[]{:S(2)}, u32[]{:S(2)}) collective-permute-start(f32[1,256,12,64]{1,3,2,0:T(8,128)} %get-tuple-element.722), channel_id=1, source_target_pairs={{0,1},{1,2},{2,3},{3,4},{4,5},{5,6},{6,7},{7,8},{8,9},{9,10},{10,1... | collective-permute-start | bytes 2359304 | tf_op jit(solution)/shard_map/while/body/eval_jaxpr/ppermute | solution.py:141
  1169.6 41.6 %collective-permute-start.4 = (f32[1,256,12,64]{1,3,2,0:T(8,128)}, f32[1,256,12,64]{1,3,2,0:T(8,128)}, u32[]{:S(2)}, u32[]{:S(2)}) collective-permute-start(f32[1,256,12,64]{1,3,2,0:T(8,128)} %get-tuple-element.721), channel_id=1, source_target_pairs={{0,1},{1,2},{2,3},{3,4},{4,5},{5,6},{6,7},{7,8},{8,9},{9,10},{10,1... | collective-permute-start | bytes 2359304 | tf_op jit(solution)/shard_map/while/body/eval_jaxpr/ppermute | solution.py:141
  1169.6 41.6 %collective-permute-start.5 = (f32[1,256,12,64]{1,3,2,0:T(8,128)}, f32[1,256,12,64]{1,3,2,0:T(8,128)}, u32[]{:S(2)}, u32[]{:S(2)}) collective-permute-start(f32[1,256,12,64]{1,3,2,0:T(8,128)} %get-tuple-element.722), channel_id=1, source_target_pairs={{0,1},{1,2},{2,3},{3,4},{4,5},{5,6},{6,7},{7,8},{8,9},{9,10},{10,1... | collective-permute-start | bytes 2359304 | tf_op jit(solution)/shard_map/while/body/eval_jaxpr/ppermute | solution.py:141
  1215.4 41.6 %collective-permute-start.4 = (f32[1,256,12,64]{1,3,2,0:T(8,128)}, f32[1,256,12,64]{1,3,2,0:T(8,128)}, u32[]{:S(2)}, u32[]{:S(2)}) collective-permute-start(f32[1,256,12,64]{1,3,2,0:T(8,128)} %get-tuple-element.721), channel_id=1, source_target_pairs={{0,1},{1,2},{2,3},{3,4},{4,5},{5,6},{6,7},{7,8},{8,9},{9,10},{10,1... | collective-permute-start | bytes 2359304 | tf_op jit(solution)/shard_map/while/body/eval_jaxpr/ppermute | solution.py:141
  1215.4 41.6 %collective-permute-start.5 = (f32[1,256,12,64]{1,3,2,0:T(8,128)}, f32[1,256,12,64]{1,3,2,0:T(8,128)}, u32[]{:S(2)}, u32[]{:S(2)}) collective-permute-start(f32[1,256,12,64]{1,3,2,0:T(8,128)} %get-tuple-element.722), channel_id=1, source_target_pairs={{0,1},{1,2},{2,3},{3,4},{4,5},{5,6},{6,7},{7,8},{8,9},{9,10},{10,1... | collective-permute-start | bytes 2359304 | tf_op jit(solution)/shard_map/while/body/eval_jaxpr/ppermute | solution.py:141
  1261.2 41.6 %collective-permute-start.4 = (f32[1,256,12,64]{1,3,2,0:T(8,128)}, f32[1,256,12,64]{1,3,2,0:T(8,128)}, u32[]{:S(2)}, u32[]{:S(2)}) collective-permute-start(f32[1,256,12,64]{1,3,2,0:T(8,128)} %get-tuple-element.721), channel_id=1, source_target_pairs={{0,1},{1,2},{2,3},{3,4},{4,5},{5,6},{6,7},{7,8},{8,9},{9,10},{10,1... | collective-permute-start | bytes 2359304 | tf_op jit(solution)/shard_map/while/body/eval_jaxpr/ppermute | solution.py:141
  1261.2 41.6 %collective-permute-start.5 = (f32[1,256,12,64]{1,3,2,0:T(8,128)}, f32[1,256,12,64]{1,3,2,0:T(8,128)}, u32[]{:S(2)}, u32[]{:S(2)}) collective-permute-start(f32[1,256,12,64]{1,3,2,0:T(8,128)} %get-tuple-element.722), channel_id=1, source_target_pairs={{0,1},{1,2},{2,3},{3,4},{4,5},{5,6},{6,7},{7,8},{8,9},{9,10},{10,1... | collective-permute-start | bytes 2359304 | tf_op jit(solution)/shard_map/while/body/eval_jaxpr/ppermute | solution.py:141
  1307.1 41.6 %collective-permute-start.4 = (f32[1,256,12,64]{1,3,2,0:T(8,128)}, f32[1,256,12,64]{1,3,2,0:T(8,128)}, u32[]{:S(2)}, u32[]{:S(2)}) collective-permute-start(f32[1,256,12,64]{1,3,2,0:T(8,128)} %get-tuple-element.721), channel_id=1, source_target_pairs={{0,1},{1,2},{2,3},{3,4},{4,5},{5,6},{6,7},{7,8},{8,9},{9,10},{10,1... | collective-permute-start | bytes 2359304 | tf_op jit(solution)/shard_map/while/body/eval_jaxpr/ppermute | solution.py:141
  1307.1 41.6 %collective-permute-start.5 = (f32[1,256,12,64]{1,3,2,0:T(8,128)}, f32[1,256,12,64]{1,3,2,0:T(8,128)}, u32[]{:S(2)}, u32[]{:S(2)}) collective-permute-start(f32[1,256,12,64]{1,3,2,0:T(8,128)} %get-tuple-element.722), channel_id=1, source_target_pairs={{0,1},{1,2},{2,3},{3,4},{4,5},{5,6},{6,7},{7,8},{8,9},{9,10},{10,1... | collective-permute-start | bytes 2359304 | tf_op jit(solution)/shard_map/while/body/eval_jaxpr/ppermute | solution.py:141
  1352.9 41.6 %collective-permute-start.4 = (f32[1,256,12,64]{1,3,2,0:T(8,128)}, f32[1,256,12,64]{1,3,2,0:T(8,128)}, u32[]{:S(2)}, u32[]{:S(2)}) collective-permute-start(f32[1,256,12,64]{1,3,2,0:T(8,128)} %get-tuple-element.721), channel_id=1, source_target_pairs={{0,1},{1,2},{2,3},{3,4},{4,5},{5,6},{6,7},{7,8},{8,9},{9,10},{10,1... | collective-permute-start | bytes 2359304 | tf_op jit(solution)/shard_map/while/body/eval_jaxpr/ppermute | solution.py:141
  1352.9 41.6 %collective-permute-start.5 = (f32[1,256,12,64]{1,3,2,0:T(8,128)}, f32[1,256,12,64]{1,3,2,0:T(8,128)}, u32[]{:S(2)}, u32[]{:S(2)}) collective-permute-start(f32[1,256,12,64]{1,3,2,0:T(8,128)} %get-tuple-element.722), channel_id=1, source_target_pairs={{0,1},{1,2},{2,3},{3,4},{4,5},{5,6},{6,7},{7,8},{8,9},{9,10},{10,1... | collective-permute-start | bytes 2359304 | tf_op jit(solution)/shard_map/while/body/eval_jaxpr/ppermute | solution.py:141
  1398.7 41.6 %collective-permute-start.4 = (f32[1,256,12,64]{1,3,2,0:T(8,128)}, f32[1,256,12,64]{1,3,2,0:T(8,128)}, u32[]{:S(2)}, u32[]{:S(2)}) collective-permute-start(f32[1,256,12,64]{1,3,2,0:T(8,128)} %get-tuple-element.721), channel_id=1, source_target_pairs={{0,1},{1,2},{2,3},{3,4},{4,5},{5,6},{6,7},{7,8},{8,9},{9,10},{10,1... | collective-permute-start | bytes 2359304 | tf_op jit(solution)/shard_map/while/body/eval_jaxpr/ppermute | solution.py:141
  1398.7 41.6 %collective-permute-start.5 = (f32[1,256,12,64]{1,3,2,0:T(8,128)}, f32[1,256,12,64]{1,3,2,0:T(8,128)}, u32[]{:S(2)}, u32[]{:S(2)}) collective-permute-start(f32[1,256,12,64]{1,3,2,0:T(8,128)} %get-tuple-element.722), channel_id=1, source_target_pairs={{0,1},{1,2},{2,3},{3,4},{4,5},{5,6},{6,7},{7,8},{8,9},{9,10},{10,1... | collective-permute-start | bytes 2359304 | tf_op jit(solution)/shard_map/while/body/eval_jaxpr/ppermute | solution.py:141
  1444.5 41.6 %collective-permute-start.4 = (f32[1,256,12,64]{1,3,2,0:T(8,128)}, f32[1,256,12,64]{1,3,2,0:T(8,128)}, u32[]{:S(2)}, u32[]{:S(2)}) collective-permute-start(f32[1,256,12,64]{1,3,2,0:T(8,128)} %get-tuple-element.721), channel_id=1, source_target_pairs={{0,1},{1,2},{2,3},{3,4},{4,5},{5,6},{6,7},{7,8},{8,9},{9,10},{10,1... | collective-permute-start | bytes 2359304 | tf_op jit(solution)/shard_map/while/body/eval_jaxpr/ppermute | solution.py:141
  1444.5 41.6 %collective-permute-start.5 = (f32[1,256,12,64]{1,3,2,0:T(8,128)}, f32[1,256,12,64]{1,3,2,0:T(8,128)}, u32[]{:S(2)}, u32[]{:S(2)}) collective-permute-start(f32[1,256,12,64]{1,3,2,0:T(8,128)} %get-tuple-element.722), channel_id=1, source_target_pairs={{0,1},{1,2},{2,3},{3,4},{4,5},{5,6},{6,7},{7,8},{8,9},{9,10},{10,1... | collective-permute-start | bytes 2359304 | tf_op jit(solution)/shard_map/while/body/eval_jaxpr/ppermute | solution.py:141
  1490.3 41.6 %collective-permute-start.4 = (f32[1,256,12,64]{1,3,2,0:T(8,128)}, f32[1,256,12,64]{1,3,2,0:T(8,128)}, u32[]{:S(2)}, u32[]{:S(2)}) collective-permute-start(f32[1,256,12,64]{1,3,2,0:T(8,128)} %get-tuple-element.721), channel_id=1, source_target_pairs={{0,1},{1,2},{2,3},{3,4},{4,5},{5,6},{6,7},{7,8},{8,9},{9,10},{10,1... | collective-permute-start | bytes 2359304 | tf_op jit(solution)/shard_map/while/body/eval_jaxpr/ppermute | solution.py:141
  1490.3 41.6 %collective-permute-start.5 = (f32[1,256,12,64]{1,3,2,0:T(8,128)}, f32[1,256,12,64]{1,3,2,0:T(8,128)}, u32[]{:S(2)}, u32[]{:S(2)}) collective-permute-start(f32[1,256,12,64]{1,3,2,0:T(8,128)} %get-tuple-element.722), channel_id=1, source_target_pairs={{0,1},{1,2},{2,3},{3,4},{4,5},{5,6},{6,7},{7,8},{8,9},{9,10},{10,1... | collective-permute-start | bytes 2359304 | tf_op jit(solution)/shard_map/while/body/eval_jaxpr/ppermute | solution.py:141
  1536.2 41.6 %collective-permute-start.4 = (f32[1,256,12,64]{1,3,2,0:T(8,128)}, f32[1,256,12,64]{1,3,2,0:T(8,128)}, u32[]{:S(2)}, u32[]{:S(2)}) collective-permute-start(f32[1,256,12,64]{1,3,2,0:T(8,128)} %get-tuple-element.721), channel_id=1, source_target_pairs={{0,1},{1,2},{2,3},{3,4},{4,5},{5,6},{6,7},{7,8},{8,9},{9,10},{10,1... | collective-permute-start | bytes 2359304 | tf_op jit(solution)/shard_map/while/body/eval_jaxpr/ppermute | solution.py:141
  1536.2 41.6 %collective-permute-start.5 = (f32[1,256,12,64]{1,3,2,0:T(8,128)}, f32[1,256,12,64]{1,3,2,0:T(8,128)}, u32[]{:S(2)}, u32[]{:S(2)}) collective-permute-start(f32[1,256,12,64]{1,3,2,0:T(8,128)} %get-tuple-element.722), channel_id=1, source_target_pairs={{0,1},{1,2},{2,3},{3,4},{4,5},{5,6},{6,7},{7,8},{8,9},{9,10},{10,1... | collective-permute-start | bytes 2359304 | tf_op jit(solution)/shard_map/while/body/eval_jaxpr/ppermute | solution.py:141
  1582.0 41.6 %collective-permute-start.4 = (f32[1,256,12,64]{1,3,2,0:T(8,128)}, f32[1,256,12,64]{1,3,2,0:T(8,128)}, u32[]{:S(2)}, u32[]{:S(2)}) collective-permute-start(f32[1,256,12,64]{1,3,2,0:T(8,128)} %get-tuple-element.721), channel_id=1, source_target_pairs={{0,1},{1,2},{2,3},{3,4},{4,5},{5,6},{6,7},{7,8},{8,9},{9,10},{10,1... | collective-permute-start | bytes 2359304 | tf_op jit(solution)/shard_map/while/body/eval_jaxpr/ppermute | solution.py:141
  1582.0 41.6 %collective-permute-start.5 = (f32[1,256,12,64]{1,3,2,0:T(8,128)}, f32[1,256,12,64]{1,3,2,0:T(8,128)}, u32[]{:S(2)}, u32[]{:S(2)}) collective-permute-start(f32[1,256,12,64]{1,3,2,0:T(8,128)} %get-tuple-element.722), channel_id=1, source_target_pairs={{0,1},{1,2},{2,3},{3,4},{4,5},{5,6},{6,7},{7,8},{8,9},{9,10},{10,1... | collective-permute-start | bytes 2359304 | tf_op jit(solution)/shard_map/while/body/eval_jaxpr/ppermute | solution.py:141
  1627.8 41.6 %collective-permute-start.4 = (f32[1,256,12,64]{1,3,2,0:T(8,128)}, f32[1,256,12,64]{1,3,2,0:T(8,128)}, u32[]{:S(2)}, u32[]{:S(2)}) collective-permute-start(f32[1,256,12,64]{1,3,2,0:T(8,128)} %get-tuple-element.721), channel_id=1, source_target_pairs={{0,1},{1,2},{2,3},{3,4},{4,5},{5,6},{6,7},{7,8},{8,9},{9,10},{10,1... | collective-permute-start | bytes 2359304 | tf_op jit(solution)/shard_map/while/body/eval_jaxpr/ppermute | solution.py:141
  1627.8 41.6 %collective-permute-start.5 = (f32[1,256,12,64]{1,3,2,0:T(8,128)}, f32[1,256,12,64]{1,3,2,0:T(8,128)}, u32[]{:S(2)}, u32[]{:S(2)}) collective-permute-start(f32[1,256,12,64]{1,3,2,0:T(8,128)} %get-tuple-element.722), channel_id=1, source_target_pairs={{0,1},{1,2},{2,3},{3,4},{4,5},{5,6},{6,7},{7,8},{8,9},{9,10},{10,1... | collective-permute-start | bytes 2359304 | tf_op jit(solution)/shard_map/while/body/eval_jaxpr/ppermute | solution.py:141
  1673.6 41.6 %collective-permute-start.4 = (f32[1,256,12,64]{1,3,2,0:T(8,128)}, f32[1,256,12,64]{1,3,2,0:T(8,128)}, u32[]{:S(2)}, u32[]{:S(2)}) collective-permute-start(f32[1,256,12,64]{1,3,2,0:T(8,128)} %get-tuple-element.721), channel_id=1, source_target_pairs={{0,1},{1,2},{2,3},{3,4},{4,5},{5,6},{6,7},{7,8},{8,9},{9,10},{10,1... | collective-permute-start | bytes 2359304 | tf_op jit(solution)/shard_map/while/body/eval_jaxpr/ppermute | solution.py:141
  1673.6 41.6 %collective-permute-start.5 = (f32[1,256,12,64]{1,3,2,0:T(8,128)}, f32[1,256,12,64]{1,3,2,0:T(8,128)}, u32[]{:S(2)}, u32[]{:S(2)}) collective-permute-start(f32[1,256,12,64]{1,3,2,0:T(8,128)} %get-tuple-element.722), channel_id=1, source_target_pairs={{0,1},{1,2},{2,3},{3,4},{4,5},{5,6},{6,7},{7,8},{8,9},{9,10},{10,1... | collective-permute-start | bytes 2359304 | tf_op jit(solution)/shard_map/while/body/eval_jaxpr/ppermute | solution.py:141
  1719.4 41.6 %collective-permute-start.4 = (f32[1,256,12,64]{1,3,2,0:T(8,128)}, f32[1,256,12,64]{1,3,2,0:T(8,128)}, u32[]{:S(2)}, u32[]{:S(2)}) collective-permute-start(f32[1,256,12,64]{1,3,2,0:T(8,128)} %get-tuple-element.721), channel_id=1, source_target_pairs={{0,1},{1,2},{2,3},{3,4},{4,5},{5,6},{6,7},{7,8},{8,9},{9,10},{10,1... | collective-permute-start | bytes 2359304 | tf_op jit(solution)/shard_map/while/body/eval_jaxpr/ppermute | solution.py:141
  1902.7 41.6 %collective-permute-start.4 = (f32[1,256,12,64]{1,3,2,0:T(8,128)}, f32[1,256,12,64]{1,3,2,0:T(8,128)}, u32[]{:S(2)}, u32[]{:S(2)}) collective-permute-start(f32[1,256,12,64]{1,3,2,0:T(8,128)} %get-tuple-element.721), channel_id=1, source_target_pairs={{0,1},{1,2},{2,3},{3,4},{4,5},{5,6},{6,7},{7,8},{8,9},{9,10},{10,1... | collective-permute-start | bytes 2359304 | tf_op jit(solution)/shard_map/while/body/eval_jaxpr/ppermute | solution.py:141
  (245 other events, 4760.3 us)
Sparse Core Ops, SparseCore 0:
  2084.5 263.5 all-reduce.3
where the time goes:
time: 2390 us; the launch traced here: 2380 us
  waiting for transfers between devices  1580 us (66%)
  local copies, waits for them, and re-layouts  388 us (16%)
  starting transfers between devices  195 us (8%)
  blocking collectives  104 us (4%)
  matrix products  70.1 us (3%)
  other arithmetic  24.4 us (1%)
    ppermute x124, waiting for transfers between devices, bwd_step(): lax.ppermute((k_cur, v_cur, dk_cur, dv_cur), 'cp', shift_perm)  1070 us
    ppermute x62, waiting for transfers between devices, fwd_step(): k_cur, v_cur = lax.ppermute((k_cur, v_cur), 'cp', shift_perm)  364 us
    while x186, local copies, waits for them, and re-layouts  349 us
    psum x1, waiting for transfers between devices, local_layer(): lax.psum((d_ln1_gain, d_ln1_bias, d_ln2_gain, d_ln2_bias, d_w_qkv, d_b_qk...  139 us
    ppermute x62, starting transfers between devices, fwd_step(): k_cur, v_cur = lax.ppermute((k_cur, v_cur), 'cp', shift_perm)  135 us
    psum x1, blocking collectives, local_layer(): lax.psum((d_ln1_gain, d_ln1_bias, d_ln2_gain, d_ln2_bias, d_w_qkv, d_b_qk...  104 us
    ppermute x124, starting transfers between devices, bwd_step(): lax.ppermute((k_cur, v_cur, dk_cur, dv_cur), 'cp', shift_perm)  60.5 us
  transfers between devices with their start and end apart: 189, of which 97 were waited for; matrix products, arithmetic and copies ran while one was open for 7% of the time, Pallas kernels for 0%

commit v1 on v0

v1 whole, which is shorter than its diff:
```python
import functools

import jax
import jax.numpy as jnp
from jax import lax
from jax.experimental import pallas as pl
from jax.experimental.pallas import tpu as pltpu
from jax.sharding import PartitionSpec as P

EPS = 1e-5
ROPE_BASE = 10000.0
NEG_BIG = -1e30
VMEM_LIMIT = 60 * 1024 * 1024
NN = (((1,), (0,)), ((), ()))
NT = (((1,), (1,)), ((), ()))


def mm(a, b, dims=NN):
    return lax.dot_general(a, b, dims, preferred_element_type=jnp.float32)


def layer_norm(row_vals, norm_gain, norm_shift):
    row_mean = jnp.mean(row_vals, axis=-1, keepdims=True)
    centered = row_vals - row_mean
    inv_std = lax.rsqrt(jnp.mean(centered * centered, axis=-1, keepdims=True) + EPS)
    x_norm = centered * inv_std
    return x_norm * norm_gain + norm_shift, x_norm, inv_std


def norm_backward(d_out, x_norm, inv_std, norm_gain):
    d_norm = d_out * norm_gain
    d_rows = inv_std * (d_norm - jnp.mean(d_norm, axis=-1, keepdims=True) - x_norm * jnp.mean(d_norm * x_norm, axis=-1, keepdims=True))
    return d_rows, jnp.sum(d_out * x_norm, axis=0), jnp.sum(d_out, axis=0)


def rope_angles(positions, head_dim):
    rot_dim = head_dim // 4
    inv_freq = ROPE_BASE ** (-2.0 * jnp.arange(rot_dim // 2, dtype=jnp.float32) / rot_dim)
    return positions.astype(jnp.float32)[:, None] * inv_freq[None, :]


def lane_tables(cos_t, sin_t, head_dim):
    rows, half = cos_t.shape
    rest = head_dim - 2 * half
    one = jnp.concatenate([cos_t, cos_t, jnp.ones((rows, rest), jnp.float32)], axis=1)
    two = jnp.concatenate([-sin_t, sin_t, jnp.zeros((rows, rest), jnp.float32)], axis=1)
    return jnp.concatenate([one, one], axis=1), jnp.concatenate([two, two], axis=1)


def rotate(z, cos_l, sin_l, half, head_dim):
    lane = lax.broadcasted_iota(jnp.int32, cos_l.shape, 1) % head_dim
    low = lane < half
    parts = []
    for t in range(z.shape[1] // 128):
        zt = z[:, t * 128:(t + 1) * 128]
        partner = jnp.where(low, pltpu.roll(zt, 128 - half, 1), pltpu.roll(zt, half, 1))
        parts.append(zt * cos_l + partner * sin_l)
    return jnp.concatenate(parts, axis=1)


def exact_gelu(pre):
    cdf = 0.5 * (1.0 + lax.erf(pre * (0.5 ** 0.5)))
    pdf = jnp.exp(-0.5 * pre * pre) * 0.3989422804014327
    return pre * cdf, cdf + pre * pdf


def put_masked(dst, mat_t, hd):
    pairs = mat_t.shape[0] // (2 * hd)
    rows = lax.broadcasted_iota(jnp.int32, (2 * hd, mat_t.shape[1]), 0)
    for p in range(pairs):
        blk = mat_t[p * 2 * hd:(p + 1) * 2 * hd]
        zero = jnp.zeros_like(blk)
        dst[2 * p] = jnp.where(rows < hd, blk, zero)
        dst[2 * p + 1] = jnp.where(rows < hd, zero, blk)


def fwd_kernel(hd, me_ref, x_hbm, cos_hbm, sin_hbm, g_ref, s_ref, wq_ref, wk_ref, wv_ref, b_ref,
               k_hbm, v_hbm, ctx_ref, lse_ref, qt_ref,
               xb, cb, sb, kst, vst, qtm, acc, mrow, lrow, in_sem, out_sem):
    me = me_ref[0]
    T = xb.shape[1]
    W = xb.shape[2]
    heads = W // hd
    half = hd // 8
    scale = hd ** -0.5

    def fetch(j, slot):
        return (pltpu.make_async_copy(x_hbm.at[pl.ds(j * T, T)], xb.at[slot], in_sem.at[slot, 0]),
                pltpu.make_async_copy(cos_hbm.at[pl.ds(j * T, T)], cb.at[slot], in_sem.at[slot, 1]),
                pltpu.make_async_copy(sin_hbm.at[pl.ds(j * T, T)], sb.at[slot], in_sem.at[slot, 2]))

    def flush(j, slot):
        return (pltpu.make_async_copy(kst.at[slot], k_hbm.at[pl.ds(j * T, T)], out_sem.at[slot, 0]),
                pltpu.make_async_copy(vst.at[slot], v_hbm.at[pl.ds(j * T, T)], out_sem.at[slot, 1]))

    def project(slot, with_q):
        h = layer_norm(xb[slot].astype(jnp.float32), g_ref[...], s_ref[...])[0].astype(jnp.bfloat16)
        k = rotate(mm(h, wk_ref[...]) + b_ref[1:2], cb[slot], sb[slot], half, hd)
        kst[slot] = k.astype(jnp.bfloat16)
        vst[slot] = (mm(h, wv_ref[...]) + b_ref[2:3]).astype(jnp.bfloat16)
        if with_q:
            q = rotate(mm(h, wq_ref[...]) + b_ref[0:1], cb[slot], sb[slot], half, hd)
            q = q.astype(jnp.bfloat16) * jnp.bfloat16(scale)
            qt = q.T
            qt_ref[...] = qt
            put_masked(qtm, qt, hd)

    def attend(slot, diag):
        if diag:
            keep = lax.broadcasted_iota(jnp.int32, (T, T), 0) <= lax.broadcasted_iota(jnp.int32, (T, T), 1)
        for p in range(heads // 2):
            cols = slice(p * 2 * hd, (p + 1) * 2 * hd)
            kp = kst[slot, :, cols]
            vt = vst[slot, :, cols].T
            for h in (2 * p, 2 * p + 1):
                s = mm(kp, qtm[h])
                rows = slice(h * hd, (h + 1) * hd)
                vh = vt[(h % 2) * hd:(h % 2 + 1) * hd]
                if diag:
                    s = jnp.where(keep, s, NEG_BIG)
                    m = jnp.max(s, axis=0, keepdims=True)
                    e = jnp.exp(s - m)
                    lrow[h:h + 1] = jnp.sum(e, axis=0, keepdims=True)
                    acc[rows] = mm(vh, e.astype(jnp.bfloat16))
                else:
                    m_old = mrow[h:h + 1]
                    m = jnp.maximum(m_old, jnp.max(s, axis=0, keepdims=True))
                    e = jnp.exp(s - m)
                    alpha = jnp.exp(m_old - m)
                    lrow[h:h + 1] = lrow[h:h + 1] * alpha + jnp.sum(e, axis=0, keepdims=True)
                    acc[rows] = acc[rows] * alpha + mm(vh, e.astype(jnp.bfloat16))
                mrow[h:h + 1] = m

    for c in fetch(me, 0):
        c.start()

    @pl.when(me > 0)
    def _():
        for c in fetch(0, 1):
            c.start()

    for c in fetch(me, 0):
        c.wait()
    project(0, True)
    for c in flush(me, 0):
        c.start()
    attend(0, True)
    for c in flush(me, 0):
        c.wait()

    def step(j, _):
        slot = (j + 1) % 2

        @pl.when(j + 1 < me)
        def _():
            for c in fetch(j + 1, 1 - slot):
                c.start()

        for c in fetch(j, slot):
            c.wait()

        @pl.when(j >= 2)
        def _():
            for c in flush(j - 2, slot):
                c.wait()

        project(slot, False)
        for c in flush(j, slot):
            c.start()
        attend(slot, False)
        return 0

    lax.fori_loop(0, me, step, 0)

    @pl.when(me >= 1)
    def _():
        for c in flush(me - 1, me % 2):
            c.wait()

    @pl.when(me >= 2)
    def _():
        for c in flush(me - 2, (me + 1) % 2):
            c.wait()

    lse_ref[...] = mrow[...] + jnp.log(lrow[...])
    inv = 1.0 / lrow[...]
    for p in range(heads // 2):
        a = acc[2 * p * hd:(2 * p + 1) * hd] * inv[2 * p:2 * p + 1]
        b = acc[(2 * p + 1) * hd:(2 * p + 2) * hd] * inv[2 * p + 1:2 * p + 2]
        ctx_ref[:, 2 * p * hd:(2 * p + 2) * hd] = jnp.concatenate([a, b], axis=0).T


def fwd_attention(me, x_all, cos_l, sin_l, gain, shift, wq, wk, wv, b3, T, hd):
    S, W = x_all.shape
    heads = W // hd
    vm = pl.BlockSpec(memory_space=pltpu.VMEM)
    anym = pl.BlockSpec(memory_space=pl.ANY)
    f32, bf = jnp.float32, jnp.bfloat16
    return pl.pallas_call(
        functools.partial(fwd_kernel, hd),
        out_shape=[jax.ShapeDtypeStruct((S, W), bf), jax.ShapeDtypeStruct((S, W), bf), jax.ShapeDtypeStruct((T, W), f32),
                   jax.ShapeDtypeStruct((heads, T), f32), jax.ShapeDtypeStruct((W, T), bf)],
        in_specs=[pl.BlockSpec(memory_space=pltpu.SMEM), anym, anym, anym] + [vm] * 6,
        out_specs=[anym, anym, vm, vm, vm],
        scratch_shapes=[pltpu.VMEM((2, T, W), bf), pltpu.VMEM((2, T, 128), f32), pltpu.VMEM((2, T, 128), f32),
                        pltpu.VMEM((2, T, W), bf), pltpu.VMEM((2, T, W), bf), pltpu.VMEM((heads, 2 * hd, T), bf),
                        pltpu.VMEM((W, T), f32), pltpu.VMEM((heads, T), f32), pltpu.VMEM((heads, T), f32),
                        pltpu.SemaphoreType.DMA((2, 3)), pltpu.SemaphoreType.DMA((2, 2))],
        compiler_params=pltpu.CompilerParams(vmem_limit_bytes=VMEM_LIMIT),
        cost_estimate=pl.CostEstimate(flops=40_000_000_000, bytes_accessed=40_000_000, transcendentals=0),
        name="attn_fwd",
    )(me, x_all, cos_l, sin_l, gain, shift, wq, wk, wv, b3)


def bwd_kernel(hd, n, me_ref, x_hbm, dy_hbm, cos_hbm, sin_hbm, k_hbm, v_hbm, stats_ref, qt_ref, own_ref, g_ref, s_ref,
               wq_ref, wot_ref, bq_ref, dq_ref, dk_ref, dv_ref,
               xb, yb, cb, sb, qsc, osc, am, bm, acc1, acc2, in_sem):
    me = me_ref[0]
    T = xb.shape[1]
    W = xb.shape[2]
    heads = W // hd
    half = hd // 8
    scale = hd ** -0.5

    def fetch_kv(j, slot):
        return (pltpu.make_async_copy(k_hbm.at[pl.ds(j * T, T)], xb.at[slot], in_sem.at[slot, 0]),
                pltpu.make_async_copy(v_hbm.at[pl.ds(j * T, T)], yb.at[slot], in_sem.at[slot, 1]))

    def fetch_xy(j, slot):
        return (pltpu.make_async_copy(x_hbm.at[pl.ds(j * T, T)], xb.at[slot], in_sem.at[slot, 0]),
                pltpu.make_async_copy(dy_hbm.at[pl.ds(j * T, T)], yb.at[slot], in_sem.at[slot, 1]),
                pltpu.make_async_copy(cos_hbm.at[pl.ds(j * T, T)], cb.at[slot], in_sem.at[slot, 2]),
                pltpu.make_async_copy(sin_hbm.at[pl.ds(j * T, T)], sb.at[slot], in_sem.at[slot, 3]))

    low_tri = lambda: lax.broadcasted_iota(jnp.int32, (T, T), 0) <= lax.broadcasted_iota(jnp.int32, (T, T), 1)

    put_masked(am, qt_ref[...], hd)
    put_masked(bm, own_ref[...].T, hd)
    acc1[...] = jnp.zeros_like(acc1)

    def dq_block(slot, diag):
        for p in range(heads // 2):
            cols = slice(p * 2 * hd, (p + 1) * 2 * hd)
            kp = xb[slot, :, cols]
            vp = yb[slot, :, cols]
            kt = kp.T
            for h in (2 * p, 2 * p + 1):
                row = pl.ds(me * 2 * heads + h, 1)
                s = mm(kp, am[h])
                if diag:
                    s = jnp.where(low_tri(), s, NEG_BIG)
                pr = jnp.exp(s - stats_ref[row, :])
                dp = mm(vp, bm[h])
                ds = (pr * (dp - stats_ref[pl.ds(me * 2 * heads + heads + h, 1), :])).astype(jnp.bfloat16)
                acc1[h * hd:(h + 1) * hd] += mm(kt[(h % 2) * hd:(h % 2 + 1) * hd], ds)

    for c in fetch_kv(0, 0):
        c.start()

    def dq_step(j, _):
        slot = j % 2
        for c in fetch_kv(j + 1, 1 - slot):
            c.start()
        for c in fetch_kv(j, slot):
            c.wait()
        dq_block(slot, False)
        return 0

    lax.fori_loop(0, me, dq_step, 0)
    last = me % 2
    for c in fetch_kv(me, last):
        c.wait()
    for c in fetch_xy(me, 1 - last):
        c.start()
    dq_block(last, True)
    dq_ref[...] = acc1[...].T * scale

    put_masked(am, xb[last].T, hd)
    put_masked(bm, yb[last].T, hd)
    acc1[...] = jnp.zeros_like(acc1)
    acc2[...] = jnp.zeros_like(acc2)

    def dkv_block(j, slot, diag):
        h_rows = layer_norm(xb[slot].astype(jnp.float32), g_ref[...], s_ref[...])[0].astype(jnp.bfloat16)
        q = rotate(mm(h_rows, wq_ref[...]) + bq_ref[...], cb[slot], sb[slot], half, hd)
        qsc[...] = q.astype(jnp.bfloat16) * jnp.bfloat16(scale)
        osc[...] = mm(yb[slot], wot_ref[...]).astype(jnp.bfloat16)
        st = stats_ref[pl.ds(j * 2 * heads, 2 * heads), :].T
        for p in range(heads // 2):
            cols = slice(p * 2 * hd, (p + 1) * 2 * hd)
            qp = qsc[:, cols]
            op = osc[:, cols]
            qt = qp.T
            ot = op.T
            for h in (2 * p, 2 * p + 1):
                s = mm(qp, am[h])
                if diag:
                    s = jnp.where(jnp.logical_not(low_tri()) | (lax.broadcasted_iota(jnp.int32, (T, T), 0) == lax.broadcasted_iota(jnp.int32, (T, T), 1)), s, NEG_BIG)
                pr = jnp.exp(s - st[:, h:h + 1])
                half_rows = slice((h % 2) * hd, (h % 2 + 1) * hd)
                rows = slice(h * hd, (h + 1) * hd)
                acc2[rows] += mm(ot[half_rows], pr.astype(jnp.bfloat16))
                dp = mm(op, bm[h])
                ds = (pr * (dp - st[:, heads + h:heads + h + 1])).astype(jnp.bfloat16)
                acc1[rows] += mm(qt[half_rows], ds)

    first = 1 - last

    @pl.when(me + 1 < n)
    def _():
        for c in fetch_xy(me + 1, 1 - first):
            c.start()

    for c in fetch_xy(me, first):
        c.wait()
    dkv_block(me, first, True)

    def dkv_step(j, _):
        slot = (j - me + first) % 2

        @pl.when(j + 1 < n)
        def _():
            for c in fetch_xy(j + 1, 1 - slot):
                c.start()

        for c in fetch_xy(j, slot):
            c.wait()
        dkv_block(j, slot, False)
        return 0

    lax.fori_loop(me + 1, n, dkv_step, 0)
    dk_ref[...] = acc1[...].T
    dv_ref[...] = acc2[...].T


def bwd_attention(me, x_all, dy_all, cos_l, sin_l, k_all, v_all, stats, qt, d_ctx_bf, gain, shift, wq, wot, bq, T, hd):
    S, W = x_all.shape
    heads = W // hd
    vm = pl.BlockSpec(memory_space=pltpu.VMEM)
    anym = pl.BlockSpec(memory_space=pl.ANY)
    f32, bf = jnp.float32, jnp.bfloat16
    return pl.pallas_call(
        functools.partial(bwd_kernel, hd, S // T),
        out_shape=[jax.ShapeDtypeStruct((T, W), f32)] * 3,
        in_specs=[pl.BlockSpec(memory_space=pltpu.SMEM)] + [anym] * 6 + [vm] * 8,
        out_specs=[vm] * 3,
        scratch_shapes=[pltpu.VMEM((2, T, W), bf), pltpu.VMEM((2, T, W), bf), pltpu.VMEM((2, T, 128), f32), pltpu.VMEM((2, T, 128), f32),
                        pltpu.VMEM((T, W), bf), pltpu.VMEM((T, W), bf), pltpu.VMEM((heads, 2 * hd, T), bf), pltpu.VMEM((heads, 2 * hd, T), bf),
                        pltpu.VMEM((W, T), f32), pltpu.VMEM((W, T), f32), pltpu.SemaphoreType.DMA((2, 4))],
        compiler_params=pltpu.CompilerParams(vmem_limit_bytes=VMEM_LIMIT),
        cost_estimate=pl.CostEstimate(flops=80_000_000_000, bytes_accessed=40_000_000, transcendentals=0),
        name="attn_bwd",
    )(me, x_all, dy_all, cos_l, sin_l, k_all, v_all, stats, qt, d_ctx_bf, gain, shift, wq, wot, bq)


def mlp_kernel(x_ref, dy_ref, g_ref, s_ref, wu_ref, bu_ref, wd_ref, du_ref, dd_ref, db_ref):
    @pl.when(pl.program_id(0) == 0)
    def _():
        du_ref[...] = jnp.zeros_like(du_ref)
        dd_ref[...] = jnp.zeros_like(dd_ref)
        db_ref[...] = jnp.zeros_like(db_ref)

    h = layer_norm(x_ref[...].astype(jnp.float32), g_ref[...], s_ref[...])[0].astype(jnp.bfloat16)
    dy = dy_ref[...]
    act, slope = exact_gelu(mm(h, wu_ref[...]) + bu_ref[...])
    d_up = mm(dy, wd_ref[...]) * slope
    keep = du_ref.shape[0]
    db_ref[...] += jnp.sum(d_up, axis=0, keepdims=True)
    du_ref[...] += mm(d_up.astype(jnp.bfloat16).T, h)[:keep]
    dd_ref[...] += mm(act.astype(jnp.bfloat16).T, dy)[:keep]


def mlp_grads(x_all, dy_all, gain, shift, wu, bu, wd, keep):
    S, W = x_all.shape
    F = wu.shape[1]
    R = 512
    const = lambda j: (0, 0)
    return pl.pallas_call(
        mlp_kernel,
        grid=(S // R,),
        out_shape=[jax.ShapeDtypeStruct((keep, W), jnp.float32)] * 2 + [jax.ShapeDtypeStruct((1, F), jnp.float32)],
        in_specs=[pl.BlockSpec((R, W), lambda j: (j, 0)), pl.BlockSpec((R, W), lambda j: (j, 0)), pl.BlockSpec((1, W), const), pl.BlockSpec((1, W), const),
                  pl.BlockSpec((W, F), const), pl.BlockSpec((1, F), const), pl.BlockSpec((W, F), const)],
        out_specs=[pl.BlockSpec((keep, W), const)] * 2 + [pl.BlockSpec((1, F), const)],
        compiler_params=pltpu.CompilerParams(vmem_limit_bytes=VMEM_LIMIT, dimension_semantics=("arbitrary",)),
        cost_estimate=pl.CostEstimate(flops=20_000_000_000, bytes_accessed=26_000_000, transcendentals=0),
        name="mlp_grads",
    )(x_all, dy_all, gain, shift, wu, bu, wd)


def solution(mesh):
    cp_size = mesh.shape['cp']
    row_spec = P('dp', 'cp', None)
    in_specs = (row_spec, row_spec) + (P(),) * 12
    out_specs = (row_spec, row_spec, P('dp'), P('dp'), P('dp'), P('dp'), P('dp', None, None, None), P('dp', None, None), P('dp', None), P('dp'), P('dp', None), P('dp'), P('dp', None), P('dp'))
    bf, f32 = jnp.bfloat16, jnp.float32

    def local_layer(x_blk, dy_blk, ln1_gain, ln1_bias, ln2_gain, ln2_bias, w_qkv, b_qkv, w_out, b_out, w_up, b_up, w_down, b_down):
        T, W = x_blk.shape[1:]
        heads, hd = w_qkv.shape[1], w_qkv.shape[3]
        FF = w_up.shape[1]
        S = T * cp_size
        me = lax.axis_index('cp')
        me1 = me.astype(jnp.int32).reshape(1)
        row = lambda v: v.reshape(1, -1).astype(f32)

        x_own = x_blk[0]
        dy_own = dy_blk[0]
        dy_bf = dy_own.astype(bf)
        x_all = lax.all_gather(x_own, 'cp', tiled=True)
        dy_all = lax.all_gather(dy_bf, 'cp', tiled=True)

        w3 = w_qkv.transpose(2, 0, 1, 3).reshape(3, W, W)
        b3 = b_qkv.astype(f32).transpose(1, 0, 2).reshape(3, W)
        ang = rope_angles(jnp.arange(S), hd)
        cos_l, sin_l = lane_tables(jnp.cos(ang), jnp.sin(ang), hd)

        x_rows = x_own.astype(f32)
        h_attn, x_norm1, inv_std1 = layer_norm(x_rows, ln1_gain, ln1_bias)
        h_attn = h_attn.astype(bf)
        h_mlp, x_norm2, inv_std2 = layer_norm(x_rows, ln2_gain, ln2_bias)
        h_mlp = h_mlp.astype(bf)
        gelu_out, slope = exact_gelu(mm(h_mlp, w_up) + b_up.astype(f32))
        mlp_proj = mm(gelu_out.astype(bf), w_down) + b_down.astype(f32)
        d_up_bf = (mm(dy_bf, w_down, NT) * slope).astype(bf)
        d_h_mlp = mm(d_up_bf, w_up, NT)
        d_ctx = mm(dy_bf, w_out, NT)
        dx_mlp, d_ln2_gain, d_ln2_bias = norm_backward(d_h_mlp, x_norm2, inv_std2, ln2_gain)

        k_all, v_all, attn_norm, lse, qt = fwd_attention(me1, x_all, cos_l, sin_l, row(ln1_gain), row(ln1_bias), w3[0], w3[1], w3[2], b3, T, hd)
        delta = jnp.sum((d_ctx * attn_norm).reshape(T, heads, hd), axis=-1).T
        stats = lax.all_gather(jnp.concatenate([lse, delta], axis=0), 'cp', tiled=True)
        attn_ctx = attn_norm.astype(bf)
        y_rows = (x_rows + (mm(attn_ctx, w_out) + b_out.astype(f32)) + mlp_proj).astype(bf)
        d_w_out = mm(attn_ctx, dy_bf, (((0,), (0,)), ((), ())))

        F = FF // cp_size
        F_pad = -(-F // 128) * 128
        pad = lambda a, ax: jnp.pad(a, [(0, F_pad - F) if d == ax else (0, 0) for d in range(a.ndim)])
        wu_s = pad(lax.dynamic_slice_in_dim(w_up, me * F, F, 1), 1)
        bu_s = pad(lax.dynamic_slice_in_dim(b_up.astype(f32), me * F, F, 0), 0).reshape(1, F_pad)
        wd_s = pad(lax.dynamic_slice_in_dim(w_down, me * F, F, 0).T, 1)
        du_s, dd_s, db_s = mlp_grads(x_all, dy_all, row(ln2_gain), row(ln2_bias), wu_s, bu_s, wd_s, F)
        d_w_up = lax.all_gather(du_s, 'cp', tiled=True).T
        d_w_down = lax.all_gather(dd_s, 'cp', tiled=True)
        d_b_up = lax.dynamic_update_slice(jnp.zeros((FF,), f32), db_s[0, :F], (me * F,))

        d_q, d_k, d_v = bwd_attention(me1, x_all, dy_all, cos_l, sin_l, k_all, v_all, stats, qt, d_ctx.astype(bf), row(ln1_gain), row(ln1_bias), w3[0], w_out.T, b3[0:1], T, hd)
        cos_o = lax.dynamic_slice_in_dim(cos_l, me * T, T, 0)[:, None, :hd]
        sin_o = lax.dynamic_slice_in_dim(sin_l, me * T, T, 0)[:, None, :hd]
        half = hd // 8

        def unrotate(g):
            g = g.reshape(T, heads, hd)
            partner = jnp.concatenate([g[..., half:2 * half], g[..., :half], g[..., 2 * half:]], axis=-1)
            return (g * cos_o - partner * sin_o).reshape(T, W)

        d3 = jnp.concatenate([unrotate(d_q), unrotate(d_k), d_v], axis=1)
        d_b_qkv = jnp.sum(d3, axis=0).reshape(3, heads, hd).transpose(1, 0, 2)
        d3_bf = d3.astype(bf)
        d_w3 = mm(h_attn, d3_bf, (((0,), (0,)), ((), ())))
        d_h_attn = mm(d3_bf, w3.transpose(0, 2, 1).reshape(3 * W, W))
        dx_attn, d_ln1_gain, d_ln1_bias = norm_backward(d_h_attn, x_norm1, inv_std1, ln1_gain)
        dx_rows = dy_own + dx_attn + dx_mlp

        d_w_qkv = d_w3.reshape(W, 3, heads, hd).transpose(0, 2, 1, 3)
        dy_sum = jnp.sum(dy_own, axis=0)
        summed = lax.psum((d_ln1_gain, d_ln1_bias, d_ln2_gain, d_ln2_bias, d_w_qkv, d_b_qkv, d_w_out, dy_sum, d_b_up), 'cp')
        return (y_rows[None], dx_rows[None]) + tuple(summed[:8]) + (d_w_up, summed[8], d_w_down, summed[7])

    return jax.shard_map(local_layer, mesh=mesh, in_specs=in_specs, out_specs=out_specs, check_vma=False)
```

time: 2390 us -> 721 us (0.30)
  waiting for transfers between devices: 1580 us -> 86.6 us
  local copies, waits for them, and re-layouts: 388 us -> 104 us
  Pallas kernels: 0 us -> 234 us
  starting transfers between devices: 195 us -> 0.32 us
  blocking collectives: 104 us -> 209 us
  matrix products: 70.1 us -> 33.6 us
    ppermute x188 -> x0, waiting for transfers between devices: 1440 us -> none  [the longest x124 1070 us: bwd_step(): lax.ppermute((k_cur, v_cur, dk_cur, dv_cur), 'cp', shift_perm)]
    while x186 -> x0, local copies, waits for them, and re-layouts: 349 us -> none
    pallas_call x0 -> x3, Pallas kernels: none -> 234 us  [the longest x1 197 us: bwd_attention(): pl.pallas_call(functools.partial(bwd_kernel, hd, S // T), out_shape=[jax....]
    ppermute x188 -> x0, starting transfers between devices: 195 us -> none  [the longest x62 135 us: fwd_step(): k_cur, v_cur = lax.ppermute((k_cur, v_cur), 'cp', shift_perm)]
    all_gather x0 -> x1, blocking collectives: none -> 158 us  [local_layer(): lax.all_gather(jnp.concatenate([lse, delta], axis=0), 'cp', tiled=True)]
    psum x1, waiting for transfers between devices: 139 us -> 0.01 us  [local_layer(): lax.psum((d_ln1_gain, d_ln1_bias, d_ln2_gain, d_ln2_bias, d_w_qkv, d_b_qk...]
    all_gather x0 -> x4, waiting for transfers between devices: none -> 85.2 us  [the longest x1 43.6 us: local_layer(): d_w_up = lax.all_gather(du_s, 'cp', tiled=True).T]
    psum x1, blocking collectives: 104 us -> 50.9 us  [local_layer(): lax.psum((d_ln1_gain, d_ln1_bias, d_ln2_gain, d_ln2_bias, d_w_qkv, d_b_qk...]
  transfers between devices with their start and end apart: 189 -> 5, of which waited for: 97 -> 2; matrix products, arithmetic and copies ran while one was open for 7% -> 20% of each run, Pallas kernels for 0% -> 5%
where the time goes in v1:
time: 721 us; the launch traced here: 712 us
  Pallas kernels  234 us (32%)
  blocking collectives  209 us (29%)
  local copies, waits for them, and re-layouts  104 us (14%)
  waiting for transfers between devices  86.6 us (12%)
  matrix products  33.6 us (5%)
  other arithmetic  29.5 us (4%)
  between operations  14.8 us (2%)
    pallas_call x1, Pallas kernels, bwd_attention(): pl.pallas_call(functools.partial(bwd_kernel, hd, S // T), out_shape=[jax....  197 us
    all_gather x1, blocking collectives, local_layer(): lax.all_gather(jnp.concatenate([lse, delta], axis=0), 'cp', tiled=True)  158 us
    psum x1, blocking collectives, local_layer(): lax.psum((d_ln1_gain, d_ln1_bias, d_ln2_gain, d_ln2_bias, d_w_qkv, d_b_qk...  50.9 us
    all_gather x1, waiting for transfers between devices, local_layer(): d_w_up = lax.all_gather(du_s, 'cp', tiled=True).T  43.6 us
    all_gather x1, waiting for transfers between devices, local_layer(): d_w_down = lax.all_gather(dd_s, 'cp', tiled=True)  41.6 us
    unnamed x79, local copies, waits for them, and re-layouts  34.4 us
    dot_general x8, matrix products, mm(): return lax.dot_general(a, b, dims, preferred_element_type=jnp.float32)  33.6 us
    pallas_call x1, Pallas kernels, mlp_grads(): pl.pallas_call(mlp_kernel, grid=(S // R,), out_shape=[jax.ShapeDtypeStruc...  23.5 us
  transfers between devices with their start and end apart: 5, of which 2 were waited for; matrix products, arithmetic and copies ran while one was open for 20% of the time, Pallas kernels for 5%

profile of v1, /device:TPU:97, one launch (start us, length us, event | category | flops | bytes accessed | tf_op | source)
XLA Modules:
  0.0 712.3 jit_solution(14082057147811022234)
XLA Ops:
  8.1 2.5 fusion.64
  10.7 2.2 copy.84
  13.0 1.9 fusion.63
  15.4 2.5 copy.61.wq_ref
  17.9 2.4 copy.62.wk_ref
  25.8 18.2 %multiply_sine_fusion = (f32[8192,8]{1,0:T(8,128)}, f32[8192,8]{1,0:T(8,128)}, f32[8192,8]{1,0:T(8,128)}) fusion(f32[8192]{0:T(1024)S(1)} %iota_convert_fusion, f32[8]{0:T(128)S(1)} %multiply_power_fusion), kind=kLoop, calls=%fused_computation | loop fusion | flops 131072 | bytes 819232 | tf_op jit(solution)/shard_map/sin | solution.py:416
  44.0 2.2 broadcast_in_dim.14
  46.2 20.4 %concatenate.22.cos_hbm = f32[8192,128]{1,0:T(8,128)} concatenate(f32[8192,8]{1,0:T(8,128)} %get-tuple-element.118, f32[8192,8]{1,0:T(8,128)} %get-tuple-element.118, f32[8192,48]{1,0:T(8,128)} %broadcast_in_dim.14, f32[8192,8]{1,0:T(8,128)} %get-tuple-element.118, f32[8192,8]{1,0:T(8,128)} %get-tuple-element.118, f32[8192,48]{1,0:T(8,128)} %broadcast_in_dim.14), dimensions={1} | concatenate | bytes 8388608 | tf_op jit(solution)/shard_map/concatenate | solution.py:47
  66.6 2.3 broadcast_in_dim.15
  68.9 19.0 %concatenate.23.sin_hbm = f32[8192,128]{1,0:T(8,128)} concatenate(f32[8192,8]{1,0:T(8,128)} %get-tuple-element.117, f32[8192,8]{1,0:T(8,128)} %get-tuple-element.116, f32[8192,48]{1,0:T(8,128)} %broadcast_in_dim.15, f32[8192,8]{1,0:T(8,128)} %get-tuple-element.117, f32[8192,8]{1,0:T(8,128)} %get-tuple-element.116, f32[8192,48]{1,0:T(8,128)} %broadcast_in_dim.15), dimensions={1} | concatenate | bytes 8388608 | tf_op jit(solution)/shard_map/concatenate | solution.py:47
  91.4 13.7 %attn_fwd.1 = (bf16[8192,768]{1,0:T(8,128)(2,1)}, bf16[8192,768]{1,0:T(8,128)(2,1)}, f32[256,768]{1,0:T(8,128)}, f32[12,256]{1,0:T(8,128)}, bf16[768,256]{1,0:T(8,128)(2,1)}) custom-call(s32[1]{0:T(128)} %bitcast.1.me_ref, bf16[8192,768]{1,0:T(8,128)(2,1)} %bitcast.134, f32[8192,128]{1,0:T(8,128)} %concatenate.22.cos_hbm, f32[8192,128]{1,0:T(8,128)} %concatenate.23.sin_hbm, ...), custom_call_target="tpu_custom_call" | custom-call | flops 40000000000 | bytes 40000000 | tf_op jit(solution)/shard_map/attn_fwd/pallas_call | solution.py:199
  105.1 2.4 fusion.67
  107.9 157.9 %all_gather.17.stats_ref = f32[768,256]{1,0:T(8,128)} all-gather(f32[24,256]{1,0:T(8,128)S(1)} %pad_maximum_fusion.1), channel_id=1, replica_groups=mesh['dp'=1,'cp'=32] {'cp'}, dimensions={0}, use_global_device_ids=true | all-gather | bytes 811008 | tf_op jit(solution)/shard_map/all_gather | solution.py:432
  265.9 197.1 %attn_bwd.1 = (f32[256,768]{1,0:T(8,128)}, f32[256,768]{1,0:T(8,128)}, f32[256,768]{1,0:T(8,128)}) custom-call(s32[1]{0:T(128)} %bitcast.1.me_ref, bf16[8192,768]{1,0:T(8,128)(2,1)} %bitcast.135, bf16[8192,768]{1,0:T(8,128)(2,1)} %all-gather.6.cloned.1.call-done.dy_hbm.dy_ref, f32[8192,128]{1,0:T(8,128)} %concatenate.22.cos_hbm, ...), custom_call_target="tpu_custom_call" | custom-call | flops 80000000000 | bytes 40000000 | tf_op jit(solution)/shard_map/attn_bwd/pallas_call | solution.py:342
  463.0 1.5 copy.69
  466.0 1.9 fusion.54
  469.6 1.7 multiply_subtract_fusion.1
  473.2 4.2 convolution_bitcast_fusion
  483.0 23.5 %mlp_grads.1 = (f32[96,768]{1,0:T(8,128)}, f32[96,768]{1,0:T(8,128)}, f32[1,128]{1,0:T(1,128)}) custom-call(bf16[8192,768]{1,0:T(8,128)(2,1)} %bitcast.136, bf16[8192,768]{1,0:T(8,128)(2,1)} %all-gather.6.cloned.1.call-done.dy_hbm.dy_ref, f32[1,768]{1,0:T(1,128)} %broadcast_in_dim.18.g_ref, f32[1,768]{1,0:T(1,128)} %broadcast_in_dim.19.s_ref, ...), custom_call_target="tpu_custom_call" | custom-call | flops 20000000000 | bytes 26000000 | tf_op jit(solution)/shard_map/mlp_grads/pallas_call | solution.py:378
  507.8 3.8 convolution_add_fusion
  511.7 1.7 copy-done.34
  513.3 4.8 fusion.11
  518.2 8.8 %fusion.24 = f32[256,768]{1,0:T(8,128)} fusion(bf16[768,3072]{1,0:T(8,128)(2,1)} %param.24, bf16[256,768]{1,0:T(8,128)(2,1)} %get-tuple-element.105, bf16[3072,768]{1,0:T(8,128)(2,1)} %param.26, f32[256,3072]{1,0:T(8,128)} %copy-done.34), kind=kOutput, calls=%fused_computation.37 | convolution fusion | flops 2423783424 | bytes 13762560 | tf_op jit(solution)/shard_map/dot_general | solution.py:19
  526.9 1.7 fusion.5
  530.3 4.6 fusion.36
  535.0 50.9 %all-reduce.3 = (f32[768]{0:T(1024)}, f32[768]{0:T(1024)}, f32[768]{0:T(1024)}, f32[768]{0:T(1024)}, f32[12,3,64]{2,0,1:T(8,128)S(1)}, /*index=5*/f32[768]{0:T(1024)S(1)}, f32[3072]{0:T(1024)}) all-reduce(f32[768]{0:T(1024)} %get-tuple-element.80, f32[768]{0:T(1024)} %get-tuple-element.85, ...), channel_id=1, replica_groups=mesh['dp'=1,'cp'=32] {'cp'}, use_global_device_ids=true, to_apply=%region_8.0 | all-reduce | flops 9216 | bytes 73728 | tf_op jit(solution)/shard_map/psum | solution.py:468
  589.2 3.1 fusion.13
  593.7 6.7 copy.77
  600.4 43.6 %all-gather.8.cloned.1.call-done = f32[3072,768]{1,0:T(8,128)} async-done(((f32[96,768]{1,0:T(8,128)}), f32[3072,768]{1,0:T(8,128)}) %all-gather.8.cloned.1.call-update) | async-done | bytes 9437200 | tf_op jit(solution)/shard_map/all_gather | solution.py:444
  644.0 9.7 %copy.79 = f32[768,3072]{1,0:T(8,128)} copy(f32[768,3072]{0,1:T(8,128)} %bitcast.117) | data formatting | bytes 18874368
  653.7 41.6 %all-gather.10.cloned.1.call-done = f32[3072,768]{1,0:T(8,128)} async-done(((f32[96,768]{1,0:T(8,128)}), f32[3072,768]{1,0:T(8,128)}) %all-gather.10.cloned.1.call-update) | async-done | bytes 9437200 | tf_op jit(solution)/shard_map/all_gather | solution.py:445
  697.3 8.0 %copy.92 = f32[3072,768]{1,0:T(8,128)} copy(f32[3072,768]{1,0:T(8,128)} %all-gather.10.cloned.1.call-done) | data formatting | bytes 18874368
  (137 shorter events, 31.0 us)
Async XLA Ops:
  7.2 84.2 %all-gather.12.cloned.1.call-start = ((), (), s32[]{:S(2)}) async-start(), calls=%async_computation.3 | async-start | bytes 12976128 | tf_op jit(solution)/shard_map/all_gather | solution.py:410
  8.0 257.9 %all-gather.6.cloned.1.call-start = ((), (), s32[]{:S(2)}) async-start(), calls=%async_computation | async-start | bytes 12976128 | tf_op jit(solution)/shard_map/all_gather | solution.py:411
  10.6 583.1 %all-reduce.7.cloned.1.call-start = ((), (), s32[]{:S(2)}) async-start(), calls=%async_computation.4 | async-start | bytes 18874368 | tf_op jit(solution)/shard_map/psum | solution.py:468
  13.0 2.4 copy-start
  15.4 6.3 copy-start.26
  15.4 7.0 copy-start.17
  15.4 7.6 %copy-start.19 = (f32[768]{0:T(1024)S(1)}, f32[768]{0:T(1024)}, u32[]{:S(2)}) copy-start(f32[768]{0:T(1024)} %param.17) | copy-start | bytes 9220
  15.4 8.9 %copy-start.4 = (bf16[768,768]{1,0:T(8,128)(2,1)S(1)}, bf16[768,768]{1,0:T(8,128)(2,1)}, u32[]{:S(2)}) copy-start(bf16[768,768]{1,0:T(8,128)(2,1)} %param.22) | copy-start | bytes 3538948
  87.8 3.1 copy-start.2
  91.1 416.8 %copy-start.24 = (f32[256]{0:T(256)}, f32[256]{0:T(256)S(1)}, u32[]{:S(2)}) copy-start(f32[256]{0:T(256)S(1)} %broadcast_multiply_fusion.4) | copy-start | bytes 3076
  91.3 416.5 %copy-start.27 = (f32[256]{0:T(256)}, f32[256]{0:T(256)S(1)}, u32[]{:S(2)}) copy-start(f32[256]{0:T(256)S(1)} %add_rsqrt_fusion) | copy-start | bytes 3076
  91.4 13.7 %copy-start.8 = (bf16[256,768]{1,0:T(8,128)(2,1)S(1)}, bf16[256,768]{1,0:T(8,128)(2,1)}, u32[]{:S(2)}) copy-start(bf16[256,768]{1,0:T(8,128)(2,1)} %get-tuple-element.105) | copy-start | bytes 1179652
  105.1 2.8 copy-start.21
  463.0 3.0 copy-start.5
  469.6 2.9 copy-start.9
  477.4 3.8 copy-start.29
  477.4 3.9 copy-start.22
  477.4 4.5 copy-start.30
  477.5 166.5 %all-gather.8.cloned.1.call-start = ((), (), s32[]{:S(2)}) async-start(), calls=%async_computation.1 | async-start | bytes 9732096 | tf_op jit(solution)/shard_map/all_gather | solution.py:444
  483.0 24.2 %copy-start.32 = (bf16[768]{0:T(1024)(128)(2,1)S(1)}, bf16[768]{0:T(1024)(128)(2,1)}, u32[]{:S(2)}) copy-start(bf16[768]{0:T(1024)(128)(2,1)} %param.27) | copy-start | bytes 4612
  483.0 24.3 %copy-start.33 = (bf16[768]{0:T(1024)(128)(2,1)S(1)}, bf16[768]{0:T(1024)(128)(2,1)}, u32[]{:S(2)}) copy-start(bf16[768]{0:T(1024)(128)(2,1)} %param.23) | copy-start | bytes 4612
  506.5 188.8 %all-gather.10.cloned.1.call-start = ((), (), s32[]{:S(2)}) async-start(), calls=%async_computation.2 | async-start | bytes 9732096 | tf_op jit(solution)/shard_map/all_gather | solution.py:445
  518.2 12.2 %copy-start.1 = (bf16[768,12,3,64]{0,3,1,2:T(8,128)(2,1)S(1)}, bf16[768,12,3,64]{0,3,1,2:T(8,128)(2,1)}, u32[]{:S(2)}) copy-start(bf16[768,12,3,64]{0,3,1,2:T(8,128)(2,1)} %copy-done) | copy-start | bytes 10616836
  535.0 57.3 %copy-start.3 = (bf16[1,256,768]{2,1,0:T(8,128)(2,1)S(1)}, bf16[1,256,768]{2,1,0:T(8,128)(2,1)}, u32[]{:S(2)}) copy-start(bf16[1,256,768]{2,1,0:T(8,128)(2,1)} %param.14) | copy-start | bytes 1179652
  535.0 57.3 %copy-start.10 = (f32[1,256,768]{2,1,0:T(8,128)S(1)}, f32[1,256,768]{2,1,0:T(8,128)}, u32[]{:S(2)}) copy-start(f32[1,256,768]{2,1,0:T(8,128)} %param.15) | copy-start | bytes 2359300
  535.0 57.3 %copy-start.14 = (f32[256,768]{1,0:T(8,128)S(1)}, f32[256,768]{1,0:T(8,128)}, u32[]{:S(2)}) copy-start(f32[256,768]{1,0:T(8,128)} %fusion.24) | copy-start | bytes 2359300
  535.0 57.3 %copy-start.15 = (f32[256,768]{1,0:T(8,128)S(1)}, f32[256,768]{1,0:T(8,128)}, u32[]{:S(2)}) copy-start(f32[256,768]{1,0:T(8,128)} %get-tuple-element.120) | copy-start | bytes 2359300
  535.0 57.3 %copy-start.23 = (f32[768]{0:T(1024)S(1)}, f32[768]{0:T(1024)}, u32[]{:S(2)}) copy-start(f32[768]{0:T(1024)} %param.18) | copy-start | bytes 9220
  535.0 57.3 %copy-start.25 = (f32[256]{0:T(256)S(1)}, f32[256]{0:T(256)}, u32[]{:S(2)}) copy-start(f32[256]{0:T(256)} %copy-done.24) | copy-start | bytes 3076
  535.0 57.3 %copy-start.28 = (f32[256]{0:T(256)S(1)}, f32[256]{0:T(256)}, u32[]{:S(2)}) copy-start(f32[256]{0:T(256)} %copy-done.27) | copy-start | bytes 3076
  585.9 109.4 %copy-start.31 = (f32[768]{0:T(1024)}, f32[768]{0:T(1024)S(1)}, u32[]{:S(2)}) copy-start(f32[768]{0:T(1024)S(1)} %get-tuple-element.176) | copy-start | bytes 9220
  644.0 51.9 %copy-start.13 = (f32[768,768]{1,0:T(8,128)S(1)}, f32[768,768]{1,0:T(8,128)}, u32[]{:S(2)}) copy-start(f32[768,768]{1,0:T(8,128)} %get-tuple-element.175) | copy-start | bytes 7077892
  (8 other events, 12.8 us)
Sparse Core Ops, SparseCore 0:
  10.1 61.6 all-gather.11
  73.8 56.8 all-gather.5
  477.6 114.4 all-reduce.6
  594.1 49.8 all-gather.7
  645.9 49.3 all-gather.9

commit v2 on v1

v2 whole, which is shorter than its diff:
```python
import functools

import jax
import jax.numpy as jnp
from jax import lax
from jax.experimental import pallas as pl
from jax.experimental.pallas import tpu as pltpu
from jax.sharding import PartitionSpec as P

EPS = 1e-5
ROPE_BASE = 10000.0
NEG_BIG = -1e30
VMEM_LIMIT = 60 * 1024 * 1024
NN = (((1,), (0,)), ((), ()))
NT = (((1,), (1,)), ((), ()))


def mm(a, b, dims=NN):
    return lax.dot_general(a, b, dims, preferred_element_type=jnp.float32)


def layer_norm(row_vals, norm_gain, norm_shift):
    row_mean = jnp.mean(row_vals, axis=-1, keepdims=True)
    centered = row_vals - row_mean
    inv_std = lax.rsqrt(jnp.mean(centered * centered, axis=-1, keepdims=True) + EPS)
    x_norm = centered * inv_std
    return x_norm * norm_gain + norm_shift, x_norm, inv_std


def norm_backward(d_out, x_norm, inv_std, norm_gain):
    d_norm = d_out * norm_gain
    d_rows = inv_std * (d_norm - jnp.mean(d_norm, axis=-1, keepdims=True) - x_norm * jnp.mean(d_norm * x_norm, axis=-1, keepdims=True))
    return d_rows, jnp.sum(d_out * x_norm, axis=0), jnp.sum(d_out, axis=0)


def rope_angles(positions, head_dim):
    rot_dim = head_dim // 4
    inv_freq = ROPE_BASE ** (-2.0 * jnp.arange(rot_dim // 2, dtype=jnp.float32) / rot_dim)
    return positions.astype(jnp.float32)[:, None] * inv_freq[None, :]


def lane_tables(positions, head_dim):
    rot_dim = head_dim // 4
    freq = ROPE_BASE ** (-2.0 * jnp.arange(rot_dim // 2, dtype=jnp.float32) / rot_dim)
    rest = jnp.zeros((head_dim // 2 - rot_dim // 2,), jnp.float32)
    lanes = jnp.concatenate([-freq, rest, -freq, rest, freq, rest, freq, rest])
    angles = positions.astype(jnp.float32)[:, None] * lanes[None, :]
    return jnp.cos(angles), jnp.sin(angles)


def turn(tab, j, cs, ss):
    cl, sl, cb, sb = tab
    ca, sa = cb[pl.ds(j, 1), :], sb[pl.ds(j, 1), :]
    cs[...] = ca * cl[...] - sa * sl[...]
    ss[...] = sa * cl[...] + ca * sl[...]


def pair_rows(w_t):
    heads, hd = w_t.shape[:2]
    half = hd // 8
    mid = (hd - 2 * half) // 2 + 2 * half
    low = jnp.concatenate([w_t[:, :half], w_t[:, 2 * half:mid]], axis=1)
    high = jnp.concatenate([w_t[:, half:2 * half], w_t[:, mid:]], axis=1)
    both = jnp.stack([low, high], axis=1).reshape(heads // 2, 2, 2, hd // 2, -1)
    return both.transpose(0, 2, 1, 3, 4).reshape(heads * hd, -1)


def rotate(z, cos_l, sin_l):
    parts = []
    for t in range(z.shape[1] // 128):
        zt = z[:, t * 128:(t + 1) * 128]
        parts.append(zt * cos_l + pltpu.roll(zt, 64, 1) * sin_l)
    return jnp.concatenate(parts, axis=1)


def exact_gelu(pre):
    cdf = 0.5 * (1.0 + lax.erf(pre * (0.5 ** 0.5)))
    pdf = jnp.exp(-0.5 * pre * pre) * 0.3989422804014327
    return pre * cdf, cdf + pre * pdf


def put_masked(dst, mat_t, hd, paired):
    rows = lax.broadcasted_iota(jnp.int32, (2 * hd, mat_t.shape[1]), 0)
    first = (rows % hd < hd // 2) if paired else (rows < hd)
    for p in range(mat_t.shape[0] // (2 * hd)):
        blk = mat_t[p * 2 * hd:(p + 1) * 2 * hd]
        zero = jnp.zeros_like(blk)
        dst[2 * p] = jnp.where(first, blk, zero)
        dst[2 * p + 1] = jnp.where(first, zero, blk)


def head_rows(mat_t, i, hd, paired):
    if not paired:
        return mat_t[i * hd:(i + 1) * hd]
    q = hd // 2
    return jnp.concatenate([mat_t[i * q:(i + 1) * q], mat_t[hd + i * q:hd + (i + 1) * q]], axis=0)


def causal(T, keys_first):
    r = lax.broadcasted_iota(jnp.int32, (T, T), 0)
    c = lax.broadcasted_iota(jnp.int32, (T, T), 1)
    return (r <= c) if keys_first else (c <= r)


def fwd_kernel(hd, me_ref, x_hbm, cl_ref, sl_ref, cb_ref, sb_ref, g_ref, s_ref, wq_ref, wk_ref, wv_ref, b_ref,
               k_hbm, v_hbm, ctx_ref, lse_ref, qt_ref,
               xb, cs, ss, hsc, kst, vst, qtm, sbuf, acc, mrow, lrow, in_sem, out_sem):
    me = me_ref[0]
    T = xb.shape[1]
    W = xb.shape[2]
    pairs = W // (2 * hd)
    scale = hd ** -0.5
    tiles = W // 256

    tab = (cl_ref, sl_ref, cb_ref, sb_ref)
    DEEP = xb.shape[0]

    def fetch(j):
        blk = jnp.where(j < 0, me, jnp.minimum(j, me))
        slot = (j + 1) % DEEP
        return (pltpu.make_async_copy(x_hbm.at[pl.ds(blk * T, T)], xb.at[slot], in_sem.at[slot]),)

    def flush(j, slot):
        return (pltpu.make_async_copy(kst.at[slot], k_hbm.at[pl.ds(j * T, T)], out_sem.at[slot, 0]),
                pltpu.make_async_copy(vst.at[slot], v_hbm.at[pl.ds(j * T, T)], out_sem.at[slot, 1]))

    def start(copies):
        for c in copies:
            c.start()

    def wait(copies):
        for c in copies:
            c.wait()

    def norm(j):
        hsc[...] = layer_norm(xb[(j + 1) % DEEP].astype(jnp.float32), g_ref[...], s_ref[...])[0].astype(jnp.bfloat16)
        turn(tab, jnp.where(j < 0, me, j), cs, ss)

    def piece(i, slot):
        cols = slice((i % tiles) * 256, (i % tiles + 1) * 256)
        if i < tiles:
            kst[slot, :, cols] = rotate(mm(hsc[...], wk_ref[:, cols]) + b_ref[1:2, cols], cs[...], ss[...]).astype(jnp.bfloat16)
        else:
            vst[slot, :, cols] = (mm(hsc[...], wv_ref[:, cols]) + b_ref[2:3, cols]).astype(jnp.bfloat16)

    def scores(slot, p):
        kp = kst[slot, :, p * 2 * hd:(p + 1) * 2 * hd]
        return [mm(kp, qtm[h]) for h in (2 * p, 2 * p + 1)]

    def attend(j, slot, diag):
        ahead = scores(slot, 0) if diag else [sbuf[0], sbuf[1]]
        norm(j + 1)
        per = -(-2 * tiles // pairs)
        for p in range(pairs):
            now = ahead
            for i in range(p * per, min((p + 1) * per, 2 * tiles)):
                piece(i, 1 - slot)
            if p + 1 < pairs:
                ahead = scores(slot, p + 1)
            else:
                ahead = scores(1 - slot, 0)
            vt = vst[slot, :, p * 2 * hd:(p + 1) * 2 * hd].T
            for i in range(2):
                h = 2 * p + i
                s = now[i]
                rows = slice(h * hd, (h + 1) * hd)
                vh = head_rows(vt, i, hd, False)
                if diag:
                    s = jnp.where(causal(T, True), s, NEG_BIG)
                    m = jnp.max(s, axis=0, keepdims=True)
                    e = jnp.exp(s - m)
                    lrow[h:h + 1] = jnp.sum(e, axis=0, keepdims=True)
                    acc[rows] = mm(vh, e.astype(jnp.bfloat16))
                else:
                    m_old = mrow[h:h + 1]
                    m = jnp.maximum(m_old, jnp.max(s, axis=0, keepdims=True))
                    e = jnp.exp(s - m)
                    alpha = jnp.exp(m_old - m)
                    lrow[h:h + 1] = lrow[h:h + 1] * alpha + jnp.sum(e, axis=0, keepdims=True)
                    acc[rows] = acc[rows] * alpha + mm(vh, e.astype(jnp.bfloat16))
                mrow[h:h + 1] = m
        sbuf[0] = ahead[0]
        sbuf[1] = ahead[1]

    for j in range(-1, DEEP - 1):
        start(fetch(jnp.int32(j)))
    own = jnp.int32(-1)
    wait(fetch(own))
    norm(own)
    for i in range(2 * tiles):
        piece(i, 0)
    for t in range(tiles):
        cols = slice(t * 256, (t + 1) * 256)
        q = rotate(mm(hsc[...], wq_ref[:, cols]) + b_ref[0:1, cols], cs[...], ss[...])
        qt_ref[cols] = (q.astype(jnp.bfloat16) * jnp.bfloat16(scale)).T
    put_masked(qtm, qt_ref[...], hd, True)
    start(flush(me, 0))
    start(fetch(own + DEEP))
    wait(fetch(own + 1))
    attend(own, 0, True)

    @pl.when(me >= 1)
    def _():
        start(flush(0, 1))

    wait(flush(me, 0))

    def step(j, slot):
        wait(fetch(j + 1))
        start(fetch(j + DEEP))

        @pl.when(j >= 1)
        def _():
            wait(flush(j - 1, 1 - slot))

        attend(j, slot, False)

        @pl.when(j + 1 < me)
        def _():
            start(flush(j + 1, 1 - slot))

        return 1 - slot

    last = lax.fori_loop(0, me, step, jnp.int32(1))

    for k in range(1, DEEP):
        wait(fetch(me + k))

    @pl.when(me >= 1)
    def _():
        wait(flush(me - 1, 1 - last))

    lse_ref[...] = mrow[...] + jnp.log(lrow[...])
    inv = 1.0 / lrow[...]
    for p in range(pairs):
        a = acc[2 * p * hd:(2 * p + 1) * hd] * inv[2 * p:2 * p + 1]
        b = acc[(2 * p + 1) * hd:(2 * p + 2) * hd] * inv[2 * p + 1:2 * p + 2]
        ctx_ref[:, 2 * p * hd:(2 * p + 2) * hd] = jnp.concatenate([a, b], axis=0).T


def fwd_attention(me, x_all, tab, gain, shift, wq, wk, wv, b3, T, hd):
    S, W = x_all.shape
    heads = W // hd
    vm = pl.BlockSpec(memory_space=pltpu.VMEM)
    anym = pl.BlockSpec(memory_space=pl.ANY)
    f32, bf = jnp.float32, jnp.bfloat16
    return pl.pallas_call(
        functools.partial(fwd_kernel, hd),
        out_shape=[jax.ShapeDtypeStruct((S, W), bf), jax.ShapeDtypeStruct((S, W), bf), jax.ShapeDtypeStruct((T, W), f32),
                   jax.ShapeDtypeStruct((heads, T), f32), jax.ShapeDtypeStruct((W, T), bf)],
        in_specs=[pl.BlockSpec(memory_space=pltpu.SMEM), anym] + [vm] * 10,
        out_specs=[anym, anym, vm, vm, vm],
        scratch_shapes=[pltpu.VMEM((4, T, W), bf), pltpu.VMEM((T, 128), f32), pltpu.VMEM((T, 128), f32), pltpu.VMEM((T, W), bf),
                        pltpu.VMEM((2, T, W), bf), pltpu.VMEM((2, T, W), bf), pltpu.VMEM((heads, 2 * hd, T), bf), pltpu.VMEM((2, T, T), f32),
                        pltpu.VMEM((W, T), f32), pltpu.VMEM((heads, T), f32), pltpu.VMEM((heads, T), f32),
                        pltpu.SemaphoreType.DMA((4,)), pltpu.SemaphoreType.DMA((2, 2))],
        compiler_params=pltpu.CompilerParams(vmem_limit_bytes=VMEM_LIMIT),
        cost_estimate=pl.CostEstimate(flops=40_000_000_000, bytes_accessed=40_000_000, transcendentals=0),
        name="attn_fwd",
    )(me, x_all, *tab, gain, shift, wq, wk, wv, b3)


def bwd_kernel(hd, n, heads, h0, width, srows, me_ref, x_hbm, dy_hbm, k_hbm, v_hbm, cl_ref, sl_ref, cb_ref, sb_ref, stats_ref, qt_ref, own_ref, g_ref, s_ref,
               wq_ref, wot_ref, bq_ref, ct_ref, st_ref, d3_ref,
               xb, yb, cs, ss, kb, vb, hsc, qsc, osc, am, bm, sbuf, acc1, acc2, kv_sem, xy_sem):
    me = me_ref[0]
    T = xb.shape[1]
    pairs = width // (2 * hd)
    half = hd // 8
    scale = hd ** -0.5
    c0 = h0 * hd

    tab = (cl_ref, sl_ref, cb_ref, sb_ref)
    DEEP = xb.shape[0]

    def fetch_kv(j):
        slot, blk = j % DEEP, jnp.minimum(j, me)
        return (pltpu.make_async_copy(k_hbm.at[pl.ds(blk * T, T), c0:c0 + width], kb.at[slot], kv_sem.at[slot, 0]),
                pltpu.make_async_copy(v_hbm.at[pl.ds(blk * T, T), c0:c0 + width], vb.at[slot], kv_sem.at[slot, 1]))

    def fetch_xy(r):
        slot, blk = r % DEEP, jnp.minimum(me + r, n - 1)
        return (pltpu.make_async_copy(x_hbm.at[pl.ds(blk * T, T)], xb.at[slot], xy_sem.at[slot, 0]),
                pltpu.make_async_copy(dy_hbm.at[pl.ds(blk * T, T)], yb.at[slot], xy_sem.at[slot, 1]))

    def start(copies):
        for c in copies:
            c.start()

    def wait(copies):
        for c in copies:
            c.wait()

    def pair_cols(p):
        return slice(p * 2 * hd, (p + 1) * 2 * hd)

    def unrotated(z):
        mid = hd // 2
        a, b = z[:half], z[mid:mid + half]
        ct, st = ct_ref[...], st_ref[...]
        return jnp.concatenate([a * ct + b * st, b * ct - a * st, z[half:mid], z[mid + half:]], axis=0)

    for r in range(DEEP - 1):
        start(fetch_kv(jnp.int32(r)))
    for r in range(DEEP):
        start(fetch_xy(jnp.int32(r)))
    put_masked(am, qt_ref[c0:c0 + width], hd, True)
    put_masked(bm, own_ref[:, c0:c0 + width].T, hd, False)
    acc1[...] = jnp.zeros_like(acc1)

    def dq_scores(slot, p):
        kp, vp = kb[slot, :, pair_cols(p)], vb[slot, :, pair_cols(p)]
        return [(mm(kp, am[h]), mm(vp, bm[h])) for h in (2 * p, 2 * p + 1)]

    def dq_block(slot, diag):
        ahead = dq_scores(slot, 0)
        for p in range(pairs):
            now = ahead
            if p + 1 < pairs:
                ahead = dq_scores(slot, p + 1)
            kt = kb[slot, :, pair_cols(p)].T
            for i in range(2):
                h = 2 * p + i
                s, dp = now[i]
                if diag:
                    s = jnp.where(causal(T, True), s, NEG_BIG)
                pr = jnp.exp(s - stats_ref[pl.ds(me * srows + h0 + h, 1), :])
                ds = (pr * (dp - stats_ref[pl.ds(me * srows + heads + h0 + h, 1), :])).astype(jnp.bfloat16)
                acc1[h * hd:(h + 1) * hd] += mm(head_rows(kt, i, hd, True), ds)

    def dq_step(j, _):
        start(fetch_kv(j + DEEP - 1))
        wait(fetch_kv(j))
        dq_block(j % DEEP, False)
        return 0

    lax.fori_loop(0, me, dq_step, 0)
    last = me % DEEP
    wait(fetch_kv(me))
    dq_block(last, True)
    for k in range(1, DEEP - 1):
        wait(fetch_kv(me + k))
    for h in range(2 * pairs):
        d3_ref[3 * h * hd:(3 * h + 1) * hd] = unrotated(acc1[h * hd:(h + 1) * hd] * scale)

    put_masked(am, kb[last].T, hd, True)
    put_masked(bm, vb[last].T, hd, False)
    acc1[...] = jnp.zeros_like(acc1)
    acc2[...] = jnp.zeros_like(acc2)

    tiles = width // 256

    def norm(r):
        hsc[...] = layer_norm(xb[r % DEEP].astype(jnp.float32), g_ref[...], s_ref[...])[0].astype(jnp.bfloat16)
        turn(tab, jnp.minimum(me + r, n - 1), cs, ss)

    def piece(i, r, slot):
        cols = slice(i // 2 * 256, (i // 2 + 1) * 256)
        if i % 2 == 0:
            q = rotate(mm(hsc[...], wq_ref[:, cols]) + bq_ref[:, cols], cs[...], ss[...])
            qsc[slot, :, cols] = q.astype(jnp.bfloat16) * jnp.bfloat16(scale)
        else:
            osc[slot, :, cols] = mm(yb[r % DEEP], wot_ref[:, cols]).astype(jnp.bfloat16)

    def dkv_scores(slot, p):
        qp, op = qsc[slot, :, pair_cols(p)], osc[slot, :, pair_cols(p)]
        return [(mm(qp, am[h]), mm(op, bm[h])) for h in (2 * p, 2 * p + 1)]

    def dkv_block(r, diag):
        j, slot = me + r, r % 2
        ahead = dkv_scores(slot, 0) if diag else [(sbuf[0], sbuf[1]), (sbuf[2], sbuf[3])]
        st = stats_ref[pl.ds(j * srows, srows), :].T
        norm(r + 1)
        per = -(-2 * tiles // pairs)
        for p in range(pairs):
            now = ahead
            for i in range(p * per, min((p + 1) * per, 2 * tiles)):
                piece(i, r + 1, 1 - slot)
            ahead = dkv_scores(slot, p + 1) if p + 1 < pairs else dkv_scores(1 - slot, 0)
            qt = qsc[slot, :, pair_cols(p)].T
            ot = osc[slot, :, pair_cols(p)].T
            for i in range(2):
                h = 2 * p + i
                s, dp = now[i]
                if diag:
                    s = jnp.where(causal(T, False), s, NEG_BIG)
                rows = slice(h * hd, (h + 1) * hd)
                pr = jnp.exp(s - st[:, h0 + h:h0 + h + 1])
                acc2[rows] += mm(head_rows(ot, i, hd, False), pr.astype(jnp.bfloat16))
                ds = (pr * (dp - st[:, heads + h0 + h:heads + h0 + h + 1])).astype(jnp.bfloat16)
                acc1[rows] += mm(head_rows(qt, i, hd, True), ds)
        for i in range(2):
            sbuf[2 * i] = ahead[i][0]
            sbuf[2 * i + 1] = ahead[i][1]

    zero = jnp.int32(0)
    wait(fetch_xy(zero))
    norm(zero)
    for i in range(2 * tiles):
        piece(i, zero, 0)

    def dkv_step(r, diag):
        wait(fetch_xy(r + 1))
        start(fetch_xy(r + DEEP))
        dkv_block(r, diag)
        return 0

    dkv_step(zero, True)
    lax.fori_loop(1, n - me, lambda r, _: dkv_step(r, False), 0)
    for k in range(1, DEEP):
        wait(fetch_xy(n - me + k))
    for h in range(2 * pairs):
        d3_ref[(3 * h + 1) * hd:(3 * h + 2) * hd] = unrotated(acc1[h * hd:(h + 1) * hd])
        d3_ref[(3 * h + 2) * hd:(3 * h + 3) * hd] = acc2[h * hd:(h + 1) * hd]


def bwd_attention(me, x_all, dy_all, tab, k_all, v_all, stats, qt, d_ctx_bf, gain, shift, wq, wot, bq, cos_t, sin_t, T, hd, h0, nh):
    S, W = x_all.shape
    heads = W // hd
    width = nh * hd
    cols = slice(h0 * hd, h0 * hd + width)
    vm = pl.BlockSpec(memory_space=pltpu.VMEM)
    anym = pl.BlockSpec(memory_space=pl.ANY)
    f32, bf = jnp.float32, jnp.bfloat16
    return pl.pallas_call(
        functools.partial(bwd_kernel, hd, S // T, heads, h0, width, stats.shape[0] * T // S),
        out_shape=jax.ShapeDtypeStruct((3 * width, T), f32),
        in_specs=[pl.BlockSpec(memory_space=pltpu.SMEM)] + [anym] * 4 + [vm] * 14,
        out_specs=vm,
        scratch_shapes=[pltpu.VMEM((4, T, W), bf), pltpu.VMEM((4, T, W), bf), pltpu.VMEM((T, 128), f32), pltpu.VMEM((T, 128), f32),
                        pltpu.VMEM((4, T, width), bf), pltpu.VMEM((4, T, width), bf), pltpu.VMEM((T, W), bf),
                        pltpu.VMEM((2, T, width), bf), pltpu.VMEM((2, T, width), bf), pltpu.VMEM((nh, 2 * hd, T), bf), pltpu.VMEM((nh, 2 * hd, T), bf),
                        pltpu.VMEM((4, T, T), f32), pltpu.VMEM((width, T), f32), pltpu.VMEM((width, T), f32),
                        pltpu.SemaphoreType.DMA((4, 2)), pltpu.SemaphoreType.DMA((4, 2))],
        compiler_params=pltpu.CompilerParams(vmem_limit_bytes=VMEM_LIMIT),
        cost_estimate=pl.CostEstimate(flops=100_000_000_000, bytes_accessed=30_000_000, transcendentals=0),
        name="attn_bwd",
    )(me, x_all, dy_all, k_all, v_all, *tab, stats, qt, d_ctx_bf, gain, shift, wq[:, cols], wot[:, cols], bq[:, cols], cos_t, sin_t)


def mlp_kernel(x_ref, dy_ref, g_ref, s_ref, wu_ref, bu_ref, wd_ref, du_ref, dd_ref, db_ref):
    @pl.when(pl.program_id(0) == 0)
    def _():
        du_ref[...] = jnp.zeros_like(du_ref)
        dd_ref[...] = jnp.zeros_like(dd_ref)
        db_ref[...] = jnp.zeros_like(db_ref)

    h = layer_norm(x_ref[...].astype(jnp.float32), g_ref[...], s_ref[...])[0].astype(jnp.bfloat16)
    dy = dy_ref[...]
    act, slope = exact_gelu(mm(h, wu_ref[...]) + bu_ref[...])
    d_up = mm(dy, wd_ref[...]) * slope
    keep = du_ref.shape[0]
    db_ref[...] += jnp.sum(d_up, axis=0, keepdims=True)
    du_ref[...] += mm(d_up.astype(jnp.bfloat16).T, h)[:keep]
    dd_ref[...] += mm(act.astype(jnp.bfloat16).T, dy)[:keep]


def mlp_grads(x_all, dy_all, gain, shift, wu, bu, wd, keep):
    S, W = x_all.shape
    F = wu.shape[1]
    R = 512
    const = lambda j: (0, 0)
    return pl.pallas_call(
        mlp_kernel,
        grid=(S // R,),
        out_shape=[jax.ShapeDtypeStruct((keep, W), jnp.float32)] * 2 + [jax.ShapeDtypeStruct((1, F), jnp.float32)],
        in_specs=[pl.BlockSpec((R, W), lambda j: (j, 0)), pl.BlockSpec((R, W), lambda j: (j, 0)), pl.BlockSpec((1, W), const), pl.BlockSpec((1, W), const),
                  pl.BlockSpec((W, F), const), pl.BlockSpec((1, F), const), pl.BlockSpec((W, F), const)],
        out_specs=[pl.BlockSpec((keep, W), const)] * 2 + [pl.BlockSpec((1, F), const)],
        compiler_params=pltpu.CompilerParams(vmem_limit_bytes=VMEM_LIMIT, dimension_semantics=("arbitrary",)),
        cost_estimate=pl.CostEstimate(flops=20_000_000_000, bytes_accessed=26_000_000, transcendentals=0),
        name="mlp_grads",
    )(x_all, dy_all, gain, shift, wu, bu, wd)


def solution(mesh):
    cp_size = mesh.shape['cp']
    row_spec = P('dp', 'cp', None)
    in_specs = (row_spec, row_spec) + (P(),) * 12
    out_specs = (row_spec, row_spec, P('dp'), P('dp'), P('dp'), P('dp'), P('dp', None, None, None), P('dp', None, None), P('dp', None), P('dp'), P('dp', None), P('dp'), P('dp', None), P('dp'))
    bf, f32 = jnp.bfloat16, jnp.float32

    def local_layer(x_blk, dy_blk, ln1_gain, ln1_bias, ln2_gain, ln2_bias, w_qkv, b_qkv, w_out, b_out, w_up, b_up, w_down, b_down):
        T, W = x_blk.shape[1:]
        heads, hd = w_qkv.shape[1], w_qkv.shape[3]
        FF = w_up.shape[1]
        S = T * cp_size
        me = lax.axis_index('cp')
        me1 = me.astype(jnp.int32).reshape(1)
        row = lambda v: v.reshape(1, -1).astype(f32)

        TN = (((0,), (0,)), ((), ()))
        x_own = x_blk[0]
        dy_own = dy_blk[0]
        dy_bf = dy_own.astype(bf)
        x_all = lax.all_gather(x_own, 'cp', tiled=True)
        dy_all = lax.all_gather(dy_bf, 'cp', tiled=True)

        w_rows = w_qkv.transpose(1, 2, 3, 0)
        wq, wk = (pair_rows(w_rows[:, c]).T for c in (0, 1))
        wv = w_rows[:, 2].reshape(W, W).T
        b_rows = b_qkv.astype(f32)[..., None]
        b3 = jnp.stack([pair_rows(b_rows[:, 0])[:, 0], pair_rows(b_rows[:, 1])[:, 0], b_rows[:, 2].reshape(W)])
        wot = w_out.T
        tab = lane_tables(jnp.arange(T), hd) + lane_tables(jnp.arange(cp_size) * T, hd)
        ang = rope_angles(me * T + jnp.arange(T), hd).T
        cos_o, sin_o = jnp.cos(ang), jnp.sin(ang)

        x_rows = x_own.astype(f32)
        h_attn, x_norm1, inv_std1 = layer_norm(x_rows, ln1_gain, ln1_bias)
        h_attn = h_attn.astype(bf)
        h_mlp, x_norm2, inv_std2 = layer_norm(x_rows, ln2_gain, ln2_bias)
        h_mlp = h_mlp.astype(bf)
        gelu_out, slope = exact_gelu(mm(h_mlp, w_up) + b_up.astype(f32))
        y_part = x_rows + (mm(gelu_out.astype(bf), w_down) + b_down.astype(f32)) + b_out.astype(f32)
        d_up_bf = (mm(dy_bf, w_down, NT) * slope).astype(bf)
        d_h_mlp = mm(d_up_bf, w_up, NT)
        d_ctx = mm(dy_bf, w_out, NT)
        d_ctx_bf = d_ctx.astype(bf)
        dx_mlp, d_ln2_gain, d_ln2_bias = norm_backward(d_h_mlp, x_norm2, inv_std2, ln2_gain)
        dx_part = dy_own + dx_mlp
        dy_sum = jnp.sum(dy_own, axis=0)
        F = FF // cp_size
        F_pad = -(-F // 128) * 128
        pad = lambda a, ax: jnp.pad(a, [(0, F_pad - F) if d == ax else (0, 0) for d in range(a.ndim)])
        wu_s = pad(lax.dynamic_slice_in_dim(w_up, me * F, F, 1), 1)
        bu_s = pad(lax.dynamic_slice_in_dim(b_up.astype(f32), me * F, F, 0), 0).reshape(1, F_pad)
        wd_s = pad(lax.dynamic_slice_in_dim(w_down, me * F, F, 0).T, 1)

        (x_in, y_part, dx_part, d_ln2_gain, d_ln2_bias, dy_sum, d_ctx, d_ctx_bf, h_attn, wq, wk, wv, wot, wu_s, wd_s) = lax.optimization_barrier(
            (x_all, y_part, dx_part, d_ln2_gain, d_ln2_bias, dy_sum, d_ctx, d_ctx_bf, h_attn, wq, wk, wv, wot, wu_s, wd_s))
        k_all, v_all, attn_norm, lse, qt = fwd_attention(me1, x_in, tab, row(ln1_gain), row(ln1_bias), wq, wk, wv, b3, T, hd)
        delta = jnp.sum((d_ctx * attn_norm).reshape(T, heads, hd), axis=-1).T
        fill = jnp.zeros((2 * heads, T), f32)
        stats = lax.all_gather(jnp.concatenate([lse, delta, fill], axis=0), 'cp', tiled=True)
        attn_ctx = attn_norm.astype(bf)
        y_rows = (y_part + mm(attn_ctx, w_out)).astype(bf)
        d_w_out = mm(attn_ctx, dy_bf, TN)

        dy_in, _ = lax.optimization_barrier((dy_all, lse))
        du_s, dd_s, db_s = mlp_grads(x_in, dy_in, row(ln2_gain), row(ln2_bias), wu_s, bu_s, wd_s, F)
        d_b_up = lax.dynamic_update_slice(jnp.zeros((FF,), f32), db_s[0, :F], (me * F,))

        stats, y_rows, d_w_out, du_s, dd_s = lax.optimization_barrier((stats, y_rows, d_w_out, du_s, dd_s))
        d_w_up = lax.all_gather(du_s, 'cp', tiled=True)
        d_w_down = lax.all_gather(dd_s, 'cp', tiled=True)
        d3 = bwd_attention(me1, x_in, dy_in, tab, k_all, v_all, stats, qt, d_ctx_bf, row(ln1_gain), row(ln1_bias), wq, wot, b3[0:1], cos_o, sin_o, T, hd, 0, heads)
        d3, d_w_up, d_w_down = lax.optimization_barrier((d3, d_w_up, d_w_down))
        d3_bf = d3.astype(bf)
        d_h = mm(d3_bf, w_rows.reshape(3 * W, W), TN)
        d_w_rows = mm(d3_bf, h_attn)
        dx_attn, d_ln1_gain, d_ln1_bias = norm_backward(d_h, x_norm1, inv_std1, ln1_gain)
        dx_rows = dx_part + dx_attn
        small = jnp.concatenate([d_ln1_gain, d_ln1_bias, d_ln2_gain, d_ln2_bias, dy_sum, jnp.sum(d3, axis=1), d_b_up]).reshape(-1, W)
        d_w_rows, tail = lax.psum((d_w_rows, jnp.concatenate([d_w_out, small], axis=0)), 'cp')
        d_w_out = tail[:W]
        small = tail[W:].reshape(-1)
        d_w_qkv = d_w_rows.reshape(heads, 3, hd, W).transpose(3, 0, 1, 2)
        vec = [small[i * W:(i + 1) * W] for i in range(5)]
        d_b_qkv = small[5 * W:8 * W].reshape(heads, 3, hd)
        d_b_up = small[8 * W:]
        return (y_rows[None], dx_rows[None], vec[0], vec[1], vec[2], vec[3], d_w_qkv, d_b_qkv, d_w_out, vec[4], d_w_up.T, d_b_up, d_w_down, vec[4])

    return jax.shard_map(local_layer, mesh=mesh, in_specs=in_specs, out_specs=out_specs, check_vma=False)
```

time: 721 us -> 503 us (0.70); the launches traced: 712 us -> 502 us
  blocking collectives: 209 us -> 0 us
  waiting for transfers between devices: 86.6 us -> 213 us
  Pallas kernels: 234 us -> 157 us
  local copies, waits for them, and re-layouts: 104 us -> 62.9 us
    all_gather x1 -> x0, blocking collectives: 158 us -> none  [local_layer(): lax.all_gather(jnp.concatenate([lse, delta], axis=0), 'cp', tiled=True)]
    psum x1, waiting for transfers between devices: 0.01 us -> 99.3 us  [local_layer(): lax.psum((d_w_rows, jnp.concatenate([d_w_out, small], axis=0)), 'cp')]
    pallas_call x1, Pallas kernels: 197 us -> 122 us  [bwd_attention(): pl.pallas_call(functools.partial(bwd_kernel, hd, S // T, heads, h0, width...]
    psum x1 -> x0, blocking collectives: 50.9 us -> none  [local_layer(): lax.psum((d_ln1_gain, d_ln1_bias, d_ln2_gain, d_ln2_bias, d_w_qkv, d_b_qk...]
    all_gather x1, waiting for transfers between devices: 41.6 us -> 0.02 us  [local_layer(): d_w_down = lax.all_gather(dd_s, 'cp', tiled=True)]
    all_gather x1, waiting for transfers between devices: 0.02 us -> 41.4 us  [local_layer(): dy_all = lax.all_gather(dy_bf, 'cp', tiled=True)]
    concatenate x2 -> x3, local copies, waits for them, and re-layouts: 39.3 us -> 1.25 us  [the longest x1 0.59 us: local_layer(): jnp.concatenate([lse, delta, fill], axis=0)]
    sin x1 -> x3, other arithmetic: 18.2 us -> 2.73 us  [the longest x2 2.01 us: lane_tables(): return (jnp.cos(angles), jnp.sin(angles))]
  transfers between devices with their start and end apart: 5 -> 6, of which waited for: 2 -> 4; matrix products, arithmetic and copies ran while one was open for 20% -> 14% of each run, Pallas kernels for 5% -> 31%
where the time goes in v2:
time: 503 us; the launch traced here: 502 us
  waiting for transfers between devices  213 us (42%)
  Pallas kernels  157 us (31%)
  local copies, waits for them, and re-layouts  62.9 us (13%)
  matrix products  30.9 us (6%)
  other arithmetic  22.3 us (4%)
  between operations  14.7 us (3%)
    pallas_call x1, Pallas kernels, bwd_attention(): pl.pallas_call(functools.partial(bwd_kernel, hd, S // T, heads, h0, width...  122 us
    psum x1, waiting for transfers between devices, local_layer(): lax.psum((d_w_rows, jnp.concatenate([d_w_out, small], axis=0)), 'cp')  99.3 us
    all_gather x1, waiting for transfers between devices, local_layer(): lax.all_gather(jnp.concatenate([lse, delta, fill], axis=0), 'cp', tiled=T...  56.4 us
    all_gather x1, waiting for transfers between devices, local_layer(): dy_all = lax.all_gather(dy_bf, 'cp', tiled=True)  41.4 us
    unnamed x93, local copies, waits for them, and re-layouts  36.8 us
    dot_general x8, matrix products, mm(): return lax.dot_general(a, b, dims, preferred_element_type=jnp.float32)  30.9 us
    pallas_call x1, Pallas kernels, mlp_grads(): pl.pallas_call(mlp_kernel, grid=(S // R,), out_shape=[jax.ShapeDtypeStruc...  23.5 us
    all_gather x1, waiting for transfers between devices, local_layer(): x_all = lax.all_gather(x_own, 'cp', tiled=True)  14.8 us
  transfers between devices with their start and end apart: 6, of which 4 were waited for; matrix products, arithmetic and copies ran while one was open for 14% of the time, Pallas kernels for 31%

profile of v2, /device:TPU:97, one launch (start us, length us, event | category | flops | bytes accessed | tf_op | source)
XLA Modules:
  0.0 501.6 jit_solution(5255132082602217888)
XLA Ops:
  8.1 2.5 fusion.58
  11.4 2.2 copy.68
  15.2 1.5 copy.54
  18.9 2.5 copy.53
  26.3 1.4 copy.55
  27.8 1.4 copy.56
  33.1 5.6 %convolution_add_fusion = f32[256,3072]{1,0:T(8,128)} fusion(bf16[768,3072]{1,0:T(8,128)(2,1)} %param.24, f32[3072]{0:T(1024)S(1)} %convert_element_type.69, bf16[1,256,768]{2,1,0:T(8,128)(2,1)S(1)} %copy-done.2, f32[768]{0:T(1024)S(1)} %copy-done.28, f32[768]{0:T(1024)S(1)} %copy-done.13, f32[256]{0:T(256)S(1)} %add_rsqrt_fusion, ...), kind=kOutput, calls=%fused_computation.2 | convolution fusion | flops 1209925632 | bytes 8278016 | tf_op jit(solution)/shard_map/dot_general | solution.py:19
  38.6 9.0 %fusion.28 = (f32[768]{0:T(1024)}, f32[256]{0:T(256)S(1)}, f32[256]{0:T(256)S(1)}, f32[768]{0:T(1024)}, bf16[256,768]{1,0:T(8,128)(2,1)}, /*index=5*/f32[256,768]{1,0:T(8,128)S(1)}) fusion(bf16[1,256,768]{2,1,0:T(8,128)(2,1)S(1)} %copy-done.2, f32[256]{0:T(256)S(1)} %add_rsqrt_fusion, f32[256]{0:T(256)S(1)} %broadcast_multiply_fusion.4, ...), kind=kOutput, calls=%fused_computation.42 | convolution fusion | flops 2426337280 | bytes 14568448 | tf_op jit(solution)/shard_map/dot_general | solution.py:19
  52.2 4.8 fusion.8
  56.9 14.8 %all-gather.15.cloned.1.call-done = bf16[1,8192,768]{2,1,0:T(8,128)(2,1)} async-done(((bf16[1,256,768]{2,1,0:T(8,128)(2,1)}), bf16[1,8192,768]{2,1,0:T(8,128)(2,1)}) %all-gather.15.cloned.1.call-update) | async-done | bytes 12582928 | tf_op jit(solution)/shard_map/all_gather | solution.py:496
  71.7 11.0 %attn_fwd.1 = (bf16[8192,768]{1,0:T(8,128)(2,1)}, bf16[8192,768]{1,0:T(8,128)(2,1)}, f32[256,768]{1,0:T(8,128)}, f32[12,256]{1,0:T(8,128)}, bf16[768,256]{1,0:T(8,128)(2,1)}) custom-call(s32[1]{0:T(128)} %bitcast.me_ref, bf16[8192,768]{1,0:T(8,128)(2,1)} %bitcast.165, f32[256,128]{1,0:T(8,128)} %get-tuple-element.163.cl_ref, ...), custom_call_target="tpu_custom_call" | custom-call | flops 40000000000 | bytes 40000000 | tf_op jit(solution)/shard_map/attn_fwd/pallas_call | solution.py:247
  82.8 2.2 mul.220
  85.0 1.4 copy.62
  89.8 41.4 %all-gather.9.cloned.1.call-done.dy_ref.dy_hbm = bf16[8192,768]{1,0:T(8,128)(2,1)} async-done(((bf16[256,768]{1,0:T(8,128)(2,1)}), bf16[8192,768]{1,0:T(8,128)(2,1)}) %all-gather.9.cloned.1.call-update) | async-done | bytes 12582928 | tf_op jit(solution)/shard_map/all_gather | solution.py:497
  131.2 2.4 fusion.9
  133.6 1.9 fusion.47
  135.5 23.5 %mlp_grads.1 = (f32[96,768]{1,0:T(8,128)}, f32[96,768]{1,0:T(8,128)}, f32[1,128]{1,0:T(1,128)}) custom-call(bf16[8192,768]{1,0:T(8,128)(2,1)} %bitcast.166, bf16[8192,768]{1,0:T(8,128)(2,1)} %all-gather.9.cloned.1.call-done.dy_ref.dy_hbm, f32[1,768]{1,0:T(1,128)} %broadcast_in_dim.26.g_ref, f32[1,768]{1,0:T(1,128)} %broadcast_in_dim.27.s_ref, ...), custom_call_target="tpu_custom_call" | custom-call | flops 20000000000 | bytes 26000000 | tf_op jit(solution)/shard_map/mlp_grads/pallas_call | solution.py:463
  159.0 56.4 %all-gather.7.cloned.1.call-done.stats_ref = f32[1536,256]{1,0:T(8,128)} async-done(((f32[48,256]{1,0:T(8,128)}), f32[1536,256]{1,0:T(8,128)}) %all-gather.7.cloned.1.call-update) | async-done | bytes 1572880 | tf_op jit(solution)/shard_map/all_gather | solution.py:535
  217.7 122.4 %attn_bwd.1 = f32[2304,256]{1,0:T(8,128)} custom-call(s32[1]{0:T(128)} %bitcast.me_ref, bf16[8192,768]{1,0:T(8,128)(2,1)} %bitcast.167, bf16[8192,768]{1,0:T(8,128)(2,1)} %all-gather.9.cloned.1.call-done.dy_ref.dy_hbm, bf16[8192,768]{1,0:T(8,128)(2,1)} %get-tuple-element.61.k_hbm, bf16[8192,768]{1,0:T(8,128)(2,1)} %get-tuple-element.62.v_hbm, ...), custom_call_target="tpu_custom_call" | custom-call | flops 99999997952 | bytes 30000000 | tf_op jit(solution)/shard_map/attn_bwd/pallas_call | solution.py:425
  340.1 2.8 reduce_sum.137
  343.0 4.1 fusion.38
  347.1 2.0 fusion.36
  351.7 1.3 constant_dynamic-update-slice_fusion.4
  353.0 1.3 constant_dynamic-update-slice_fusion.3
  355.6 1.3 constant_dynamic-update-slice_fusion.1
  358.2 3.2 pad_maximum_fusion
  361.6 9.7 %copy.64 = f32[768,3072]{1,0:T(8,128)} copy(f32[768,3072]{0,1:T(8,128)} %bitcast.143) | data formatting | bytes 18874368
  372.5 99.3 %all-reduce.6.cloned.1.call-done = (f32[780,768]{1,0:T(8,128)}, f32[768,12,3,64]{0,3,2,1:T(8,128)}) async-done(((f32[780,768]{1,0:T(8,128)}, f32[768,12,3,64]{0,3,2,1:T(8,128)}), (f32[780,768]{1,0:T(8,128)}, f32[768,12,3,64]{0,3,2,1:T(8,128)})) %all-reduce.6.cloned.1.call-update) | async-done | bytes 9474064 | tf_op jit(solution)/shard_map/psum | solution.py:555
  471.8 3.2 slice.184
  475.7 1.7 slice_reduce_fusion.1
  480.0 6.7 %copy.82 = f32[768,12,3,64]{0,3,2,1:T(8,128)} copy(f32[768,12,3,64]{0,3,2,1:T(8,128)} %get-tuple-element.230) | data formatting | bytes 14155776
  486.7 8.0 %copy.83 = f32[3072,768]{1,0:T(8,128)} copy(f32[3072,768]{1,0:T(8,128)} %all-gather.13.cloned.1.call-done) | data formatting | bytes 18874368
  (166 shorter events, 34.1 us)
Async XLA Ops:
  7.2 64.5 %all-gather.15.cloned.1.call-start = ((), (), s32[]{:S(2)}) async-start(), calls=%async_computation.4 | async-start | bytes 12976128 | tf_op jit(solution)/shard_map/all_gather | solution.py:496
  8.0 123.2 %all-gather.9.cloned.1.call-start = ((), (), s32[]{:S(2)}) async-start(), calls=%async_computation.1 | async-start | bytes 12976128 | tf_op jit(solution)/shard_map/all_gather | solution.py:497
  10.6 204.7 %all-gather.7.cloned.1.call-start = ((), (), s32[]{:S(2)}) async-start(), calls=%async_computation | async-start | bytes 1622016 | tf_op jit(solution)/shard_map/all_gather | solution.py:535
  18.9 8.8 %copy-start.1 = (bf16[768,768]{1,0:T(8,128)(2,1)S(1)}, bf16[768,768]{1,0:T(8,128)(2,1)}, u32[]{:S(2)}) copy-start(bf16[768,768]{1,0:T(8,128)(2,1)} %param.22) | copy-start | bytes 3538948
  23.5 5.7 %copy-start.20 = (bf16[12,3,64]{2,1,0:T(4,128)(2,1)S(1)}, bf16[12,3,64]{2,1,0:T(4,128)(2,1)}, u32[]{:S(2)}) copy-start(bf16[12,3,64]{2,1,0:T(4,128)(2,1)} %param.21) | copy-start | bytes 13828
  23.7 6.4 %copy-start.14 = (f32[768]{0:T(1024)S(1)}, f32[768]{0:T(1024)}, u32[]{:S(2)}) copy-start(f32[768]{0:T(1024)} %param.16) | copy-start | bytes 9220
  23.7 7.0 %copy-start.27 = (f32[768]{0:T(1024)S(1)}, f32[768]{0:T(1024)}, u32[]{:S(2)}) copy-start(f32[768]{0:T(1024)} %param.17) | copy-start | bytes 9220
  23.7 8.9 %copy-start.2 = (bf16[1,256,768]{2,1,0:T(8,128)(2,1)S(1)}, bf16[1,256,768]{2,1,0:T(8,128)(2,1)}, u32[]{:S(2)}) copy-start(bf16[1,256,768]{2,1,0:T(8,128)(2,1)} %param.14) | copy-start | bytes 1179652
  25.6 7.4 %copy-start.13 = (f32[768]{0:T(1024)S(1)}, f32[768]{0:T(1024)}, u32[]{:S(2)}) copy-start(f32[768]{0:T(1024)} %param.18) | copy-start | bytes 9220
  25.6 7.4 %copy-start.28 = (f32[768]{0:T(1024)S(1)}, f32[768]{0:T(1024)}, u32[]{:S(2)}) copy-start(f32[768]{0:T(1024)} %param.19) | copy-start | bytes 9220
  29.8 8.8 %copy-start.21 = (f32[1,768]{1,0:T(1,128)}, f32[1,768]{1,0:T(1,128)S(1)}, u32[]{:S(2)}) copy-start(f32[1,768]{1,0:T(1,128)S(1)} %stack_squeeze_reshape.6.bq_ref) | copy-start | bytes 9220
  31.9 6.7 %copy-start.25 = (f32[8]{0:T(128)}, f32[8]{0:T(128)S(1)}, u32[]{:S(2)}) copy-start(f32[8]{0:T(128)S(1)} %get-tuple-element.176) | copy-start | bytes 100
  32.8 18.2 %copy-start.11 = (f32[256]{0:T(256)}, f32[256]{0:T(256)S(1)}, u32[]{:S(2)}) copy-start(f32[256]{0:T(256)S(1)} %broadcast_multiply_fusion.4) | copy-start | bytes 3076
  33.0 17.9 %copy-start.22 = (f32[256]{0:T(256)}, f32[256]{0:T(256)S(1)}, u32[]{:S(2)}) copy-start(f32[256]{0:T(256)S(1)} %add_rsqrt_fusion) | copy-start | bytes 3076
  33.1 5.6 %copy-start.5 = (bf16[256,768]{1,0:T(8,128)(2,1)S(1)}, bf16[256,768]{1,0:T(8,128)(2,1)}, u32[]{:S(2)}) copy-start(bf16[256,768]{1,0:T(8,128)(2,1)} %get-tuple-element.147) | copy-start | bytes 1179652
  82.8 5.9 %copy-start.29 = (f32[768]{0:T(1024)S(1)}, f32[768]{0:T(1024)}, u32[]{:S(2)}) copy-start(f32[768]{0:T(1024)} %param.19) | copy-start | bytes 9220
  82.8 48.4 %copy-start.4 = (f32[256,768]{1,0:T(8,128)S(1)}, f32[256,768]{1,0:T(8,128)}, u32[]{:S(2)}) copy-start(f32[256,768]{1,0:T(8,128)} %get-tuple-element.52) | copy-start | bytes 2359300
  87.2 252.8 %all-gather.11.cloned.1.call-start = ((), (), s32[]{:S(2)}) async-start(), calls=%async_computation.2 | async-start | bytes 9732096 | tf_op jit(solution)/shard_map/all_gather | solution.py:545
  135.5 80.7 %copy-start.26 = (f32[8]{0:T(128)S(1)}, f32[8]{0:T(128)}, u32[]{:S(2)}) copy-start(f32[8]{0:T(128)} %copy-done.25) | copy-start | bytes 100
  215.4 124.7 %all-gather.13.cloned.1.call-start = ((), (), s32[]{:S(2)}) async-start(), calls=%async_computation.3 | async-start | bytes 9732096 | tf_op jit(solution)/shard_map/all_gather | solution.py:546
  216.1 255.7 %all-reduce.6.cloned.1.call-start = ((), (), s32[]{:S(2)}) async-start(), calls=%async_computation.5 | async-start | bytes 18972672 | tf_op jit(solution)/shard_map/psum | solution.py:555
  217.7 125.3 %copy-start.9 = (bf16[256,768]{1,0:T(8,128)(2,1)S(1)}, bf16[256,768]{1,0:T(8,128)(2,1)}, u32[]{:S(2)}) copy-start(bf16[256,768]{1,0:T(8,128)(2,1)} %get-tuple-element.75) | copy-start | bytes 1179652
  347.0 4.6 copy-start.33
  347.1 5.9 %copy-start.32 = (f32[768]{0:T(1024)S(1)}, f32[768]{0:T(1024)}, u32[]{:S(2)}) copy-start(f32[768]{0:T(1024)} %get-tuple-element.72) | copy-start | bytes 9220
  347.1 7.2 %copy-start.17 = (f32[768]{0:T(1024)S(1)}, f32[768]{0:T(1024)}, u32[]{:S(2)}) copy-start(f32[768]{0:T(1024)} %get-tuple-element.73) | copy-start | bytes 9220
  347.1 8.5 %copy-start.10 = (f32[2304]{0:T(1024)S(1)}, f32[2304]{0:T(1024)}, u32[]{:S(2)}) copy-start(f32[2304]{0:T(1024)} %reduce_sum.137) | copy-start | bytes 27652
  361.5 9.7 %copy-start.37 = (f32[256]{0:T(256)S(1)}, f32[256]{0:T(256)}, u32[]{:S(2)}) copy-start(f32[256]{0:T(256)} %get-tuple-element.126) | copy-start | bytes 3076
  361.5 9.7 %copy-start.36 = (f32[256]{0:T(256)S(1)}, f32[256]{0:T(256)}, u32[]{:S(2)}) copy-start(f32[256]{0:T(256)} %get-tuple-element.130) | copy-start | bytes 3076
  361.6 9.7 %copy-start.8 = (f32[256,768]{1,0:T(8,128)S(1)}, f32[256,768]{1,0:T(8,128)}, u32[]{:S(2)}) copy-start(f32[256,768]{1,0:T(8,128)} %fusion.27) | copy-start | bytes 2359300
  361.6 9.7 %copy-start.16 = (f32[768]{0:T(1024)S(1)}, f32[768]{0:T(1024)}, u32[]{:S(2)}) copy-start(f32[768]{0:T(1024)} %param.16) | copy-start | bytes 9220
  361.6 9.7 %copy-start.24 = (f32[256]{0:T(256)S(1)}, f32[256]{0:T(256)}, u32[]{:S(2)}) copy-start(f32[256]{0:T(256)} %copy-done.22) | copy-start | bytes 3076
  477.4 9.4 %copy-start.19 = (f32[768]{0:T(1024)}, f32[768]{0:T(1024)S(1)}, u32[]{:S(2)}) copy-start(f32[768]{0:T(1024)S(1)} %get-tuple-element.233) | copy-start | bytes 9220
  (14 other events, 55.4 us)
Sparse Core Ops, SparseCore 0:
  10.1 61.5 all-gather.14
  74.4 56.7 all-gather.8
  133.9 81.4 all-gather.6
  217.9 49.2 all-gather.10
  269.6 49.3 all-gather.12
  361.7 110.0 all-reduce.5

commit v3 on v2

--- a/solution.py
+++ b/solution.py
@@ -136,29 +136,20 @@
         hsc[...] = layer_norm(xb[(j + 1) % DEEP].astype(jnp.float32), g_ref[...], s_ref[...])[0].astype(jnp.bfloat16)
         turn(tab, jnp.where(j < 0, me, j), cs, ss)
 
-    def piece(i, slot):
-        cols = slice((i % tiles) * 256, (i % tiles + 1) * 256)
-        if i < tiles:
-            kst[slot, :, cols] = rotate(mm(hsc[...], wk_ref[:, cols]) + b_ref[1:2, cols], cs[...], ss[...]).astype(jnp.bfloat16)
-        else:
-            vst[slot, :, cols] = (mm(hsc[...], wv_ref[:, cols]) + b_ref[2:3, cols]).astype(jnp.bfloat16)
-
-    def scores(slot, p):
-        kp = kst[slot, :, p * 2 * hd:(p + 1) * 2 * hd]
-        return [mm(kp, qtm[h]) for h in (2 * p, 2 * p + 1)]
+    def project(slot):
+        kst[slot] = rotate(mm(hsc[...], wk_ref[...]) + b_ref[1:2], cs[...], ss[...]).astype(jnp.bfloat16)
+        vst[slot] = (mm(hsc[...], wv_ref[...]) + b_ref[2:3]).astype(jnp.bfloat16)
+
+    def scores(slot, h):
+        return mm(kst[slot, :, h // 2 * 2 * hd:(h // 2 + 1) * 2 * hd], qtm[h])
 
     def attend(j, slot, diag):
-        ahead = scores(slot, 0) if diag else [sbuf[0], sbuf[1]]
+        ahead = [scores(slot, 0), scores(slot, 1)] if diag else [sbuf[0], sbuf[1]]
         norm(j + 1)
-        per = -(-2 * tiles // pairs)
+        project(1 - slot)
         for p in range(pairs):
             now = ahead
-            for i in range(p * per, min((p + 1) * per, 2 * tiles)):
-                piece(i, 1 - slot)
-            if p + 1 < pairs:
-                ahead = scores(slot, p + 1)
-            else:
-                ahead = scores(1 - slot, 0)
+            ahead = [scores(slot, 2 * p + 2 + i) if p + 1 < pairs else scores(1 - slot, i) for i in range(2)]
             vt = vst[slot, :, p * 2 * hd:(p + 1) * 2 * hd].T
             for i in range(2):
                 h = 2 * p + i
@@ -179,16 +170,14 @@
                     lrow[h:h + 1] = lrow[h:h + 1] * alpha + jnp.sum(e, axis=0, keepdims=True)
                     acc[rows] = acc[rows] * alpha + mm(vh, e.astype(jnp.bfloat16))
                 mrow[h:h + 1] = m
-        sbuf[0] = ahead[0]
-        sbuf[1] = ahead[1]
+        sbuf[0], sbuf[1] = ahead
 
     for j in range(-1, DEEP - 1):
         start(fetch(jnp.int32(j)))
     own = jnp.int32(-1)
     wait(fetch(own))
     norm(own)
-    for i in range(2 * tiles):
-        piece(i, 0)
+    project(0)
     for t in range(tiles):
         cols = slice(t * 256, (t + 1) * 256)
         q = rotate(mm(hsc[...], wq_ref[:, cols]) + b_ref[0:1, cols], cs[...], ss[...])
@@ -260,28 +249,22 @@
     )(me, x_all, *tab, gain, shift, wq, wk, wv, b3)
 
 
-def bwd_kernel(hd, n, heads, h0, width, srows, me_ref, x_hbm, dy_hbm, k_hbm, v_hbm, cl_ref, sl_ref, cb_ref, sb_ref, stats_ref, qt_ref, own_ref, g_ref, s_ref,
-               wq_ref, wot_ref, bq_ref, ct_ref, st_ref, d3_ref,
-               xb, yb, cs, ss, kb, vb, hsc, qsc, osc, am, bm, sbuf, acc1, acc2, kv_sem, xy_sem):
+def proj_kernel(hd, n, me_ref, x_hbm, dy_hbm, cl_ref, sl_ref, cb_ref, sb_ref, g_ref, s_ref, wq_ref, wot_ref, bq_ref, q_hbm, o_hbm,
+                xb, yb, cs, ss, hsc, qst, ost, in_sem, out_sem):
     me = me_ref[0]
-    T = xb.shape[1]
-    pairs = width // (2 * hd)
-    half = hd // 8
+    DEEP, T, W = xb.shape
     scale = hd ** -0.5
-    c0 = h0 * hd
-
     tab = (cl_ref, sl_ref, cb_ref, sb_ref)
-    DEEP = xb.shape[0]
-
-    def fetch_kv(j):
-        slot, blk = j % DEEP, jnp.minimum(j, me)
-        return (pltpu.make_async_copy(k_hbm.at[pl.ds(blk * T, T), c0:c0 + width], kb.at[slot], kv_sem.at[slot, 0]),
-                pltpu.make_async_copy(v_hbm.at[pl.ds(blk * T, T), c0:c0 + width], vb.at[slot], kv_sem.at[slot, 1]))
-
-    def fetch_xy(r):
+
+    def fetch(r):
         slot, blk = r % DEEP, jnp.minimum(me + r, n - 1)
-        return (pltpu.make_async_copy(x_hbm.at[pl.ds(blk * T, T)], xb.at[slot], xy_sem.at[slot, 0]),
-                pltpu.make_async_copy(dy_hbm.at[pl.ds(blk * T, T)], yb.at[slot], xy_sem.at[slot, 1]))
+        return (pltpu.make_async_copy(x_hbm.at[pl.ds(blk * T, T)], xb.at[slot], in_sem.at[slot, 0]),
+                pltpu.make_async_copy(dy_hbm.at[pl.ds(blk * T, T)], yb.at[slot], in_sem.at[slot, 1]))
+
+    def flush(r):
+        slot = r % 2
+        return (pltpu.make_async_copy(qst.at[slot], q_hbm.at[pl.ds((me + r) * T, T)], out_sem.at[slot, 0]),
+                pltpu.make_async_copy(ost.at[slot], o_hbm.at[pl.ds((me + r) * T, T)], out_sem.at[slot, 1]))
 
     def start(copies):
         for c in copies:
@@ -291,8 +274,86 @@
         for c in copies:
             c.wait()
 
-    def pair_cols(p):
-        return slice(p * 2 * hd, (p + 1) * 2 * hd)
+    for r in range(DEEP - 1):
+        start(fetch(jnp.int32(r)))
+
+    def step(r, _):
+        start(fetch(r + DEEP - 1))
+        wait(fetch(r))
+
+        @pl.when(r >= 2)
+        def _():
+            wait(flush(r - 2))
+
+        turn(tab, me + r, cs, ss)
+        for t in range(W // 256):
+            cols = slice(t * 256, (t + 1) * 256)
+            ost[r % 2, :, cols] = mm(yb[r % DEEP], wot_ref[:, cols]).astype(jnp.bfloat16)
+        hsc[...] = layer_norm(xb[r % DEEP].astype(jnp.float32), g_ref[...], s_ref[...])[0].astype(jnp.bfloat16)
+        for t in range(W // 256):
+            cols = slice(t * 256, (t + 1) * 256)
+            q = rotate(mm(hsc[...], wq_ref[:, cols]) + bq_ref[:, cols], cs[...], ss[...])
+            qst[r % 2, :, cols] = q.astype(jnp.bfloat16) * jnp.bfloat16(scale)
+        start(flush(r))
+        return 0
+
+    count = n - me
+    lax.fori_loop(0, count, step, 0)
+    for k in range(DEEP - 1):
+        wait(fetch(count + k))
+    wait(flush(count - 1))
+
+    @pl.when(count >= 2)
+    def _():
+        wait(flush(count - 2))
+
+
+def later_blocks(me, x_all, dy_all, tab, gain, shift, wq, wot, bq, T, hd):
+    S, W = x_all.shape
+    vm = pl.BlockSpec(memory_space=pltpu.VMEM)
+    anym = pl.BlockSpec(memory_space=pl.ANY)
+    f32, bf = jnp.float32, jnp.bfloat16
+    return pl.pallas_call(
+        functools.partial(proj_kernel, hd, S // T),
+        out_shape=[jax.ShapeDtypeStruct((S, W), bf)] * 2,
+        in_specs=[pl.BlockSpec(memory_space=pltpu.SMEM), anym, anym] + [vm] * 9,
+        out_specs=[anym, anym],
+        scratch_shapes=[pltpu.VMEM((4, T, W), bf), pltpu.VMEM((4, T, W), bf), pltpu.VMEM((T, 128), f32), pltpu.VMEM((T, 128), f32), pltpu.VMEM((T, W), bf),
+                        pltpu.VMEM((2, T, W), bf), pltpu.VMEM((2, T, W), bf), pltpu.SemaphoreType.DMA((4, 2)), pltpu.SemaphoreType.DMA((2, 2))],
+        compiler_params=pltpu.CompilerParams(vmem_limit_bytes=VMEM_LIMIT),
+        cost_estimate=pl.CostEstimate(flops=20_000_000_000, bytes_accessed=40_000_000, transcendentals=0),
+        name="later_blocks",
+    )(me, x_all, dy_all, *tab, gain, shift, wq, wot, bq)
+
+
+def bwd_kernel(hd, n, srows, me_ref, k_hbm, v_hbm, q_hbm, o_hbm, stats_ref, qt_ref, own_ref, ct_ref, st_ref, d3_ref,
+               kb, vb, qb, ob, am, bm, sbuf, acc1, acc2, kv_sem, qo_sem):
+    me = me_ref[0]
+    DEEP, T, W = kb.shape
+    heads = W // hd
+    half = hd // 8
+    scale = hd ** -0.5
+
+    def fetch_kv(j):
+        slot, blk = j % DEEP, jnp.minimum(j, me)
+        return (pltpu.make_async_copy(k_hbm.at[pl.ds(blk * T, T)], kb.at[slot], kv_sem.at[slot, 0]),
+                pltpu.make_async_copy(v_hbm.at[pl.ds(blk * T, T)], vb.at[slot], kv_sem.at[slot, 1]))
+
+    def fetch_qo(r):
+        slot, blk = r % DEEP, jnp.minimum(me + r, n - 1)
+        return (pltpu.make_async_copy(q_hbm.at[pl.ds(blk * T, T)], qb.at[slot], qo_sem.at[slot, 0]),
+                pltpu.make_async_copy(o_hbm.at[pl.ds(blk * T, T)], ob.at[slot], qo_sem.at[slot, 1]))
+
+    def start(copies):
+        for c in copies:
+            c.start()
+
+    def wait(copies):
+        for c in copies:
+            c.wait()
+
+    def pair_cols(h):
+        return slice(h // 2 * 2 * hd, (h // 2 + 1) * 2 * hd)
 
     def unrotated(z):
         mid = hd // 2
@@ -300,47 +361,48 @@
         ct, st = ct_ref[...], st_ref[...]
         return jnp.concatenate([a * ct + b * st, b * ct - a * st, z[half:mid], z[mid + half:]], axis=0)
 
+    def two_scores(left, right, slot, h):
+        return mm(left[slot, :, pair_cols(h)], am[h]), mm(right[slot, :, pair_cols(h)], bm[h])
+
     for r in range(DEEP - 1):
         start(fetch_kv(jnp.int32(r)))
-    for r in range(DEEP):
-        start(fetch_xy(jnp.int32(r)))
-    put_masked(am, qt_ref[c0:c0 + width], hd, True)
-    put_masked(bm, own_ref[:, c0:c0 + width].T, hd, False)
+        start(fetch_qo(jnp.int32(r)))
+    put_masked(am, qt_ref[...], hd, True)
+    put_masked(bm, own_ref[...].T, hd, False)
     acc1[...] = jnp.zeros_like(acc1)
-
-    def dq_scores(slot, p):
-        kp, vp = kb[slot, :, pair_cols(p)], vb[slot, :, pair_cols(p)]
-        return [(mm(kp, am[h]), mm(vp, bm[h])) for h in (2 * p, 2 * p + 1)]
-
-    def dq_block(slot, diag):
-        ahead = dq_scores(slot, 0)
-        for p in range(pairs):
-            now = ahead
-            if p + 1 < pairs:
-                ahead = dq_scores(slot, p + 1)
-            kt = kb[slot, :, pair_cols(p)].T
-            for i in range(2):
-                h = 2 * p + i
-                s, dp = now[i]
-                if diag:
-                    s = jnp.where(causal(T, True), s, NEG_BIG)
-                pr = jnp.exp(s - stats_ref[pl.ds(me * srows + h0 + h, 1), :])
-                ds = (pr * (dp - stats_ref[pl.ds(me * srows + heads + h0 + h, 1), :])).astype(jnp.bfloat16)
-                acc1[h * hd:(h + 1) * hd] += mm(head_rows(kt, i, hd, True), ds)
+    zero = jnp.int32(0)
+
+    def dq_block(j, diag):
+        slot = j % DEEP
+        ahead = [(sbuf[0], sbuf[1]), (sbuf[2], sbuf[3])]
+        for h in range(heads):
+            s, dp = ahead.pop(0)
+            ahead.append(two_scores(kb, vb, slot, h + 2) if h + 2 < heads else two_scores(kb, vb, (j + 1) % DEEP, h + 2 - heads))
+            if h % 2 == 0:
+                kt = kb[slot, :, pair_cols(h)].T
+            if diag:
+                s = jnp.where(causal(T, True), s, NEG_BIG)
+            pr = jnp.exp(s - stats_ref[pl.ds(me * srows + h, 1), :])
+            ds = (pr * (dp - stats_ref[pl.ds(me * srows + heads + h, 1), :])).astype(jnp.bfloat16)
+            acc1[h * hd:(h + 1) * hd] += mm(head_rows(kt, h % 2, hd, True), ds)
+        (sbuf[0], sbuf[1]), (sbuf[2], sbuf[3]) = ahead
+
+    wait(fetch_kv(zero))
+    sbuf[0], sbuf[1] = two_scores(kb, vb, 0, 0)
+    sbuf[2], sbuf[3] = two_scores(kb, vb, 0, 1)
 
     def dq_step(j, _):
         start(fetch_kv(j + DEEP - 1))
-        wait(fetch_kv(j))
-        dq_block(j % DEEP, False)
+        wait(fetch_kv(j + 1))
+        dq_block(j, False)
         return 0
 
     lax.fori_loop(0, me, dq_step, 0)
-    last = me % DEEP
-    wait(fetch_kv(me))
-    dq_block(last, True)
     for k in range(1, DEEP - 1):
         wait(fetch_kv(me + k))
-    for h in range(2 * pairs):
+    dq_block(me, True)
+    last = me % DEEP
+    for h in range(heads):
         d3_ref[3 * h * hd:(3 * h + 1) * hd] = unrotated(acc1[h * hd:(h + 1) * hd] * scale)
 
     put_masked(am, kb[last].T, hd, True)
@@ -348,94 +410,62 @@
     acc1[...] = jnp.zeros_like(acc1)
     acc2[...] = jnp.zeros_like(acc2)
 
-    tiles = width // 256
-
-    def norm(r):
-        hsc[...] = layer_norm(xb[r % DEEP].astype(jnp.float32), g_ref[...], s_ref[...])[0].astype(jnp.bfloat16)
-        turn(tab, jnp.minimum(me + r, n - 1), cs, ss)
-
-    def piece(i, r, slot):
-        cols = slice(i // 2 * 256, (i // 2 + 1) * 256)
-        if i % 2 == 0:
-            q = rotate(mm(hsc[...], wq_ref[:, cols]) + bq_ref[:, cols], cs[...], ss[...])
-            qsc[slot, :, cols] = q.astype(jnp.bfloat16) * jnp.bfloat16(scale)
-        else:
-            osc[slot, :, cols] = mm(yb[r % DEEP], wot_ref[:, cols]).astype(jnp.bfloat16)
-
-    def dkv_scores(slot, p):
-        qp, op = qsc[slot, :, pair_cols(p)], osc[slot, :, pair_cols(p)]
-        return [(mm(qp, am[h]), mm(op, bm[h])) for h in (2 * p, 2 * p + 1)]
-
     def dkv_block(r, diag):
-        j, slot = me + r, r % 2
-        ahead = dkv_scores(slot, 0) if diag else [(sbuf[0], sbuf[1]), (sbuf[2], sbuf[3])]
-        st = stats_ref[pl.ds(j * srows, srows), :].T
-        norm(r + 1)
-        per = -(-2 * tiles // pairs)
-        for p in range(pairs):
-            now = ahead
-            for i in range(p * per, min((p + 1) * per, 2 * tiles)):
-                piece(i, r + 1, 1 - slot)
-            ahead = dkv_scores(slot, p + 1) if p + 1 < pairs else dkv_scores(1 - slot, 0)
-            qt = qsc[slot, :, pair_cols(p)].T
-            ot = osc[slot, :, pair_cols(p)].T
-            for i in range(2):
-                h = 2 * p + i
-                s, dp = now[i]
-                if diag:
-                    s = jnp.where(causal(T, False), s, NEG_BIG)
-                rows = slice(h * hd, (h + 1) * hd)
-                pr = jnp.exp(s - st[:, h0 + h:h0 + h + 1])
-                acc2[rows] += mm(head_rows(ot, i, hd, False), pr.astype(jnp.bfloat16))
-                ds = (pr * (dp - st[:, heads + h0 + h:heads + h0 + h + 1])).astype(jnp.bfloat16)
-                acc1[rows] += mm(head_rows(qt, i, hd, True), ds)
-        for i in range(2):
-            sbuf[2 * i] = ahead[i][0]
-            sbuf[2 * i + 1] = ahead[i][1]
-
-    zero = jnp.int32(0)
-    wait(fetch_xy(zero))
-    norm(zero)
-    for i in range(2 * tiles):
-        piece(i, zero, 0)
+        slot = r % DEEP
+        ahead = [(sbuf[0], sbuf[1]), (sbuf[2], sbuf[3])]
+        stc = stats_ref[pl.ds((me + r) * srows, 2 * heads), :].T
+        for h in range(heads):
+            s, dp = ahead.pop(0)
+            ahead.append(two_scores(qb, ob, slot, h + 2) if h + 2 < heads else two_scores(qb, ob, (r + 1) % DEEP, h + 2 - heads))
+            if h % 2 == 0:
+                qt = qb[slot, :, pair_cols(h)].T
+                ot = ob[slot, :, pair_cols(h)].T
+            if diag:
+                s = jnp.where(causal(T, False), s, NEG_BIG)
+            rows = slice(h * hd, (h + 1) * hd)
+            pr = jnp.exp(s - stc[:, h:h + 1])
+            acc2[rows] += mm(head_rows(ot, h % 2, hd, False), pr.astype(jnp.bfloat16))
+            ds = (pr * (dp - stc[:, heads + h:heads + h + 1])).astype(jnp.bfloat16)
+            acc1[rows] += mm(head_rows(qt, h % 2, hd, True), ds)
+        (sbuf[0], sbuf[1]), (sbuf[2], sbuf[3]) = ahead
+
+    wait(fetch_qo(zero))
+    sbuf[0], sbuf[1] = two_scores(qb, ob, 0, 0)
+    sbuf[2], sbuf[3] = two_scores(qb, ob, 0, 1)
 
     def dkv_step(r, diag):
-        wait(fetch_xy(r + 1))
-        start(fetch_xy(r + DEEP))
+        start(fetch_qo(r + DEEP - 1))
+        wait(fetch_qo(r + 1))
         dkv_block(r, diag)
         return 0
 
     dkv_step(zero, True)
     lax.fori_loop(1, n - me, lambda r, _: dkv_step(r, False), 0)
-    for k in range(1, DEEP):
-        wait(fetch_xy(n - me + k))
-    for h in range(2 * pairs):
+    for k in range(1, DEEP - 1):
+        wait(fetch_qo(n - me + k))
+    for h in range(heads):
         d3_ref[(3 * h + 1) * hd:(3 * h + 2) * hd] = unrotated(acc1[h * hd:(h + 1) * hd])
         d3_ref[(3 * h + 2) * hd:(3 * h + 3) * hd] = acc2[h * hd:(h + 1) * hd]
 
 
-def bwd_attention(me, x_all, dy_all, tab, k_all, v_all, stats, qt, d_ctx_bf, gain, shift, wq, wot, bq, cos_t, sin_t, T, hd, h0, nh):
-    S, W = x_all.shape
+def bwd_attention(me, k_all, v_all, q_all, o_all, stats, qt, d_ctx_bf, cos_t, sin_t, T, hd):
+    S, W = k_all.shape
     heads = W // hd
-    width = nh * hd
-    cols = slice(h0 * hd, h0 * hd + width)
     vm = pl.BlockSpec(memory_space=pltpu.VMEM)
     anym = pl.BlockSpec(memory_space=pl.ANY)
     f32, bf = jnp.float32, jnp.bfloat16
     return pl.pallas_call(
-        functools.partial(bwd_kernel, hd, S // T, heads, h0, width, stats.shape[0] * T // S),
-        out_shape=jax.ShapeDtypeStruct((3 * width, T), f32),
-        in_specs=[pl.BlockSpec(memory_space=pltpu.SMEM)] + [anym] * 4 + [vm] * 14,
+        functools.partial(bwd_kernel, hd, S // T, stats.shape[0] * T // S),
+        out_shape=jax.ShapeDtypeStruct((3 * W, T), f32),
+        in_specs=[pl.BlockSpec(memory_space=pltpu.SMEM)] + [anym] * 4 + [vm] * 5,
         out_specs=vm,
-        scratch_shapes=[pltpu.VMEM((4, T, W), bf), pltpu.VMEM((4, T, W), bf), pltpu.VMEM((T, 128), f32), pltpu.VMEM((T, 128), f32),
-                        pltpu.VMEM((4, T, width), bf), pltpu.VMEM((4, T, width), bf), pltpu.VMEM((T, W), bf),
-                        pltpu.VMEM((2, T, width), bf), pltpu.VMEM((2, T, width), bf), pltpu.VMEM((nh, 2 * hd, T), bf), pltpu.VMEM((nh, 2 * hd, T), bf),
-                        pltpu.VMEM((4, T, T), f32), pltpu.VMEM((width, T), f32), pltpu.VMEM((width, T), f32),
+        scratch_shapes=[pltpu.VMEM((4, T, W), bf)] * 4 + [pltpu.VMEM((heads, 2 * hd, T), bf), pltpu.VMEM((heads, 2 * hd, T), bf),
+                        pltpu.VMEM((4, T, T), f32), pltpu.VMEM((W, T), f32), pltpu.VMEM((W, T), f32),
                         pltpu.SemaphoreType.DMA((4, 2)), pltpu.SemaphoreType.DMA((4, 2))],
         compiler_params=pltpu.CompilerParams(vmem_limit_bytes=VMEM_LIMIT),
         cost_estimate=pl.CostEstimate(flops=100_000_000_000, bytes_accessed=30_000_000, transcendentals=0),
         name="attn_bwd",
-    )(me, x_all, dy_all, k_all, v_all, *tab, stats, qt, d_ctx_bf, gain, shift, wq[:, cols], wot[:, cols], bq[:, cols], cos_t, sin_t)
+    )(me, k_all, v_all, q_all, o_all, stats, qt, d_ctx_bf, cos_t, sin_t)
 
 
 def mlp_kernel(x_ref, dy_ref, g_ref, s_ref, wu_ref, bu_ref, wd_ref, du_ref, dd_ref, db_ref):
@@ -541,10 +571,11 @@
         du_s, dd_s, db_s = mlp_grads(x_in, dy_in, row(ln2_gain), row(ln2_bias), wu_s, bu_s, wd_s, F)
         d_b_up = lax.dynamic_update_slice(jnp.zeros((FF,), f32), db_s[0, :F], (me * F,))
 
-        stats, y_rows, d_w_out, du_s, dd_s = lax.optimization_barrier((stats, y_rows, d_w_out, du_s, dd_s))
+        q_all, o_all = later_blocks(me1, x_in, dy_in, tab, row(ln1_gain), row(ln1_bias), wq, wot, b3[0:1], T, hd)
+        stats, d_w_out, du_s, dd_s, q_all = lax.optimization_barrier((stats, d_w_out, du_s, dd_s, q_all))
         d_w_up = lax.all_gather(du_s, 'cp', tiled=True)
         d_w_down = lax.all_gather(dd_s, 'cp', tiled=True)
-        d3 = bwd_attention(me1, x_in, dy_in, tab, k_all, v_all, stats, qt, d_ctx_bf, row(ln1_gain), row(ln1_bias), wq, wot, b3[0:1], cos_o, sin_o, T, hd, 0, heads)
+        d3 = bwd_attention(me1, k_all, v_all, q_all, o_all, stats, qt, d_ctx_bf, cos_o, sin_o, T, hd)
         d3, d_w_up, d_w_down = lax.optimization_barrier((d3, d_w_up, d_w_down))
         d3_bf = d3.astype(bf)
         d_h = mm(d3_bf, w_rows.reshape(3 * W, W), TN)

time: 503 us -> 446 us (0.89)
  Pallas kernels: 157 us -> 123 us
  waiting for transfers between devices: 213 us -> 200 us
  local copies, waits for them, and re-layouts: 62.9 us -> 54.6 us
    all_gather x1, waiting for transfers between devices: 56.4 us -> 0.01 us  [local_layer(): lax.all_gather(jnp.concatenate([lse, delta, fill], axis=0), 'cp', tiled=T...]
    all_gather x1, waiting for transfers between devices: 0.02 us -> 41.2 us  [local_layer(): d_w_down = lax.all_gather(dd_s, 'cp', tiled=True)]
    pallas_call x1 -> x2, Pallas kernels: 122 us -> 89.1 us  [the longest x1 55.2 us: bwd_attention(): pl.pallas_call(functools.partial(bwd_kernel, hd, S // T, stats.shape[0] *...]
    all_gather x1, waiting for transfers between devices: 41.4 us -> 48.5 us  [local_layer(): dy_all = lax.all_gather(dy_bf, 'cp', tiled=True)]
    unnamed x93 -> x91, local copies, waits for them, and re-layouts: 36.8 us -> 31 us
  transfers between devices with their start and end apart: 6 -> 6, of which waited for: 4 -> 4; matrix products, arithmetic and copies ran while one was open for 14% -> 15% of each run, Pallas kernels for 31% -> 28%
where the time goes in v3:
time: 446 us; the launch traced here: 444 us
  waiting for transfers between devices  200 us (45%)
  Pallas kernels  123 us (28%)
  local copies, waits for them, and re-layouts  54.6 us (12%)
  matrix products  31.1 us (7%)
  other arithmetic  20.2 us (5%)
  between operations  14.7 us (3%)
    psum x1, waiting for transfers between devices, local_layer(): lax.psum((d_w_rows, jnp.concatenate([d_w_out, small], axis=0)), 'cp')  97.5 us
    pallas_call x1, Pallas kernels, bwd_attention(): pl.pallas_call(functools.partial(bwd_kernel, hd, S // T, stats.shape[0] *...  55.2 us
    all_gather x1, waiting for transfers between devices, local_layer(): dy_all = lax.all_gather(dy_bf, 'cp', tiled=True)  48.5 us
    all_gather x1, waiting for transfers between devices, local_layer(): d_w_down = lax.all_gather(dd_s, 'cp', tiled=True)  41.2 us
    pallas_call x1, Pallas kernels, later_blocks(): pl.pallas_call(functools.partial(proj_kernel, hd, S // T), out_shape=[jax...  33.9 us
    dot_general x8, matrix products, mm(): return lax.dot_general(a, b, dims, preferred_element_type=jnp.float32)  31.1 us
    unnamed x91, local copies, waits for them, and re-layouts  31 us
    pallas_call x1, Pallas kernels, mlp_grads(): pl.pallas_call(mlp_kernel, grid=(S // R,), out_shape=[jax.ShapeDtypeStruc...  23.5 us
  transfers between devices with their start and end apart: 6, of which 4 were waited for; matrix products, arithmetic and copies ran while one was open for 15% of the time, Pallas kernels for 28%

profile of v3, /device:TPU:97, one launch (start us, length us, event | category | flops | bytes accessed | tf_op | source)
XLA Modules:
  0.0 444.4 jit_solution(12494005597190258869)
XLA Ops:
  8.1 2.5 fusion.59
  11.4 2.2 copy.68
  15.2 1.5 copy.54
  19.0 2.5 copy.53
  27.1 1.4 copy.55
  28.5 1.4 copy.56
  35.5 5.5 %convolution_add_fusion = f32[256,3072]{1,0:T(8,128)} fusion(bf16[768,3072]{1,0:T(8,128)(2,1)} %param.24, f32[3072]{0:T(1024)S(1)} %convert_element_type.69, bf16[1,256,768]{2,1,0:T(8,128)(2,1)S(1)} %copy-done.3, f32[768]{0:T(1024)S(1)} %copy-done.28, f32[768]{0:T(1024)S(1)} %copy-done.16, f32[256]{0:T(256)S(1)} %add_rsqrt_fusion, ...), kind=kOutput, calls=%fused_computation.2 | convolution fusion | flops 1209925632 | bytes 8278016 | tf_op jit(solution)/shard_map/dot_general | solution.py:19
  41.1 9.0 %fusion.29 = (f32[768]{0:T(1024)}, f32[256]{0:T(256)S(1)}, f32[256]{0:T(256)S(1)}, f32[768]{0:T(1024)}, bf16[256,768]{1,0:T(8,128)(2,1)}, /*index=5*/f32[256,768]{1,0:T(8,128)S(1)}) fusion(bf16[1,256,768]{2,1,0:T(8,128)(2,1)S(1)} %copy-done.3, f32[256]{0:T(256)S(1)} %add_rsqrt_fusion, f32[256]{0:T(256)S(1)} %broadcast_multiply_fusion.4, ...), kind=kOutput, calls=%fused_computation.43 | convolution fusion | flops 2426337280 | bytes 14568448 | tf_op jit(solution)/shard_map/dot_general | solution.py:19
  50.8 1.2 multiply_sine_fusion
  52.1 1.3 fusion.64
  53.4 1.9 fusion.28
  55.3 4.8 %fusion.8 = f32[256,768]{1,0:T(8,128)} fusion(bf16[3072,768]{1,0:T(8,128)(2,1)} %param.26, f32[256,3072]{1,0:T(8,128)S(1)} %copy-done.38, bf16[1,256,768]{2,1,0:T(8,128)(2,1)S(1)} %copy-done.3, f32[768]{0:T(1024)S(1)} %copy-done.32, f32[768]{0:T(1024)S(1)} %copy-done.31), kind=kOutput, calls=%fused_computation.16 | convolution fusion | flops 1212678144 | bytes 9050112 | tf_op jit(solution)/shard_map/dot_general | solution.py:19
  60.1 11.7 %all-gather.15.cloned.1.call-done = bf16[1,8192,768]{2,1,0:T(8,128)(2,1)} async-done(((bf16[1,256,768]{2,1,0:T(8,128)(2,1)}), bf16[1,8192,768]{2,1,0:T(8,128)(2,1)}) %all-gather.15.cloned.1.call-update) | async-done | bytes 12582928 | tf_op jit(solution)/shard_map/all_gather | solution.py:526
  71.7 10.4 %attn_fwd.1 = (bf16[8192,768]{1,0:T(8,128)(2,1)}, bf16[8192,768]{1,0:T(8,128)(2,1)}, f32[256,768]{1,0:T(8,128)}, f32[12,256]{1,0:T(8,128)}, bf16[768,256]{1,0:T(8,128)(2,1)}) custom-call(s32[1]{0:T(128)} %bitcast.20.me_ref, bf16[8192,768]{1,0:T(8,128)(2,1)} %bitcast.165, f32[256,128]{1,0:T(8,128)} %get-tuple-element.167.cl_ref, ...), custom_call_target="tpu_custom_call" | custom-call | flops 40000000000 | bytes 40000000 | tf_op jit(solution)/shard_map/attn_fwd/pallas_call | solution.py:236
  82.1 48.5 %all-gather.9.cloned.1.call-done.dy_ref.dy_hbm = bf16[8192,768]{1,0:T(8,128)(2,1)} async-done(((bf16[256,768]{1,0:T(8,128)(2,1)}), bf16[8192,768]{1,0:T(8,128)(2,1)}) %all-gather.9.cloned.1.call-update) | async-done | bytes 12582928 | tf_op jit(solution)/shard_map/all_gather | solution.py:527
  130.6 3.1 fusion.48
  135.2 33.9 %later_blocks.1 = (bf16[8192,768]{1,0:T(8,128)(2,1)}, bf16[8192,768]{1,0:T(8,128)(2,1)}) custom-call(s32[1]{0:T(128)} %bitcast.20.me_ref, bf16[8192,768]{1,0:T(8,128)(2,1)} %bitcast.166, bf16[8192,768]{1,0:T(8,128)(2,1)} %all-gather.9.cloned.1.call-done.dy_ref.dy_hbm, f32[256,128]{1,0:T(8,128)} %get-tuple-element.167.cl_ref, ...), custom_call_target="tpu_custom_call" | custom-call | flops 20000000000 | bytes 40000000 | tf_op jit(solution)/shard_map/later_blocks/pallas_call | solution.py:316
  169.2 23.5 %mlp_grads.1 = (f32[96,768]{1,0:T(8,128)}, f32[96,768]{1,0:T(8,128)}, f32[1,128]{1,0:T(1,128)}) custom-call(bf16[8192,768]{1,0:T(8,128)(2,1)} %bitcast.167, bf16[8192,768]{1,0:T(8,128)(2,1)} %all-gather.9.cloned.1.call-done.dy_ref.dy_hbm, f32[1,768]{1,0:T(1,128)} %broadcast_in_dim.27.g_ref, f32[1,768]{1,0:T(1,128)} %broadcast_in_dim.56.s_ref, ...), custom_call_target="tpu_custom_call" | custom-call | flops 20000000000 | bytes 26000000 | tf_op jit(solution)/shard_map/mlp_grads/pallas_call | solution.py:493
  194.9 55.2 %attn_bwd.1 = f32[2304,256]{1,0:T(8,128)} custom-call(s32[1]{0:T(128)} %bitcast.20.me_ref, bf16[8192,768]{1,0:T(8,128)(2,1)} %get-tuple-element.55.k_hbm, bf16[8192,768]{1,0:T(8,128)(2,1)} %get-tuple-element.56.v_hbm, bf16[8192,768]{1,0:T(8,128)(2,1)} %get-tuple-element.66.q_hbm, bf16[8192,768]{1,0:T(8,128)(2,1)} %get-tuple-element.67.o_hbm, ...), custom_call_target="tpu_custom_call" | custom-call | flops 99999997952 | bytes 30000000 | tf_op jit(solution)/shard_map/attn_bwd/pallas_call | solution.py:457
  250.2 41.2 %all-gather.13.cloned.1.call-done = f32[3072,768]{1,0:T(8,128)} async-done(((f32[96,768]{1,0:T(8,128)}), f32[3072,768]{1,0:T(8,128)}) %all-gather.13.cloned.1.call-update) | async-done | bytes 9437200 | tf_op jit(solution)/shard_map/all_gather | solution.py:577
  291.4 2.0 reduce_sum.137
  293.5 4.0 fusion.39
  297.6 2.2 fusion.37
  299.9 3.2 pad_maximum_fusion
  303.2 1.2 copy-done.2
  304.8 1.2 fusion.10
  306.1 9.7 %copy.64 = f32[768,3072]{1,0:T(8,128)} copy(f32[768,3072]{0,1:T(8,128)} %bitcast.144) | data formatting | bytes 18874368
  317.0 97.5 %all-reduce.6.cloned.1.call-done = (f32[780,768]{1,0:T(8,128)}, f32[768,12,3,64]{0,3,2,1:T(8,128)}) async-done(((f32[780,768]{1,0:T(8,128)}, f32[768,12,3,64]{0,3,2,1:T(8,128)}), (f32[780,768]{1,0:T(8,128)}, f32[768,12,3,64]{0,3,2,1:T(8,128)})) %all-reduce.6.cloned.1.call-update) | async-done | bytes 9474064 | tf_op jit(solution)/shard_map/psum | solution.py:586
  414.5 3.2 slice.184
  418.4 1.6 slice_reduce_fusion.1
  422.7 6.7 %copy.82 = f32[768,12,3,64]{0,3,2,1:T(8,128)} copy(f32[768,12,3,64]{0,3,2,1:T(8,128)} %get-tuple-element.234) | data formatting | bytes 14155776
  429.5 8.0 %copy.83 = f32[3072,768]{1,0:T(8,128)} copy(f32[3072,768]{1,0:T(8,128)} %all-gather.13.cloned.1.call-done) | data formatting | bytes 18874368
  (165 shorter events, 26.2 us)
Async XLA Ops:
  7.2 64.5 %all-gather.15.cloned.1.call-start = ((), (), s32[]{:S(2)}) async-start(), calls=%async_computation.4 | async-start | bytes 12976128 | tf_op jit(solution)/shard_map/all_gather | solution.py:526
  8.0 122.7 %all-gather.9.cloned.1.call-start = ((), (), s32[]{:S(2)}) async-start(), calls=%async_computation.1 | async-start | bytes 12976128 | tf_op jit(solution)/shard_map/all_gather | solution.py:527
  10.6 182.0 %all-gather.7.cloned.1.call-start = ((), (), s32[]{:S(2)}) async-start(), calls=%async_computation | async-start | bytes 1622016 | tf_op jit(solution)/shard_map/all_gather | solution.py:565
  17.8 4.3 copy-start.36
  18.9 9.6 %copy-start.1 = (bf16[768,768]{1,0:T(8,128)(2,1)S(1)}, bf16[768,768]{1,0:T(8,128)(2,1)}, u32[]{:S(2)}) copy-start(bf16[768,768]{1,0:T(8,128)(2,1)} %param.22) | copy-start | bytes 3538948
  24.3 5.7 %copy-start.22 = (bf16[12,3,64]{2,1,0:T(4,128)(2,1)S(1)}, bf16[12,3,64]{2,1,0:T(4,128)(2,1)}, u32[]{:S(2)}) copy-start(bf16[12,3,64]{2,1,0:T(4,128)(2,1)} %param.21) | copy-start | bytes 13828
  24.5 6.4 %copy-start.17 = (f32[768]{0:T(1024)S(1)}, f32[768]{0:T(1024)}, u32[]{:S(2)}) copy-start(f32[768]{0:T(1024)} %param.16) | copy-start | bytes 9220
  24.5 7.0 %copy-start.29 = (f32[768]{0:T(1024)S(1)}, f32[768]{0:T(1024)}, u32[]{:S(2)}) copy-start(f32[768]{0:T(1024)} %param.17) | copy-start | bytes 9220
  24.5 7.6 %copy-start.16 = (f32[768]{0:T(1024)S(1)}, f32[768]{0:T(1024)}, u32[]{:S(2)}) copy-start(f32[768]{0:T(1024)} %param.18) | copy-start | bytes 9220
  24.5 8.1 %copy-start.28 = (f32[768]{0:T(1024)S(1)}, f32[768]{0:T(1024)}, u32[]{:S(2)}) copy-start(f32[768]{0:T(1024)} %param.19) | copy-start | bytes 9220
  24.5 10.5 %copy-start.3 = (bf16[1,256,768]{2,1,0:T(8,128)(2,1)S(1)}, bf16[1,256,768]{2,1,0:T(8,128)(2,1)}, u32[]{:S(2)}) copy-start(bf16[1,256,768]{2,1,0:T(8,128)(2,1)} %param.14) | copy-start | bytes 1179652
  30.5 10.5 %copy-start.23 = (f32[1,768]{1,0:T(1,128)}, f32[1,768]{1,0:T(1,128)S(1)}, u32[]{:S(2)}) copy-start(f32[1,768]{1,0:T(1,128)S(1)} %stack_squeeze_reshape.6.bq_ref) | copy-start | bytes 9220
  35.2 18.2 %copy-start.14 = (f32[256]{0:T(256)}, f32[256]{0:T(256)S(1)}, u32[]{:S(2)}) copy-start(f32[256]{0:T(256)S(1)} %broadcast_multiply_fusion.4) | copy-start | bytes 3076
  35.5 5.6 %copy-start.24 = (f32[256]{0:T(256)}, f32[256]{0:T(256)S(1)}, u32[]{:S(2)}) copy-start(f32[256]{0:T(256)S(1)} %add_rsqrt_fusion) | copy-start | bytes 3076
  35.5 5.6 %copy-start.7 = (bf16[256,768]{1,0:T(8,128)(2,1)S(1)}, bf16[256,768]{1,0:T(8,128)(2,1)}, u32[]{:S(2)}) copy-start(bf16[256,768]{1,0:T(8,128)(2,1)} %get-tuple-element.151) | copy-start | bytes 1179652
  35.5 5.6 %copy-start.30 = (f32[768]{0:T(1024)S(1)}, f32[768]{0:T(1024)}, u32[]{:S(2)}) copy-start(f32[768]{0:T(1024)} %param.17) | copy-start | bytes 9220
  50.1 5.2 %copy-start.31 = (f32[768]{0:T(1024)S(1)}, f32[768]{0:T(1024)}, u32[]{:S(2)}) copy-start(f32[768]{0:T(1024)} %convert_element_type.71) | copy-start | bytes 9220
  50.1 5.2 %copy-start.32 = (f32[768]{0:T(1024)S(1)}, f32[768]{0:T(1024)}, u32[]{:S(2)}) copy-start(f32[768]{0:T(1024)} %convert_element_type.72) | copy-start | bytes 9220
  50.1 5.2 %copy-start.38 = (f32[256,3072]{1,0:T(8,128)S(1)}, f32[256,3072]{1,0:T(8,128)}, u32[]{:S(2)}) copy-start(f32[256,3072]{1,0:T(8,128)} %convolution_add_fusion) | copy-start | bytes 9437188
  82.1 51.6 %copy-start.5 = (f32[256,768]{1,0:T(8,128)S(1)}, f32[256,768]{1,0:T(8,128)}, u32[]{:S(2)}) copy-start(f32[256,768]{1,0:T(8,128)} %get-tuple-element.53) | copy-start | bytes 2359300
  135.2 115.0 %all-gather.11.cloned.1.call-start = ((), (), s32[]{:S(2)}) async-start(), calls=%async_computation.2 | async-start | bytes 9732096 | tf_op jit(solution)/shard_map/all_gather | solution.py:576
  169.1 24.3 %copy-start.27 = (f32[8]{0:T(128)S(1)}, f32[8]{0:T(128)}, u32[]{:S(2)}) copy-start(f32[8]{0:T(128)} %copy-done.26) | copy-start | bytes 100
  192.7 98.7 %all-gather.13.cloned.1.call-start = ((), (), s32[]{:S(2)}) async-start(), calls=%async_computation.3 | async-start | bytes 9732096 | tf_op jit(solution)/shard_map/all_gather | solution.py:577
  193.3 221.2 %all-reduce.6.cloned.1.call-start = ((), (), s32[]{:S(2)}) async-start(), calls=%async_computation.5 | async-start | bytes 18972672 | tf_op jit(solution)/shard_map/psum | solution.py:586
  194.9 98.5 %copy-start.13 = (bf16[256,768]{1,0:T(8,128)(2,1)S(1)}, bf16[256,768]{1,0:T(8,128)(2,1)}, u32[]{:S(2)}) copy-start(bf16[256,768]{1,0:T(8,128)(2,1)} %get-tuple-element.79) | copy-start | bytes 1179652
  250.1 43.3 %copy-start = (f32[2304,256]{1,0:T(8,128)S(1)}, f32[2304,256]{1,0:T(8,128)}, u32[]{:S(2)}) copy-start(f32[2304,256]{1,0:T(8,128)} %attn_bwd.1) | copy-start | bytes 7077892
  293.4 4.1 copy-start.4
  293.4 4.1 copy-start.8
  293.4 4.1 copy-start.15
  306.1 9.7 %copy-start.10 = (f32[256,768]{1,0:T(8,128)S(1)}, f32[256,768]{1,0:T(8,128)}, u32[]{:S(2)}) copy-start(f32[256,768]{1,0:T(8,128)} %fusion.28) | copy-start | bytes 2359300
  306.1 9.7 %copy-start.12 = (f32[256,768]{1,0:T(8,128)S(1)}, f32[256,768]{1,0:T(8,128)}, u32[]{:S(2)}) copy-start(f32[256,768]{1,0:T(8,128)} %get-tuple-element.173) | copy-start | bytes 2359300
  420.1 9.4 %copy-start.21 = (f32[768]{0:T(1024)}, f32[768]{0:T(1024)S(1)}, u32[]{:S(2)}) copy-start(f32[768]{0:T(1024)S(1)} %get-tuple-element.237) | copy-start | bytes 9220
  (13 other events, 29.4 us)
Sparse Core Ops, SparseCore 0:
  10.1 61.5 all-gather.14
  73.8 56.7 all-gather.8
  135.3 51.4 all-gather.6
  192.8 46.6 all-gather.10
  242.0 49.3 all-gather.12
  303.3 111.1 all-reduce.5

commit v4 on v3

--- a/solution.py
+++ b/solution.py
@@ -468,35 +468,34 @@
     )(me, k_all, v_all, q_all, o_all, stats, qt, d_ctx_bf, cos_t, sin_t)
 
 
-def mlp_kernel(x_ref, dy_ref, g_ref, s_ref, wu_ref, bu_ref, wd_ref, du_ref, dd_ref, db_ref):
+def mlp_kernel(x_ref, dy_ref, g_ref, s_ref, wu_ref, bu_ref, wd_ref, du_ref, db_ref):
     @pl.when(pl.program_id(0) == 0)
     def _():
         du_ref[...] = jnp.zeros_like(du_ref)
-        dd_ref[...] = jnp.zeros_like(dd_ref)
         db_ref[...] = jnp.zeros_like(db_ref)
 
     h = layer_norm(x_ref[...].astype(jnp.float32), g_ref[...], s_ref[...])[0].astype(jnp.bfloat16)
     dy = dy_ref[...]
     act, slope = exact_gelu(mm(h, wu_ref[...]) + bu_ref[...])
     d_up = mm(dy, wd_ref[...]) * slope
-    keep = du_ref.shape[0]
+    keep = du_ref.shape[0] // 2
     db_ref[...] += jnp.sum(d_up, axis=0, keepdims=True)
-    du_ref[...] += mm(d_up.astype(jnp.bfloat16).T, h)[:keep]
-    dd_ref[...] += mm(act.astype(jnp.bfloat16).T, dy)[:keep]
+    du_ref[:keep] += mm(d_up.astype(jnp.bfloat16).T, h)[:keep]
+    du_ref[keep:] += mm(act.astype(jnp.bfloat16).T, dy)[:keep]
 
 
 def mlp_grads(x_all, dy_all, gain, shift, wu, bu, wd, keep):
     S, W = x_all.shape
     F = wu.shape[1]
-    R = 512
+    R = 256
     const = lambda j: (0, 0)
     return pl.pallas_call(
         mlp_kernel,
         grid=(S // R,),
-        out_shape=[jax.ShapeDtypeStruct((keep, W), jnp.float32)] * 2 + [jax.ShapeDtypeStruct((1, F), jnp.float32)],
+        out_shape=[jax.ShapeDtypeStruct((2 * keep, W), jnp.float32)] + [jax.ShapeDtypeStruct((1, F), jnp.float32)],
         in_specs=[pl.BlockSpec((R, W), lambda j: (j, 0)), pl.BlockSpec((R, W), lambda j: (j, 0)), pl.BlockSpec((1, W), const), pl.BlockSpec((1, W), const),
                   pl.BlockSpec((W, F), const), pl.BlockSpec((1, F), const), pl.BlockSpec((W, F), const)],
-        out_specs=[pl.BlockSpec((keep, W), const)] * 2 + [pl.BlockSpec((1, F), const)],
+        out_specs=[pl.BlockSpec((2 * keep, W), const)] + [pl.BlockSpec((1, F), const)],
         compiler_params=pltpu.CompilerParams(vmem_limit_bytes=VMEM_LIMIT, dimension_semantics=("arbitrary",)),
         cost_estimate=pl.CostEstimate(flops=20_000_000_000, bytes_accessed=26_000_000, transcendentals=0),
         name="mlp_grads",
@@ -561,22 +560,24 @@
             (x_all, y_part, dx_part, d_ln2_gain, d_ln2_bias, dy_sum, d_ctx, d_ctx_bf, h_attn, wq, wk, wv, wot, wu_s, wd_s))
         k_all, v_all, attn_norm, lse, qt = fwd_attention(me1, x_in, tab, row(ln1_gain), row(ln1_bias), wq, wk, wv, b3, T, hd)
         delta = jnp.sum((d_ctx * attn_norm).reshape(T, heads, hd), axis=-1).T
-        fill = jnp.zeros((2 * heads, T), f32)
+        fill = jnp.zeros((-2 * heads % 32, T), f32)
         stats = lax.all_gather(jnp.concatenate([lse, delta, fill], axis=0), 'cp', tiled=True)
         attn_ctx = attn_norm.astype(bf)
         y_rows = (y_part + mm(attn_ctx, w_out)).astype(bf)
         d_w_out = mm(attn_ctx, dy_bf, TN)
 
         dy_in, _ = lax.optimization_barrier((dy_all, lse))
-        du_s, dd_s, db_s = mlp_grads(x_in, dy_in, row(ln2_gain), row(ln2_bias), wu_s, bu_s, wd_s, F)
+        du_s, db_s = mlp_grads(x_in, dy_in, row(ln2_gain), row(ln2_bias), wu_s, bu_s, wd_s, F)
         d_b_up = lax.dynamic_update_slice(jnp.zeros((FF,), f32), db_s[0, :F], (me * F,))
 
-        q_all, o_all = later_blocks(me1, x_in, dy_in, tab, row(ln1_gain), row(ln1_bias), wq, wot, b3[0:1], T, hd)
-        stats, d_w_out, du_s, dd_s, q_all = lax.optimization_barrier((stats, d_w_out, du_s, dd_s, q_all))
-        d_w_up = lax.all_gather(du_s, 'cp', tiled=True)
-        d_w_down = lax.all_gather(dd_s, 'cp', tiled=True)
+        dy_late, _ = lax.optimization_barrier((dy_in, db_s))
+        q_all, o_all = later_blocks(me1, x_in, dy_late, tab, row(ln1_gain), row(ln1_bias), wq, wot, b3[0:1], T, hd)
+        stats, d_w_out, q_all = lax.optimization_barrier((stats, d_w_out, q_all))
+        d_w_mlp = lax.all_gather(du_s, 'cp', tiled=True)
         d3 = bwd_attention(me1, k_all, v_all, q_all, o_all, stats, qt, d_ctx_bf, cos_o, sin_o, T, hd)
-        d3, d_w_up, d_w_down = lax.optimization_barrier((d3, d_w_up, d_w_down))
+        d3, d_w_mlp = lax.optimization_barrier((d3, d_w_mlp))
+        d_w_mlp = d_w_mlp.reshape(cp_size, 2, F, W)
+        d_w_up, d_w_down = d_w_mlp[:, 0].reshape(FF, W), d_w_mlp[:, 1].reshape(FF, W)
         d3_bf = d3.astype(bf)
         d_h = mm(d3_bf, w_rows.reshape(3 * W, W), TN)
         d_w_rows = mm(d3_bf, h_attn)

time: 446 us -> 418 us (0.937)
  waiting for transfers between devices: 200 us -> 141 us
  local copies, waits for them, and re-layouts: 54.6 us -> 71.9 us
  Pallas kernels: 123 us -> 133 us
    all_gather x2 -> x1, waiting for transfers between devices: 41.2 us -> 1.12 us  [local_layer(): d_w_mlp = lax.all_gather(du_s, 'cp', tiled=True)]
    slice x0 -> x1, local copies, waits for them, and re-layouts: none -> 12.9 us  [local_layer(): d_w_mlp[:, 1].reshape(FF, W)]
    psum x1, waiting for transfers between devices: 97.5 us -> 84.6 us  [local_layer(): lax.psum((d_w_rows, jnp.concatenate([d_w_out, small], axis=0)), 'cp')]
    pallas_call x1, Pallas kernels: 23.5 us -> 34.1 us  [mlp_grads(): pl.pallas_call(mlp_kernel, grid=(S // R,), out_shape=[jax.ShapeDtypeStruc...]
    all_gather x1, waiting for transfers between devices: 48.5 us -> 43.7 us  [local_layer(): dy_all = lax.all_gather(dy_bf, 'cp', tiled=True)]
    unnamed x91 -> x98, local copies, waits for them, and re-layouts: 31 us -> 30.3 us
  transfers between devices with their start and end apart: 6 -> 5, of which waited for: 4 -> 4; matrix products, arithmetic and copies ran while one was open for 15% -> 21% of each run, Pallas kernels for 28% -> 32%
where the time goes in v4:
time: 418 us; the launch traced here: 416 us
  waiting for transfers between devices  141 us (34%)
  Pallas kernels  133 us (32%)
  local copies, waits for them, and re-layouts  71.9 us (17%)
  matrix products  34.4 us (8%)
  other arithmetic  20.2 us (5%)
  between operations  14.4 us (3%)
    psum x1, waiting for transfers between devices, local_layer(): lax.psum((d_w_rows, jnp.concatenate([d_w_out, small], axis=0)), 'cp')  84.6 us
    pallas_call x1, Pallas kernels, bwd_attention(): pl.pallas_call(functools.partial(bwd_kernel, hd, S // T, stats.shape[0] *...  55 us
    all_gather x1, waiting for transfers between devices, local_layer(): dy_all = lax.all_gather(dy_bf, 'cp', tiled=True)  43.7 us
    dot_general x8, matrix products, mm(): return lax.dot_general(a, b, dims, preferred_element_type=jnp.float32)  34.4 us
    pallas_call x1, Pallas kernels, mlp_grads(): pl.pallas_call(mlp_kernel, grid=(S // R,), out_shape=[jax.ShapeDtypeStruc...  34.1 us
    pallas_call x1, Pallas kernels, later_blocks(): pl.pallas_call(functools.partial(proj_kernel, hd, S // T), out_shape=[jax...  33.9 us
    unnamed x98, local copies, waits for them, and re-layouts  30.3 us
    slice x1, local copies, waits for them, and re-layouts, local_layer(): d_w_mlp[:, 1].reshape(FF, W)  12.9 us
  transfers between devices with their start and end apart: 5, of which 4 were waited for; matrix products, arithmetic and copies ran while one was open for 21% of the time, Pallas kernels for 32%

profile of v4, /device:TPU:97, one launch (start us, length us, event | category | flops | bytes accessed | tf_op | source)
XLA Modules:
  0.0 415.9 jit_solution(2881279949504292693)
XLA Ops:
  8.1 2.5 fusion.60
  22.4 1.5 copy.57
  23.8 2.2 copy.71
  26.1 1.3 fusion.55
  27.4 2.4 copy.56
  31.9 1.5 copy.55
  33.6 1.5 copy.54
  37.0 5.6 %convolution_add_fusion = f32[256,3072]{1,0:T(8,128)} fusion(bf16[768,3072]{1,0:T(8,128)(2,1)} %param.24, f32[3072]{0:T(1024)S(1)} %copy-done.26, bf16[1,256,768]{2,1,0:T(8,128)(2,1)S(1)} %copy-done.3, f32[768]{0:T(1024)S(1)} %copy-done.33, f32[768]{0:T(1024)S(1)} %copy-done.20, f32[256]{0:T(256)S(1)} %add_rsqrt_fusion, f32[256]{0:T(256)S(1)} %broadcast_multiply_fusion.4), kind=kOutput, calls=%fused_computation.2 | convolution fusion | flops 1209925632 | bytes 8278016 | tf_op jit(solution)/shard_map/dot_general | solution.py:19
  42.5 9.0 %fusion.29 = (f32[768]{0:T(1024)}, f32[256]{0:T(256)S(1)}, f32[256]{0:T(256)S(1)}, f32[768]{0:T(1024)}, bf16[256,768]{1,0:T(8,128)(2,1)}, /*index=5*/f32[256,768]{1,0:T(8,128)S(1)}) fusion(bf16[1,256,768]{2,1,0:T(8,128)(2,1)S(1)} %copy-done.3, f32[256]{0:T(256)S(1)} %add_rsqrt_fusion, f32[256]{0:T(256)S(1)} %broadcast_multiply_fusion.4, ...), kind=kOutput, calls=%fused_computation.43 | convolution fusion | flops 2426337280 | bytes 14568448 | tf_op jit(solution)/shard_map/dot_general | solution.py:19
  56.1 4.8 %fusion.8 = f32[256,768]{1,0:T(8,128)} fusion(bf16[3072,768]{1,0:T(8,128)(2,1)} %param.26, f32[256,3072]{1,0:T(8,128)S(1)} %copy-done.42, bf16[1,256,768]{2,1,0:T(8,128)(2,1)S(1)} %copy-done.3, f32[768]{0:T(1024)S(1)} %copy-done.35, f32[768]{0:T(1024)S(1)} %copy-done.36), kind=kOutput, calls=%fused_computation.16 | convolution fusion | flops 1212678144 | bytes 9050112 | tf_op jit(solution)/shard_map/dot_general | solution.py:19
  60.9 10.9 %all-gather.12.cloned.1.call-done = bf16[1,8192,768]{2,1,0:T(8,128)(2,1)} async-done(((bf16[1,256,768]{2,1,0:T(8,128)(2,1)}), bf16[1,8192,768]{2,1,0:T(8,128)(2,1)}) %all-gather.12.cloned.1.call-update) | async-done | bytes 12582928 | tf_op jit(solution)/shard_map/all_gather | solution.py:525
  71.8 10.3 %attn_fwd.1 = (bf16[8192,768]{1,0:T(8,128)(2,1)}, bf16[8192,768]{1,0:T(8,128)(2,1)}, f32[256,768]{1,0:T(8,128)}, f32[12,256]{1,0:T(8,128)}, bf16[768,256]{1,0:T(8,128)(2,1)}) custom-call(s32[1]{0:T(128)} %bitcast.20.me_ref, bf16[8192,768]{1,0:T(8,128)(2,1)} %bitcast.173, f32[256,128]{1,0:T(8,128)} %get-tuple-element.149.cl_ref, ...), custom_call_target="tpu_custom_call" | custom-call | flops 40000000000 | bytes 40000000 | tf_op jit(solution)/shard_map/attn_fwd/pallas_call | solution.py:236
  87.0 43.7 %all-gather.8.cloned.1.call-done.dy_ref.dy_hbm = bf16[8192,768]{1,0:T(8,128)(2,1)} async-done(((bf16[256,768]{1,0:T(8,128)(2,1)}), bf16[8192,768]{1,0:T(8,128)(2,1)}) %all-gather.8.cloned.1.call-update) | async-done | bytes 12582928 | tf_op jit(solution)/shard_map/all_gather | solution.py:526
  130.7 34.1 %mlp_grads.1 = (f32[192,768]{1,0:T(8,128)}, f32[1,128]{1,0:T(1,128)}) custom-call(bf16[8192,768]{1,0:T(8,128)(2,1)} %bitcast.174, bf16[8192,768]{1,0:T(8,128)(2,1)} %all-gather.8.cloned.1.call-done.dy_ref.dy_hbm, f32[1,768]{1,0:T(1,128)} %broadcast_in_dim.27.g_ref, f32[1,768]{1,0:T(1,128)} %broadcast_in_dim.56.s_ref, bf16[768,128]{1,0:T(8,128)(2,1)} %pad.11.wu_ref, ...), custom_call_target="tpu_custom_call" | custom-call | flops 20000000000 | bytes 26000000 | tf_op jit(solution)/shard_map/mlp_grads/pallas_call | solution.py:492
  166.4 1.9 fusion.48
  168.4 33.9 %later_blocks.1 = (bf16[8192,768]{1,0:T(8,128)(2,1)}, bf16[8192,768]{1,0:T(8,128)(2,1)}) custom-call(s32[1]{0:T(128)} %bitcast.20.me_ref, bf16[8192,768]{1,0:T(8,128)(2,1)} %bitcast.175, bf16[8192,768]{1,0:T(8,128)(2,1)} %all-gather.8.cloned.1.call-done.dy_ref.dy_hbm, f32[256,128]{1,0:T(8,128)} %get-tuple-element.149.cl_ref, ...), custom_call_target="tpu_custom_call" | custom-call | flops 20000000000 | bytes 40000000 | tf_op jit(solution)/shard_map/later_blocks/pallas_call | solution.py:316
  202.3 55.0 %attn_bwd.1 = f32[2304,256]{1,0:T(8,128)} custom-call(s32[1]{0:T(128)} %bitcast.20.me_ref, bf16[8192,768]{1,0:T(8,128)(2,1)} %get-tuple-element.52.k_hbm, bf16[8192,768]{1,0:T(8,128)(2,1)} %get-tuple-element.53.v_hbm, bf16[8192,768]{1,0:T(8,128)(2,1)} %get-tuple-element.63.q_hbm, bf16[8192,768]{1,0:T(8,128)(2,1)} %get-tuple-element.64.o_hbm, ...), custom_call_target="tpu_custom_call" | custom-call | flops 99999997952 | bytes 30000000 | tf_op jit(solution)/shard_map/attn_bwd/pallas_call | solution.py:457
  258.4 2.6 reduce_sum.137
  261.1 5.6 %fusion.37 = (f32[768]{0:T(1024)S(1)}, f32[256]{0:T(256)}, f32[256]{0:T(256)}, f32[768]{0:T(1024)S(1)}, f32[256,768]{1,0:T(8,128)}) fusion(bf16[1,256,768]{2,1,0:T(8,128)(2,1)S(1)} %copy-done.4, f32[256]{0:T(256)} %copy-done.28, f32[256]{0:T(256)S(1)} %copy-done.19, f32[768]{0:T(1024)} %param.16, bf16[2304,768]{1,0:T(8,128)(2,1)} %bitcast.156, ...), kind=kOutput, calls=%fused_computation.51 | convolution fusion | flops 908523520 | bytes 7091200 | tf_op jit(solution)/shard_map/dot_general | solution.py:19
  269.2 1.3 constant_dynamic-update-slice_fusion.4
  270.5 1.3 constant_dynamic-update-slice_fusion.3
  271.8 1.3 constant_dynamic-update-slice_fusion.2
  273.1 1.3 constant_dynamic-update-slice_fusion.1
  275.0 1.4 reshape.154
  276.4 5.2 %fusion.39 = f32[2304,768]{1,0:T(8,128)} fusion(bf16[256,768]{1,0:T(8,128)(2,1)} %get-tuple-element.74, f32[2304,256]{1,0:T(8,128)S(1)} %copy-done), kind=kOutput, calls=%fused_computation.60 | convolution fusion | flops 906559488 | bytes 9830400 | tf_op jit(solution)/shard_map/dot_general | solution.py:19
  281.6 1.6 pad_maximum_fusion
  285.9 12.9 %fusion.54 = (f32[32,1,96,768]{3,2,1,0:T(8,128)}, f32[32,1,96,768]{3,2,1,0:T(8,128)}) fusion(f32[32,2,96,768]{3,2,1,0:T(8,128)} %bitcast.150), kind=kLoop, calls=%fused_computation.118 | loop fusion | bytes 37748736 | tf_op jit(solution)/shard_map/slice | solution.py:580
  298.8 9.7 %copy.66 = f32[768,3072]{1,0:T(8,128)} copy(f32[768,3072]{0,1:T(8,128)} %bitcast.149) | data formatting | bytes 18874368
  309.7 84.6 %all-reduce.6.cloned.1.call-done = (f32[780,768]{1,0:T(8,128)}, f32[768,12,3,64]{0,3,2,1:T(8,128)}) async-done(((f32[780,768]{1,0:T(8,128)}, f32[768,12,3,64]{0,3,2,1:T(8,128)}), (f32[780,768]{1,0:T(8,128)}, f32[768,12,3,64]{0,3,2,1:T(8,128)})) %all-reduce.6.cloned.1.call-update) | async-done | bytes 9474064 | tf_op jit(solution)/shard_map/psum | solution.py:587
  395.9 1.6 slice_reduce_fusion.1
  397.5 3.2 slice.192
  402.6 6.7 %copy.84 = f32[768,12,3,64]{0,3,2,1:T(8,128)} copy(f32[768,12,3,64]{0,3,2,1:T(8,128)} %get-tuple-element.202) | data formatting | bytes 14155776
  (171 shorter events, 39.2 us)
Async XLA Ops:
  7.2 15.2 %copy-start.1 = (bf16[768,768]{1,0:T(8,128)(2,1)S(1)}, bf16[768,768]{1,0:T(8,128)(2,1)}, u32[]{:S(2)}) copy-start(bf16[768,768]{1,0:T(8,128)(2,1)} %param.22) | copy-start | bytes 3538948
  7.2 64.6 %all-gather.12.cloned.1.call-start = ((), (), s32[]{:S(2)}) async-start(), calls=%async_computation.3 | async-start | bytes 12976128 | tf_op jit(solution)/shard_map/all_gather | solution.py:525
  8.0 122.7 %all-gather.8.cloned.1.call-start = ((), (), s32[]{:S(2)}) async-start(), calls=%async_computation.1 | async-start | bytes 12976128 | tf_op jit(solution)/shard_map/all_gather | solution.py:526
  10.7 191.6 %all-gather.6.cloned.1.call-start = ((), (), s32[]{:S(2)}) async-start(), calls=%async_computation | async-start | bytes 1081344 | tf_op jit(solution)/shard_map/all_gather | solution.py:564
  18.7 17.2 %copy-start.27 = (f32[1,768]{1,0:T(1,128)}, f32[1,768]{1,0:T(1,128)S(1)}, u32[]{:S(2)}) copy-start(f32[1,768]{1,0:T(1,128)S(1)} %stack_squeeze_reshape.6.bq_ref) | copy-start | bytes 9220
  36.6 18.2 %copy-start.18 = (f32[256]{0:T(256)}, f32[256]{0:T(256)S(1)}, u32[]{:S(2)}) copy-start(f32[256]{0:T(256)S(1)} %broadcast_multiply_fusion.4) | copy-start | bytes 3076
  36.9 17.9 %copy-start.28 = (f32[256]{0:T(256)}, f32[256]{0:T(256)S(1)}, u32[]{:S(2)}) copy-start(f32[256]{0:T(256)S(1)} %add_rsqrt_fusion) | copy-start | bytes 3076
  36.9 5.6 %copy-start.7 = (bf16[256,768]{1,0:T(8,128)(2,1)S(1)}, bf16[256,768]{1,0:T(8,128)(2,1)}, u32[]{:S(2)}) copy-start(bf16[256,768]{1,0:T(8,128)(2,1)} %get-tuple-element.133) | copy-start | bytes 1179652
  37.0 5.6 %copy-start.21 = (f32[768]{0:T(1024)S(1)}, f32[768]{0:T(1024)}, u32[]{:S(2)}) copy-start(f32[768]{0:T(1024)} %param.16) | copy-start | bytes 9220
  37.0 5.6 %copy-start.32 = (f32[768]{0:T(1024)S(1)}, f32[768]{0:T(1024)}, u32[]{:S(2)}) copy-start(f32[768]{0:T(1024)} %param.17) | copy-start | bytes 9220
  51.5 4.6 %copy-start.36 = (f32[768]{0:T(1024)S(1)}, f32[768]{0:T(1024)}, u32[]{:S(2)}) copy-start(f32[768]{0:T(1024)} %convert_element_type.71) | copy-start | bytes 9220
  51.5 4.6 %copy-start.42 = (f32[256,3072]{1,0:T(8,128)S(1)}, f32[256,3072]{1,0:T(8,128)}, u32[]{:S(2)}) copy-start(f32[256,3072]{1,0:T(8,128)} %convolution_add_fusion) | copy-start | bytes 9437188
  84.4 173.9 %all-gather.10.cloned.1.call-start = ((), (), s32[]{:S(2)}) async-start(), calls=%async_computation.2 | async-start | bytes 19464192 | tf_op jit(solution)/shard_map/all_gather | solution.py:576
  87.0 78.0 %copy-start.31 = (f32[8]{0:T(128)S(1)}, f32[8]{0:T(128)}, u32[]{:S(2)}) copy-start(f32[8]{0:T(128)} %copy-done.30) | copy-start | bytes 100
  87.0 79.5 %copy-start.6 = (f32[256,768]{1,0:T(8,128)S(1)}, f32[256,768]{1,0:T(8,128)}, u32[]{:S(2)}) copy-start(f32[256,768]{1,0:T(8,128)} %get-tuple-element.50) | copy-start | bytes 2359300
  164.9 229.5 %all-reduce.6.cloned.1.call-start = ((), (), s32[]{:S(2)}) async-start(), calls=%async_computation.4 | async-start | bytes 18972672 | tf_op jit(solution)/shard_map/psum | solution.py:587
  202.3 58.8 %copy-start.4 = (bf16[1,256,768]{2,1,0:T(8,128)(2,1)S(1)}, bf16[1,256,768]{2,1,0:T(8,128)(2,1)}, u32[]{:S(2)}) copy-start(bf16[1,256,768]{2,1,0:T(8,128)(2,1)} %param.14) | copy-start | bytes 1179652
  202.3 58.8 %copy-start.19 = (f32[256]{0:T(256)S(1)}, f32[256]{0:T(256)}, u32[]{:S(2)}) copy-start(f32[256]{0:T(256)} %copy-done.18) | copy-start | bytes 3076
  261.0 8.2 %copy-start.38 = (f32[768]{0:T(1024)S(1)}, f32[768]{0:T(1024)}, u32[]{:S(2)}) copy-start(f32[768]{0:T(1024)} %get-tuple-element.71) | copy-start | bytes 9220
  261.0 9.5 %copy-start.37 = (f32[768]{0:T(1024)S(1)}, f32[768]{0:T(1024)}, u32[]{:S(2)}) copy-start(f32[768]{0:T(1024)} %get-tuple-element.72) | copy-start | bytes 9220
  261.0 10.8 %copy-start.23 = (f32[768]{0:T(1024)S(1)}, f32[768]{0:T(1024)}, u32[]{:S(2)}) copy-start(f32[768]{0:T(1024)} %get-tuple-element.73) | copy-start | bytes 9220
  261.0 12.0 %copy-start.17 = (f32[2304]{0:T(1024)S(1)}, f32[2304]{0:T(1024)}, u32[]{:S(2)}) copy-start(f32[2304]{0:T(1024)} %reduce_sum.137) | copy-start | bytes 27652
  261.1 15.3 %copy-start = (f32[2304,256]{1,0:T(8,128)S(1)}, f32[2304,256]{1,0:T(8,128)}, u32[]{:S(2)}) copy-start(f32[2304,256]{1,0:T(8,128)} %attn_bwd.1) | copy-start | bytes 7077892
  276.4 5.2 %copy-start.5 = (f32[768,768]{1,0:T(8,128)S(1)}, f32[768,768]{1,0:T(8,128)}, u32[]{:S(2)}) copy-start(f32[768,768]{1,0:T(8,128)} %fusion.48) | copy-start | bytes 7077892
  276.4 5.2 %copy-start.16 = (f32[12,768]{1,0:T(8,128)S(1)}, f32[12,768]{1,0:T(8,128)}, u32[]{:S(2)}) copy-start(f32[12,768]{1,0:T(8,128)} %reshape.154) | copy-start | bytes 110596
  298.8 9.7 %copy-start.40 = (f32[256]{0:T(256)S(1)}, f32[256]{0:T(256)}, u32[]{:S(2)}) copy-start(f32[256]{0:T(256)} %get-tuple-element.110) | copy-start | bytes 3076
  298.8 9.8 %copy-start.39 = (f32[256]{0:T(256)S(1)}, f32[256]{0:T(256)}, u32[]{:S(2)}) copy-start(f32[256]{0:T(256)} %get-tuple-element.114) | copy-start | bytes 3076
  298.8 9.8 %copy-start.9 = (f32[256,768]{1,0:T(8,128)S(1)}, f32[256,768]{1,0:T(8,128)}, u32[]{:S(2)}) copy-start(f32[256,768]{1,0:T(8,128)} %fusion.28) | copy-start | bytes 2359300
  298.8 9.8 %copy-start.13 = (f32[256,768]{1,0:T(8,128)S(1)}, f32[256,768]{1,0:T(8,128)}, u32[]{:S(2)}) copy-start(f32[256,768]{1,0:T(8,128)} %get-tuple-element.155) | copy-start | bytes 2359300
  298.8 9.8 %copy-start.22 = (f32[768]{0:T(1024)S(1)}, f32[768]{0:T(1024)}, u32[]{:S(2)}) copy-start(f32[768]{0:T(1024)} %param.16) | copy-start | bytes 9220
  298.8 9.8 %copy-start.29 = (f32[256]{0:T(256)S(1)}, f32[256]{0:T(256)}, u32[]{:S(2)}) copy-start(f32[256]{0:T(256)} %copy-done.28) | copy-start | bytes 3076
  397.5 11.9 %copy-start.24 = (f32[768]{0:T(1024)}, f32[768]{0:T(1024)S(1)}, u32[]{:S(2)}) copy-start(f32[768]{0:T(1024)S(1)} %get-tuple-element.205) | copy-start | bytes 9220
  (16 other events, 38.5 us)
Sparse Core Ops, SparseCore 0:
  10.1 61.6 all-gather.11
  73.8 56.7 all-gather.7
  132.8 51.4 all-gather.5
  186.7 71.5 all-gather.9
  283.3 111.0 all-reduce.5
